TPU v7x, 16 devices: a whole 2x2x2 slice. The times are simulated.
16 devices in a mesh: dp: 4 (over z, y), sp: 4 (over x, core).
Axes of the slice: x: 2, y: 2, z: 2, core: 2. Of those that a mesh axis runs over, the one named last changes fastest.
Arguments:
- resid: float32 [16, 256, 1536], P('dp', 'sp'), parts along dimension 0
- pre_norm: float32 [2, 1536], replicated
- w_in: bfloat16 [2, 1536, 6448], replicated
- conv_w: float32 [2, 3328, 4], replicated
- conv_b: float32 [2, 3328], replicated
- dt_bias: float32 [2, 48], replicated
- a_log: float32 [2, 48], replicated
- d_skip: float32 [2, 48], replicated
- gate_norm: float32 [2, 1, 3072], replicated
- w_out: bfloat16 [2, 3072, 1536], replicated
Outputs:
- output 1: float32 [16, 256, 1536], P('dp', 'sp'), parts along dimension 0
- output 2: float32 [16, 2, 48, 64, 128], P('dp', None, 'sp'), parts along dimension 0
- output 3: bfloat16 [16, 2, 3328, 3], P('dp'), parts along dimension 0
There are 4 independent parts. A program takes and returns all parts, laid end to end along the dimension named above; an argument that names none is the same for every part.
All inputs are finite; a program needn't handle non-finite values.
Results may differ from a plain program's by a relative error of at most 0.017486.
Values are sent between devices in bfloat16 or wider.
A program may use at most 1 GiB of HBM per device.

v0:
```python
import jax
import jax.numpy as jnp
from jax import lax
from jax.sharding import PartitionSpec as P

CONV_WIDTH = 4
CHUNK = 256
EPSILON = 1e-5


def rms_norm(values, gain_vec):
    mean_sq = jnp.mean(values * values, axis=-1, keepdims=True)
    return values * lax.rsqrt(mean_sq + EPSILON) * gain_vec


def ssd_scan(x_in, dt_in, bc_in, a_neg, d_vec):
    batch, seq_len, groups, per_group, head_dim = x_in.shape
    d_state = bc_in.shape[-1]
    causal = jnp.arange(CHUNK)[:, None] >= jnp.arange(CHUNK)[None, :]

    def body(chunk_index, carry):
        state, y_buffer = carry
        start = chunk_index * CHUNK
        x_chunk = lax.dynamic_slice_in_dim(x_in, start, CHUNK, axis=1)
        dt_chunk = lax.dynamic_slice_in_dim(dt_in, start, CHUNK, axis=1).astype(jnp.float32)
        bc_chunk = lax.dynamic_slice_in_dim(bc_in, start, CHUNK, axis=1)
        b_chunk = bc_chunk[:, :, 0]
        c_chunk = bc_chunk[:, :, 1]
        cum_log = jnp.cumsum(dt_chunk * a_neg, axis=1)
        cum_heads = jnp.transpose(cum_log, (0, 2, 3, 1))
        log_diff = cum_heads[..., :, None] - cum_heads[..., None, :]
        decay_mat = jnp.exp(jnp.where(causal, log_diff, -jnp.inf))
        scores = jnp.einsum('btgn,bsgn->bgts', c_chunk, b_chunk, preferred_element_type=jnp.float32)
        mix_mat = decay_mat * scores[:, :, None]
        x_float = x_chunk.astype(jnp.float32)
        x_scaled = x_float * dt_chunk[..., None]
        y_intra = jnp.einsum('bghts,bsghp->btghp', mix_mat, x_scaled, preferred_element_type=jnp.float32)
        y_inter = jnp.einsum('btgn,bghpn->btghp', c_chunk.astype(jnp.float32), state, preferred_element_type=jnp.float32)
        to_end = jnp.exp(cum_log[:, -1:] - cum_log)
        state = state * jnp.exp(cum_log[:, -1])[..., None, None] + jnp.einsum('bsghp,bsgn->bghpn', x_scaled * to_end[..., None], b_chunk.astype(jnp.float32), preferred_element_type=jnp.float32)
        y_chunk = y_intra + y_inter * jnp.exp(cum_log)[..., None] + d_vec[:, :, None] * x_float
        y_buffer = lax.dynamic_update_slice_in_dim(y_buffer, y_chunk.astype(jnp.bfloat16), start, axis=1)
        return state, y_buffer

    state_zero = jnp.zeros((batch, groups, per_group, head_dim, d_state), jnp.float32)
    y_zero = jnp.zeros(x_in.shape, jnp.bfloat16)
    return lax.fori_loop(0, seq_len // CHUNK, body, (state_zero, y_zero))


def solution(mesh):
    seg_count = mesh.shape['sp']

    def layer(resid, pre_w, w_in_l, conv_w_l, conv_b_l, dt_b, a_log_l, d_l, gate_w, w_out_l):
        batch, seg_len, d_model = resid.shape
        n_groups, group_width = gate_w.shape
        d_inner = n_groups * group_width
        n_heads = dt_b.shape[0]
        conv_dim = conv_b_l.shape[0]
        d_state = (conv_dim - d_inner) // (2 * n_groups)
        head_dim = d_inner // n_heads
        seq_len = seg_len * seg_count
        local_heads = n_heads // seg_count
        local_groups = max(n_groups // seg_count, 1)
        local_per_group = local_heads // local_groups
        repeat_count = max(seg_count // n_groups, 1)
        seg_index = lax.axis_index('sp')

        normed = rms_norm(resid, pre_w).astype(jnp.bfloat16)
        projected = jnp.einsum('bld,de->ble', normed, w_in_l, preferred_element_type=jnp.float32).astype(jnp.bfloat16)
        gate_z = projected[..., :d_inner]
        xbc = projected[..., d_inner:d_inner + conv_dim]
        dt_raw = projected[..., d_inner + conv_dim:]
        halo_rows = lax.ppermute(xbc[:, seg_len - (CONV_WIDTH - 1):], 'sp', [(source, source + 1) for source in range(seg_count - 1)])
        padded = jnp.concatenate([halo_rows, xbc], axis=1)
        conv_out = conv_b_l + sum(padded[:, tap_index:tap_index + seg_len].astype(jnp.float32) * conv_w_l[:, tap_index] for tap_index in range(CONV_WIDTH))
        activated = jax.nn.silu(conv_out).astype(jnp.bfloat16)
        delta = jax.nn.softplus(dt_raw.astype(jnp.float32) + dt_b).astype(jnp.bfloat16)
        bc_tokens = jnp.repeat(activated[..., d_inner:].reshape(batch, seg_len, 2, n_groups, d_state), repeat_count, axis=3)

        x_local = lax.all_to_all(activated[..., :d_inner], 'sp', 2, 1, tiled=True)
        dt_local = lax.all_to_all(delta, 'sp', 2, 1, tiled=True)
        bc_local = lax.all_to_all(bc_tokens, 'sp', 3, 1, tiled=True)

        head_start = seg_index * local_heads
        a_neg = -jnp.exp(lax.dynamic_slice_in_dim(a_log_l, head_start, local_heads)).reshape(local_groups, local_per_group)
        d_local = lax.dynamic_slice_in_dim(d_l, head_start, local_heads).reshape(local_groups, local_per_group)
        final, y_local = ssd_scan(x_local.reshape(batch, seq_len, local_groups, local_per_group, head_dim), dt_local.reshape(batch, seq_len, local_groups, local_per_group), bc_local, a_neg, d_local)

        y_tokens = lax.all_to_all(y_local.reshape(batch, seq_len, local_heads * head_dim), 'sp', 1, 2, tiled=True)

        gated = y_tokens.reshape(batch, seg_len, n_groups, group_width).astype(jnp.float32) * jax.nn.silu(gate_z.reshape(batch, seg_len, n_groups, group_width).astype(jnp.float32))
        normed_y = (gated * lax.rsqrt(jnp.mean(gated * gated, axis=-1, keepdims=True) + EPSILON) * gate_w).astype(jnp.bfloat16)
        out_proj = jnp.einsum('blgc,gcd->bld', normed_y, w_out_l.reshape(n_groups, group_width, d_model), preferred_element_type=jnp.float32)
        tail_rows = jnp.where(seg_index == seg_count - 1, xbc[:, seg_len - (CONV_WIDTH - 1):], jnp.zeros((), jnp.bfloat16))
        conv_state = lax.psum(tail_rows, 'sp')
        return resid + out_proj, final.reshape(batch, local_heads, head_dim, d_state), jnp.swapaxes(conv_state, 1, 2)

    def forward(resid, pre_norm, w_in, conv_w, conv_b, dt_bias, a_log, d_skip, gate_norm, w_out):
        finals = []
        tails = []
        for layer_index in range(w_in.shape[0]):
            resid, final, tail_rows = layer(resid, pre_norm[layer_index], w_in[layer_index], conv_w[layer_index], conv_b[layer_index], dt_bias[layer_index], a_log[layer_index], d_skip[layer_index], gate_norm[layer_index], w_out[layer_index])
            finals.append(final)
            tails.append(tail_rows)
        return resid, jnp.stack(finals, axis=1), jnp.stack(tails, axis=1)

    return jax.shard_map(forward, mesh=mesh, in_specs=(P('dp', 'sp', None), P(), P(), P(), P(), P(), P(), P(), P(), P()), out_specs=(P('dp', 'sp', None), P('dp', None, 'sp', None, None), P('dp', None, None, None)), check_vma=False)
```

profile of v0, /device:TPU:0, one launch (start us, length us, event | category | flops | bytes accessed | tf_op | source)
XLA Modules:
  0.0 441.1 jit_solution(15712911071892186384)
XLA Ops:
  11.5 14.6 %fusion.16 = bf16[4,64,6448]{1,2,0:T(8,128)(2,1)S(1)} fusion(bf16[2,1536,6448]{1,2,0:T(8,128)(2,1)} %param.12, f32[4,64,1536]{2,1,0:T(8,128)} %param.10, f32[1536]{0:T(1024)S(1)} %get-tuple-element.92, f32[4,64]{1,0:T(4,128)S(1)} %add_rsqrt_fusion.3), kind=kOutput, calls=%fused_computation.16 | convolution fusion | flops 5073743872 | bytes 24689664 | tf_op jit(solution)/shard_map/bld,de->ble/dot_general | solution.py:69
  34.2 4.7 %select_bitcast_fusion.1 = (bf16[4,1,3328,3]{3,2,0,1:T(8,128)(2,1)}, bf16[4,3,3328]{1,2,0:T(8,128)(2,1)S(1)}) fusion(pred[]{:T(512)S(6)} %eq.4, bf16[4,64,6448]{1,2,0:T(8,128)(2,1)} %copy-done.1), kind=kLoop, calls=%fused_computation.57 | loop fusion | flops 39936 | bytes 239617 | tf_op jit(solution)/shard_map/stack | solution.py:105
  50.3 11.0 %multiply_convert_fusion.1 = bf16[4,64,3328]{1,2,0:T(8,128)(2,1)S(1)} fusion(bf16[4,64,3328]{1,2,0:T(8,128)(2,1)S(1)} %slice-done.1, bf16[4,3,3328]{1,2,0:T(8,128)(2,1)} %copy.215, f32[3328]{0:T(1024)S(1)} %copy-done.18, f32[3328]{0:T(1024)S(1)} %copy-done.19, f32[3328]{0:T(1024)} %get-tuple-element.88, f32[3328]{0:T(1024)S(1)} %copy-done.17, ...), kind=kLoop, calls=%fused_computation.29 | loop fusion | flops 22151168 | bytes 3554304 | tf_op jit(solution)/shard_map/convert_element_type | solution.py:76
  64.2 4.7 %all-to-all-start.2 = ((bf16[4,64,2,4,128]{4,1,0,2,3:T(8,128)(2,1)}), bf16[4,64,2,4,128]{4,1,0,2,3:T(8,128)(2,1)}, u32[]{:S(2)}, u32[]{:S(2)}) async-start(bf16[4,64,2,4,128]{4,1,0,2,3:T(8,128)(2,1)} %reshape.534), calls=%async_computation.2 | async-start | bytes 1048576 | tf_op jit(solution)/shard_map/all_to_all | solution.py:82
  72.6 15.6 %copy.302 = bf16[4,64,3072]{1,0,2:T(4,128)(2,1)} copy(bf16[4,64,3072]{1,2,0:T(8,128)(2,1)S(1)} %slice-done.2) | data formatting | bytes 3145728 | tf_op jit(solution)/shard_map/slice | solution.py:80
  88.2 5.0 %reshape.598 = bf16[4,2,98304]{2,1,0:T(2,128)(2,1)} reshape(bf16[3072,4,64]{2,1,0:T(4,128)(2,1)} %bitcast.248) | data formatting | bytes 3145728
  104.5 13.0 %all-to-all-done = bf16[4,2,98304]{2,1,0:T(2,128)(2,1)} async-done(((bf16[4,2,98304]{2,1,0:T(2,128)(2,1)}), bf16[4,2,98304]{2,1,0:T(2,128)(2,1)}, u32[]{:S(2)}, u32[]{:S(2)}) %all-to-all-start) | async-done | bytes 1572896 | tf_op jit(solution)/shard_map/all_to_all | solution.py:80
  121.3 5.1 %copy.300 = f32[4,64,4,768]{1,2,3,0:T(4,128)} copy(bf16[4,64,4,768]{1,0,3,2:T(4,128)(2,1)S(1)} %bitcast.250) | data formatting | bytes 4718592 | tf_op jit(solution)/shard_map/while/body/eval_jaxpr/convert_element_type | solution.py:35
  126.3 5.7 %reshape.554 = f32[4,256,12,64]{1,3,2,0:T(8,128)S(1)} reshape(f32[4,4,64,768]{2,1,3,0:T(4,128)} %bitcast.244) | data formatting | bytes 6291456 | tf_op jit(solution)/shard_map/while/body/eval_jaxpr/convert_element_type | solution.py:35
  132.0 8.0 %reshape.557 = f32[4,256,1,12,64]{1,4,3,0,2:T(8,128)} reshape(f32[4,4,64,768]{2,1,3,0:T(4,128)} %bitcast.245) | data formatting | bytes 6291456 | tf_op jit(solution)/shard_map/while/body/eval_jaxpr/convert_element_type | solution.py:35
  152.1 18.7 %all-to-all-done.3 = bf16[4,256,768]{2,0,1:T(4,128)(2,1)S(1)} async-done(((bf16[4,256,768]{2,0,1:T(4,128)(2,1)}), bf16[4,256,768]{2,0,1:T(4,128)(2,1)S(1)}, u32[]{:S(2)}, u32[]{:S(2)}) %all-to-all-start.3) | async-done | bytes 1572896 | tf_op jit(solution)/shard_map/all_to_all | solution.py:89
  175.4 5.0 %multiply_reduce_fusion.1 = (f32[4,64]{1,0:T(4,128)S(1)}, f32[4,64,3072]{1,2,0:T(8,128)S(1)}) fusion(bf16[4,64,6448]{1,2,0:T(8,128)(2,1)} %copy-done.1, f32[4,64,4,768]{1,3,2,0:T(8,128)} %copy.236), kind=kLoop, calls=%fused_computation.46 | loop fusion | flops 6291200 | bytes 7865344 | tf_op jit(solution)/shard_map/reduce_sum | solution.py:92
  180.4 6.6 %multiply_reduce_fusion.2 = (f32[4,64]{1,0:T(4,128)S(1)}, f32[4,64,1536]{2,1,0:T(8,128)S(1)}) fusion(f32[4,64,1536]{2,1,0:T(8,128)S(1)} %copy-done.9, bf16[2,3072,1536]{2,1,0:T(8,128)(2,1)} %param.19, f32[4,64,3072]{1,2,0:T(8,128)S(1)} %get-tuple-element.100, f32[3072]{0:T(1024)S(1)} %bitcast.273, f32[4,64]{1,0:T(4,128)S(1)} %add_rsqrt_fusion.2), kind=kOutput, calls=%fused_computation.90 | convolution fusion | flops 2419457792 | bytes 15742976 | tf_op jit(solution)/shard_map/blgc,gcd->bld/dot_general | solution.py:93
  187.1 14.6 %fusion.19 = bf16[4,64,6448]{1,2,0:T(8,128)(2,1)S(1)} fusion(bf16[2,1536,6448]{1,2,0:T(8,128)(2,1)} %param.12, f32[4,64,1536]{2,1,0:T(8,128)S(1)} %get-tuple-element.118, f32[1536]{0:T(1024)S(1)} %copy-done.23, f32[4,64]{1,0:T(4,128)S(1)} %add_rsqrt_fusion.1), kind=kOutput, calls=%fused_computation.17 | convolution fusion | flops 5073743872 | bytes 24689664 | tf_op jit(solution)/shard_map/bld,de->ble/dot_general | solution.py:69
  221.2 11.2 %multiply_convert_fusion = bf16[4,64,3328]{1,2,0:T(8,128)(2,1)S(1)} fusion(bf16[4,64,3328]{1,2,0:T(8,128)(2,1)S(1)} %slice-done, bf16[4,3,3328]{1,2,0:T(8,128)(2,1)} %copy.240, f32[3328]{0:T(1024)} %get-tuple-element.82, f32[3328]{0:T(1024)} %get-tuple-element.83, f32[3328]{0:T(1024)} %get-tuple-element.84, f32[3328]{0:T(1024)} %get-tuple-element.81, ...), kind=kLoop, calls=%fused_computation.28 | loop fusion | flops 22151168 | bytes 3554304 | tf_op jit(solution)/shard_map/convert_element_type | solution.py:76
  245.6 15.6 %copy.301 = bf16[4,64,3072]{1,0,2:T(4,128)(2,1)} copy(bf16[4,64,3072]{1,2,0:T(8,128)(2,1)S(1)} %slice-done.3) | data formatting | bytes 3145728 | tf_op jit(solution)/shard_map/slice | solution.py:80
  261.1 5.0 %reshape.602 = bf16[4,2,98304]{2,1,0:T(2,128)(2,1)} reshape(bf16[3072,4,64]{2,1,0:T(4,128)(2,1)} %bitcast.249) | data formatting | bytes 3145728
  277.8 29.9 %all-to-all-done.4 = bf16[4,2,98304]{2,1,0:T(2,128)(2,1)} async-done(((bf16[4,2,98304]{2,1,0:T(2,128)(2,1)}), bf16[4,2,98304]{2,1,0:T(2,128)(2,1)}, u32[]{:S(2)}, u32[]{:S(2)}) %all-to-all-start.4) | async-done | bytes 1572896 | tf_op jit(solution)/shard_map/all_to_all | solution.py:80
  311.5 5.1 %copy.299 = f32[4,64,4,768]{1,2,3,0:T(4,128)} copy(bf16[4,64,4,768]{1,0,3,2:T(4,128)(2,1)S(1)} %bitcast.251) | data formatting | bytes 4718592 | tf_op jit(solution)/shard_map/while/body/eval_jaxpr/convert_element_type | solution.py:35
  316.6 5.7 %reshape.559 = f32[4,256,12,64]{1,3,2,0:T(8,128)S(1)} reshape(f32[4,4,64,768]{2,1,3,0:T(4,128)} %bitcast.246) | data formatting | bytes 6291456 | tf_op jit(solution)/shard_map/while/body/eval_jaxpr/convert_element_type | solution.py:35
  322.3 6.9 %reshape.562 = f32[4,256,1,12,64]{1,4,3,0,2:T(8,128)} reshape(f32[4,4,64,768]{2,1,3,0:T(4,128)} %bitcast.247) | data formatting | bytes 6291456 | tf_op jit(solution)/shard_map/while/body/eval_jaxpr/convert_element_type | solution.py:35
  343.9 59.8 %all-reduce.3.cloned.1.call-done = (bf16[4,1,3328,3]{3,2,0,1:T(8,128)(2,1)}, bf16[4,1,3328,3]{3,2,0,1:T(8,128)(2,1)}) async-done(((bf16[4,1,3328,3]{3,2,0,1:T(8,128)(2,1)}, bf16[4,1,3328,3]{3,2,0,1:T(8,128)(2,1)}), (bf16[4,1,3328,3]{3,2,0,1:T(8,128)(2,1)}, bf16[4,1,3328,3]{3,2,0,1:T(8,128)(2,1)})) %all-reduce.3.cloned.1.call-update) | async-done | bytes 159760 | tf_op jit(solution)/shard_map/psum | solution.py:95
  421.3 5.0 %multiply_reduce_fusion = (f32[4,64]{1,0:T(4,128)S(1)}, f32[4,64,3072]{1,2,0:T(8,128)S(1)}) fusion(bf16[4,64,6448]{1,2,0:T(8,128)(2,1)} %copy-done, f32[4,64,4,768]{1,3,2,0:T(8,128)} %copy.261), kind=kLoop, calls=%fused_computation.41 | loop fusion | flops 6291200 | bytes 7865344 | tf_op jit(solution)/shard_map/reduce_sum | solution.py:92
  426.3 7.7 %fusion.67 = f32[4,64,1536]{2,1,0:T(8,128)} fusion(f32[4,64,1536]{2,1,0:T(8,128)S(1)} %copy-done.8, bf16[2,3072,1536]{2,1,0:T(8,128)(2,1)} %param.19, f32[4,64,3072]{1,2,0:T(8,128)S(1)} %get-tuple-element.96, f32[3072]{0:T(1024)S(1)} %bitcast.272, f32[4,64]{1,0:T(4,128)S(1)} %add_rsqrt_fusion), kind=kOutput, calls=%fused_computation.82 | convolution fusion | flops 2418671616 | bytes 15741952 | tf_op jit(solution)/shard_map/blgc,gcd->bld/dot_general | solution.py:93
  (204 shorter events, 141.8 us)
Async XLA Ops:
  29.7 33.6 %all-to-all-start.1 = ((bf16[4,2,1536]{2,1,0:T(2,128)(2,1)}), bf16[4,2,1536]{2,1,0:T(2,128)(2,1)S(1)}, u32[]{:S(2)}, u32[]{:S(2)}) async-start(bf16[4,2,1536]{2,1,0:T(2,128)(2,1)} %reshape.596), calls=%async_computation.1 | async-start | bytes 49152 | tf_op jit(solution)/shard_map/all_to_all | solution.py:81
  41.5 4.4 %copy-start.21 = (f32[2,3328]{1,0:T(2,128)S(1)}, f32[2,3328]{1,0:T(2,128)}, u32[]{:S(2)}) copy-start(f32[2,3328]{1,0:T(2,128)} %param.14) | copy-start | bytes 79876
  41.5 5.1 %collective-permute-start = (bf16[4,3,3328]{2,0,1:T(4,128)(2,1)}, bf16[4,3,3328]{2,0,1:T(4,128)(2,1)}, u32[]{:S(2)}, u32[]{:S(2)}) collective-permute-start(bf16[4,3,3328]{2,0,1:T(4,128)(2,1)} %copy.214), channel_id=1, source_target_pairs={{0,1},{1,2},{2,3},{4,5},{5,6},{6,7},{8,9},{9,10},{10,11},{12,13},{... | collective-permute-start | bytes 239624 | tf_op jit(solution)/shard_map/ppermute | solution.py:73
  44.7 5.6 %slice-start.1 = ((bf16[4,64,6448]{1,2,0:T(8,128)(2,1)}), bf16[4,64,3328]{1,2,0:T(8,128)(2,1)S(1)}, s32[]{:S(2)}) async-start(bf16[4,64,6448]{1,2,0:T(8,128)(2,1)} %copy-done.1), calls=%async_computation.10 | async-start | bytes 6815744 | tf_op jit(solution)/shard_map/slice | solution.py:71
  64.2 28.9 %all-to-all-start.2 = ((bf16[4,64,2,4,128]{4,1,0,2,3:T(8,128)(2,1)}), bf16[4,64,2,4,128]{4,1,0,2,3:T(8,128)(2,1)}, u32[]{:S(2)}, u32[]{:S(2)}) async-start(bf16[4,64,2,4,128]{4,1,0,2,3:T(8,128)(2,1)} %reshape.534), calls=%async_computation.2 | async-start | bytes 1048576 | tf_op jit(solution)/shard_map/all_to_all | solution.py:82
  93.2 24.3 %all-to-all-start = ((bf16[4,2,98304]{2,1,0:T(2,128)(2,1)}), bf16[4,2,98304]{2,1,0:T(2,128)(2,1)}, u32[]{:S(2)}, u32[]{:S(2)}) async-start(bf16[4,2,98304]{2,1,0:T(2,128)(2,1)} %reshape.598), calls=%async_computation | async-start | bytes 3145728 | tf_op jit(solution)/shard_map/all_to_all | solution.py:80
  132.0 8.0 %copy-start.4 = (f32[4,256,12,64]{1,3,2,0:T(8,128)}, f32[4,256,12,64]{1,3,2,0:T(8,128)S(1)}, u32[]{:S(2)}) copy-start(f32[4,256,12,64]{1,3,2,0:T(8,128)S(1)} %reshape.554) | copy-start | bytes 9437188
  145.0 6.7 %copy-start.22 = (f32[2,1,3072]{2,1,0:T(1,128)S(1)}, f32[2,1,3072]{2,1,0:T(1,128)}, u32[]{:S(2)}) copy-start(f32[2,1,3072]{2,1,0:T(1,128)} %param.18) | copy-start | bytes 73732
  147.2 23.6 %all-to-all-start.3 = ((bf16[4,256,768]{2,0,1:T(4,128)(2,1)}), bf16[4,256,768]{2,0,1:T(4,128)(2,1)S(1)}, u32[]{:S(2)}, u32[]{:S(2)}) async-start(bf16[4,256,768]{2,0,1:T(4,128)(2,1)} %copy.234), calls=%async_computation.3 | async-start | bytes 3145728 | tf_op jit(solution)/shard_map/all_to_all | solution.py:89
  175.4 5.1 %copy-start.9 = (f32[4,64,1536]{2,1,0:T(8,128)S(1)}, f32[4,64,1536]{2,1,0:T(8,128)}, u32[]{:S(2)}) copy-start(f32[4,64,1536]{2,1,0:T(8,128)} %param.10) | copy-start | bytes 4718596
  180.4 6.7 %copy-start.23 = (f32[1536]{0:T(1024)S(1)}, f32[1536]{0:T(1024)}, u32[]{:S(2)}) copy-start(f32[1536]{0:T(1024)} %get-tuple-element.91) | copy-start | bytes 18436
  187.1 14.7 %copy-start.7 = (f32[4,64,1536]{2,1,0:T(8,128)}, f32[4,64,1536]{2,1,0:T(8,128)S(1)}, u32[]{:S(2)}) copy-start(f32[4,64,1536]{2,1,0:T(8,128)S(1)} %get-tuple-element.118) | copy-start | bytes 4718596
  205.5 4.7 %copy-start.26 = (f32[48]{0:T(128)S(1)}, f32[48]{0:T(128)}, u32[]{:S(2)}) copy-start(f32[48]{0:T(128)} %get-tuple-element.115) | copy-start | bytes 580
  208.1 9.4 %collective-permute-start.1 = (bf16[4,3,3328]{2,0,1:T(4,128)(2,1)}, bf16[4,3,3328]{2,0,1:T(4,128)(2,1)}, u32[]{:S(2)}, u32[]{:S(2)}) collective-permute-start(bf16[4,3,3328]{2,0,1:T(4,128)(2,1)} %copy.239), channel_id=1, source_target_pairs={{0,1},{1,2},{2,3},{4,5},{5,6},{6,7},{8,9},{9,10},{10,11},{12,13},{... | collective-permute-start | bytes 239624 | tf_op jit(solution)/shard_map/ppermute | solution.py:73
  211.1 10.1 %slice-start = ((bf16[4,64,6448]{1,2,0:T(8,128)(2,1)}), bf16[4,64,3328]{1,2,0:T(8,128)(2,1)S(1)}, s32[]{:S(2)}) async-start(bf16[4,64,6448]{1,2,0:T(8,128)(2,1)} %copy-done), calls=%async_computation.9 | async-start | bytes 6815744 | tf_op jit(solution)/shard_map/slice | solution.py:71
  211.1 10.1 %copy-start.16 = (f32[3328]{0:T(1024)S(1)}, f32[3328]{0:T(1024)}, u32[]{:S(2)}) copy-start(f32[3328]{0:T(1024)} %get-tuple-element.89) | copy-start | bytes 39940
  213.6 20.8 %all-to-all-start.5 = ((bf16[4,2,1536]{2,1,0:T(2,128)(2,1)}), bf16[4,2,1536]{2,1,0:T(2,128)(2,1)}, u32[]{:S(2)}, u32[]{:S(2)}) async-start(bf16[4,2,1536]{2,1,0:T(2,128)(2,1)} %reshape.600), calls=%async_computation.5 | async-start | bytes 49152 | tf_op jit(solution)/shard_map/all_to_all | solution.py:81
  235.4 30.8 %all-to-all-start.6 = ((bf16[4,64,2,4,128]{4,1,0,2,3:T(8,128)(2,1)}), bf16[4,64,2,4,128]{4,1,0,2,3:T(8,128)(2,1)}, u32[]{:S(2)}, u32[]{:S(2)}) async-start(bf16[4,64,2,4,128]{4,1,0,2,3:T(8,128)(2,1)} %reshape.547), calls=%async_computation.6 | async-start | bytes 1048576 | tf_op jit(solution)/shard_map/all_to_all | solution.py:82
  239.5 164.2 %all-reduce.3.cloned.1.call-start = ((), (), s32[]{:S(2)}) async-start(), calls=%async_computation.8 | async-start | bytes 13631488 | tf_op jit(solution)/shard_map/psum | solution.py:95
  261.1 9.8 %copy-start.25 = (f32[12]{0:T(128)S(1)}, f32[12]{0:T(128)}, u32[]{:S(2)}) copy-start(f32[12]{0:T(128)} %get-tuple-element.119) | copy-start | bytes 148
  266.2 41.6 %all-to-all-start.4 = ((bf16[4,2,98304]{2,1,0:T(2,128)(2,1)}), bf16[4,2,98304]{2,1,0:T(2,128)(2,1)}, u32[]{:S(2)}, u32[]{:S(2)}) async-start(bf16[4,2,98304]{2,1,0:T(2,128)(2,1)} %reshape.602), calls=%async_computation.4 | async-start | bytes 3145728 | tf_op jit(solution)/shard_map/all_to_all | solution.py:80
  322.3 6.9 %copy-start.20 = (pred[256,256]{1,0:T(8,128)(4,1)S(1)}, pred[256,256]{1,0:T(8,128)(4,1)}, u32[]{:S(2)}) copy-start(pred[256,256]{1,0:T(8,128)(4,1)} %iota_compare_fusion) | copy-start | bytes 196612
  339.2 76.1 %all-to-all-start.7 = ((bf16[4,256,768]{2,0,1:T(4,128)(2,1)}), bf16[4,256,768]{2,0,1:T(4,128)(2,1)}, u32[]{:S(2)}, u32[]{:S(2)}) async-start(bf16[4,256,768]{2,0,1:T(4,128)(2,1)} %copy.259), calls=%async_computation.7 | async-start | bytes 3145728 | tf_op jit(solution)/shard_map/all_to_all | solution.py:89
  421.3 5.1 %copy-start.8 = (f32[4,64,1536]{2,1,0:T(8,128)S(1)}, f32[4,64,1536]{2,1,0:T(8,128)}, u32[]{:S(2)}) copy-start(f32[4,64,1536]{2,1,0:T(8,128)} %copy-done.7) | copy-start | bytes 4718596
  (19 other events, 61.4 us)
Sparse Core Ops, SparseCore 0:
  243.8 159.8 all-reduce.2
where the time goes:
time: 448 us; the launch traced here: 441 us
  local copies, waits for them, and re-layouts  151 us (34%)
  waiting for transfers between devices  121 us (27%)
  matrix products  62.4 us (14%)
  other arithmetic  51.2 us (11%)
  starting transfers between devices  40.3 us (9%)
  between operations  15.2 us (3%)
    psum x1, waiting for transfers between devices, layer(): conv_state = lax.psum(tail_rows, 'sp')  59.8 us
    all_to_all x2, waiting for transfers between devices, layer(): x_local = lax.all_to_all(activated[..., :d_inner], 'sp', 2, 1, tiled=True)  43 us
    convert_element_type x6, local copies, waits for them, and re-layouts, body(): x_float = x_chunk.astype(jnp.float32)  36.3 us
    unnamed x66, local copies, waits for them, and re-layouts  32.4 us
    slice x6, local copies, waits for them, and re-layouts, layer(): x_local = lax.all_to_all(activated[..., :d_inner], 'sp', 2, 1, tiled=True)  32 us
    dot_general x2, matrix products, layer(): jnp.einsum('bld,de->ble', normed, w_in_l, preferred_element_type=jnp.floa...  29.2 us
    convert_element_type x2, other arithmetic, layer(): activated = jax.nn.silu(conv_out).astype(jnp.bfloat16)  22.3 us
    all_to_all x2, waiting for transfers between devices, layer(): lax.all_to_all(y_local.reshape(batch, seq_len, local_heads * head_dim), '...  18.7 us
  transfers between devices with their start and end apart: 11, of which 4 were waited for; matrix products, arithmetic and copies ran while one was open for 34% of the time, Pallas kernels for 0%

commit v1 on v0

v1 whole, which is shorter than its diff:
```python
import jax
import jax.numpy as jnp
from jax import lax
from jax.experimental import pallas as pl
from jax.experimental.pallas import tpu as pltpu
from jax.sharding import PartitionSpec as P

F32 = jnp.float32
BF16 = jnp.bfloat16
EPSILON = 1e-5
LAYERS = 2
NB = 4
SEG = 64
BLK = 128
HALO = 16
EXT = BLK + HALO
ROWS = HALO + 2 * BLK
D_MODEL = 1536
D_INNER = 3072
CONV_DIM = 3328
HEADS = 48
HALF = 768
LOC = 1536
ACT = LOC + 256
PAIRS = 12
NT = (((1,), (1,)), ((), ()))


def dot(a, b):
    return jnp.dot(a, b, preferred_element_type=F32)


def dot_nt(a, b):
    return lax.dot_general(a, b, NT, preferred_element_type=F32)


def round_bf16(v):
    return v.astype(BF16).astype(F32)


def silu(v):
    half = 0.5 * v
    return half * jnp.tanh(half) + half


def head_row(i):
    return i if i < 12 else i + 12


def kernel(resid_ref, pre_ref, w_in_ref, cw_ref, cb_ref, dtb_ref, alog_ref, dskip_ref, gw_ref, w_out_ref,
           r_out, ssm_out, tail_out,
           hbuf, sz, wz, wx, wbc, wout, raw, act_o, act_r, yloc, ybuf, yrecv, gn, stg, tails, tail_o, tail_r,
           cum_o, cumt_o, cumt_r, dtt_o, dtt_r, cwl, prm,
           wsem, hsend, hrecv, ysend, yrecv_sem, tsend, trecv, osem):
    me = lax.axis_index('sp')
    chip = me // 2
    core = me % 2
    partner = chip * 2 + (1 - core)
    other = (1 - chip) * 2 + core
    chip_f = chip.astype(F32)
    core_f = core.astype(F32)

    def weight_copies(l):
        zc = [pltpu.make_async_copy(w_in_ref.at[l, pl.ds(HALF * j, HALF), :], wz.at[pl.ds(HALF * j, HALF), :], wsem.at[j]) for j in range(4)]
        xc = [pltpu.make_async_copy(w_in_ref.at[l, pl.ds(pl.multiple_of(D_INNER + LOC * b + HALF * core, 16), HALF), :], wx.at[pl.ds(HALF * b, HALF), :], wsem.at[4 + b]) for b in range(2)]
        bc = pltpu.make_async_copy(w_in_ref.at[l, pl.ds(2 * D_INNER, 304), :], wbc.at[pl.ds(0, 304), :], wsem.at[6])
        oc = pltpu.make_async_copy(w_out_ref.at[l], wout, wsem.at[7])
        return zc, xc, bc, oc

    zc0, xc0, bc0, oc0 = weight_copies(0)
    for c in zc0 + xc0 + [bc0, oc0]:
        c.start()

    barrier = pltpu.get_barrier_semaphore()
    for step in range(1, 4):
        pl.semaphore_signal(barrier, inc=1, device_id={'sp': (me + step) % 4}, device_id_type=pl.DeviceIdType.MESH)

    hbuf[:, 0:HALO, :] = jnp.zeros((LAYERS * NB, HALO, D_MODEL), BF16)
    wbc[304:384, :] = jnp.zeros((80, D_MODEL), BF16)
    prm[...] = jnp.zeros((8, 128), F32)
    r_out[...] = resid_ref[...]
    pl.semaphore_wait(barrier, 3)

    own_row = pl.multiple_of(HALO + BLK * chip + SEG * core, 16)
    oth_row = pl.multiple_of(HALO + BLK * (1 - chip) + SEG * core, 16)
    own_blk = pl.multiple_of(BLK * chip, 16)
    oth_blk = pl.multiple_of(BLK * (1 - chip), 16)

    iota_r = lax.broadcasted_iota(jnp.int32, (BLK, BLK), 0)
    iota_c = lax.broadcasted_iota(jnp.int32, (BLK, BLK), 1)

    def remote(src, dst, ssem, rsem, dev):
        return pltpu.make_async_remote_copy(src_ref=src, dst_ref=dst, send_sem=ssem, recv_sem=rsem, device_id={'sp': dev}, device_id_type=pl.DeviceIdType.MESH)

    def layer(l, carry):
        lb = NB * l
        tri = (iota_r >= iota_c).astype(F32)
        low = iota_c < 64

        def norm_body(p, c):
            v = r_out[p]
            ms = jnp.mean(v * v, axis=-1, keepdims=True)
            hbuf[lb + p, pl.ds(own_row, SEG), :] = (v * lax.rsqrt(ms + EPSILON) * pre_ref[l]).astype(BF16)
            return c
        lax.fori_loop(0, NB, norm_body, 0)

        def hslice(p0, n, row, size):
            return hbuf.at[pl.ds(lb + p0, n), pl.ds(row, size), :]

        def same(idx, p0, n, row, size, dev):
            s = hslice(p0, n, row, size)
            return remote(s, s, hsend.at[l, idx], hrecv.at[l, idx], dev)

        c_par = same(0, 0, NB, own_row, SEG, partner)
        c_tail = same(1, 0, NB, own_row + 48, 16, other)
        c_r0 = same(2, 0, 2, own_row, 48, other)
        c_r1 = same(3, 2, 2, own_row, 48, other)
        f_tail = same(4, 0, NB, oth_row + 48, 16, partner)
        f_r0 = same(5, 0, 2, oth_row, 48, partner)
        f_r1 = same(6, 2, 2, oth_row, 48, partner)
        c_tail.start()
        c_par.start()
        c_r0.start()
        c_r1.start()

        zc, xc, bc, oc = weight_copies(l)
        znx, xnx, bnx, onx = weight_copies(1)

        for b in range(2):
            src = pl.multiple_of(LOC * b + HALF * core, 128)
            cwl[0:4, HALF * b:HALF * (b + 1)] = cw_ref[l, :, pl.ds(src, HALF)]
            cwl[4:5, HALF * b:HALF * (b + 1)] = cb_ref[l, :, pl.ds(src, HALF)]
        cwl[0:4, LOC:ACT] = cw_ref[l, :, D_INNER:CONV_DIM]
        cwl[4:5, LOC:ACT] = cb_ref[l, :, D_INNER:CONV_DIM]
        prm[0:1, 0:HEADS] = dtb_ref[l]
        prm[1:2, 0:HEADS] = -jnp.exp(alog_ref[l])

        for c in zc:
            c.wait()

        def z_body(n, c):
            lhs = hbuf[pl.ds(lb, NB), pl.ds(own_row, SEG), :].reshape(NB * SEG, D_MODEL)
            z = round_bf16(dot_nt(lhs, wz[pl.ds(pl.multiple_of(512 * n, 512), 512), :]))
            sz[:, :, pl.ds(pl.multiple_of(512 * n, 512), 512)] = silu(z).reshape(NB, SEG, 512)
            return c
        lax.fori_loop(0, 6, z_body, 0)

        @pl.when(l == 0)
        def _():
            for c in znx:
                c.start()

        def conv_chunk(act, i, p, src_col, dst_col, width):
            for s in range(width // 128):
                cols = pl.ds(src_col + 128 * s, 128)
                dcol = pl.ds(dst_col + 128 * s if isinstance(dst_col, int) else pl.multiple_of(dst_col + 128 * s, 128), 128)
                acc = cwl[0:1, dcol] * raw[i, 13:141, cols]
                for k in range(1, 4):
                    acc = acc + cwl[k:k + 1, dcol] * raw[i, 13 + k:141 + k, cols]
                act[p, :, dcol] = silu(acc + cwl[4:5, dcol]).astype(BF16)

        def block(p0, np_, row, act, tail, cumt, dtt, cum):
            def lhs():
                return hbuf[pl.ds(lb + p0, np_), pl.ds(row, EXT), :].reshape(np_ * EXT, D_MODEL)

            raw[0:np_, :, 0:384] = round_bf16(dot_nt(lhs(), wbc[...])).reshape(np_, EXT, 384)

            def bc_body(i, c):
                p = p0 + i
                tail[p, :, LOC:ACT] = raw[i, BLK:EXT, 0:256].astype(BF16)
                conv_chunk(act, i, p, 0, LOC, 256)
                v = raw[i, HALO:EXT, 256:384] + prm[0:1, :]
                dt = round_bf16(jnp.maximum(v, 0.0) + jnp.log1p(jnp.exp(-jnp.abs(v))))
                logs = dt * prm[1:2, :]
                dt = dt * (1.0 - core_f) + pltpu.roll(dt, 116, 1) * core_f
                logs = logs * (1.0 - core_f) + pltpu.roll(logs, 116, 1) * core_f
                cums = jnp.dot(tri, logs, precision=lax.Precision.HIGHEST, preferred_element_type=F32)
                cumt[p] = cums.T[0:40]
                dtt[p] = dt.T[0:40]
                if cum is not None:
                    cum[p] = cums
                return c
            lax.fori_loop(0, np_, bc_body, 0)

            def x_body(n, c):
                col = pl.multiple_of(512 * n, 512)
                raw[0:np_, :, :] = round_bf16(dot_nt(lhs(), wx[pl.ds(col, 512), :])).reshape(np_, EXT, 512)

                def conv_body(i, cc):
                    tail[p0 + i, :, pl.ds(col, 512)] = raw[i, BLK:EXT, :].astype(BF16)
                    conv_chunk(act, i, p0 + i, 0, col, 512)
                    return cc
                lax.fori_loop(0, np_, conv_body, 0)
                return c
            lax.fori_loop(0, 3, x_body, 0)

        c_par.wait_recv()
        c_tail.wait_recv()
        f_tail.start()
        bc.wait()
        for c in xc:
            c.wait()
        f_tail.wait_recv()
        block(0, NB, own_blk, act_o, tail_o, cumt_o, dtt_o, cum_o)
        c_r0.wait_recv()
        f_r0.start()

        def intra_body(p, c):
            cb = act_o[p, :, LOC + 128:ACT]
            scores = dot_nt(cb, act_o[p, :, LOC:LOC + 128]) * tri
            for j in range(PAIRS):
                mats = []
                for i in (2 * j, 2 * j + 1):
                    h = head_row(i)
                    col = jnp.broadcast_to(cum_o[p, :, h:h + 1], (BLK, BLK))
                    mats.append(jnp.exp(jnp.minimum(col - cumt_o[p, h:h + 1, :], 0.0)) * (scores * dtt_o[p, h:h + 1, :]))
                xp = act_o[p, :, 128 * j:128 * (j + 1)].astype(F32)
                rhs = jnp.concatenate([jnp.where(low, xp, 0.0), jnp.where(low, 0.0, xp)], axis=0)
                blk = (0 if j < 6 else 24) + 12 * core + (2 * j) % 12
                dv = jnp.where(low[0:1], dskip_ref[l, blk], dskip_ref[l, blk + 1])
                yloc[p, :, 128 * j:128 * (j + 1)] = dot(jnp.concatenate(mats, axis=1), rhs) + dv * xp
            return c
        lax.fori_loop(0, NB, intra_body, 0)

        def y_copy(p):
            src = ybuf.at[p, pl.ds(pl.multiple_of(SEG * (1 - core), 16), SEG), :]
            return remote(src, yrecv.at[lb + p], ysend.at[l, p], yrecv_sem.at[l, p], partner)

        def out_copy(p, ll):
            return pltpu.make_async_copy(stg.at[p], ssm_out.at[p, ll], osem.at[p])

        def decays(p, h, cumt, dtt, extra):
            row = cumt[p, pl.ds(h, 1), :]
            return dtt[p, pl.ds(h, 1), :] * jnp.exp(row[:, 127:128] - row + extra)

        def inter_body(p, c):
            bt = act_r[p, :, LOC:LOC + 128].astype(F32).T
            cf = act_o[p, :, LOC + 128:ACT].astype(F32)
            for j in range(PAIRS):
                ha, hb = head_row(2 * j), head_row(2 * j + 1)
                lhs = jnp.concatenate([bt * decays(p, h, cumt_r, dtt_r, 0.0) for h in (ha, hb)], axis=1)
                xp = act_r[p, :, 128 * j:128 * (j + 1)].astype(F32)
                rhs = jnp.concatenate([jnp.where(low, xp, 0.0), jnp.where(low, 0.0, xp)], axis=0)
                state = dot(lhs, rhs)
                ca = jnp.broadcast_to(cum_o[p, :, ha:ha + 1], (BLK, BLK))
                cb = jnp.broadcast_to(cum_o[p, :, hb:hb + 1], (BLK, BLK))
                y = yloc[p, :, 128 * j:128 * (j + 1)] + chip_f * (dot(cf, state) * jnp.exp(jnp.where(low, ca, cb)))
                ybuf[p, :, 128 * j:128 * (j + 1)] = y.astype(BF16)
            y_copy(p).start()

            @pl.when(l > 0)
            def _():
                out_copy(p, 0).wait()
            bto = act_o[p, :, LOC:LOC + 128].astype(F32).T

            def final_body(q, cc):
                h = 24 * chip + 2 * q
                cols = pl.ds(pl.multiple_of(128 * (6 * chip + q), 128), 128)
                left, right = [], []
                for hh in (h, h + 1):
                    end_o = cumt_o[p, pl.ds(hh, 1), :][:, 127:128]
                    end_r = cumt_r[p, pl.ds(hh, 1), :][:, 127:128]
                    left.append(bto * decays(p, hh, cumt_o, dtt_o, end_r * (1.0 - chip_f)))
                    right.append(bt * decays(p, hh, cumt_r, dtt_r, end_o * chip_f))
                xo = act_o[p, :, cols].astype(F32)
                xr = act_r[p, :, cols].astype(F32)
                rhs = jnp.concatenate([jnp.where(low, xo, 0.0), jnp.where(low, 0.0, xo), jnp.where(low, xr, 0.0), jnp.where(low, 0.0, xr)], axis=0)
                state = dot(jnp.concatenate(left + right, axis=1), rhs)
                stg[p, pl.ds(2 * q, 2)] = state.T.reshape(2, 64, 128)
                return cc
            lax.fori_loop(0, 6, final_body, 0)
            out_copy(p, l).start()
            return c

        c_r1.wait_recv()
        f_r1.start()
        f_r0.wait_recv()
        block(0, 2, oth_blk, act_r, tail_r, cumt_r, dtt_r, None)
        lax.fori_loop(0, 2, inter_body, 0)
        f_r1.wait_recv()
        block(2, 2, oth_blk, act_r, tail_r, cumt_r, dtt_r, None)
        lax.fori_loop(2, NB, inter_body, 0)

        @pl.when(l == 0)
        def _():
            for c in xnx + [bnx]:
                c.start()

        def put_tail(src):
            for b in range(2):
                tails[l, :, :, pl.ds(pl.multiple_of(LOC * b + HALF * core, 128), HALF)] = src[:, :, HALF * b:HALF * (b + 1)]
            tails[l, :, :, D_INNER:CONV_DIM] = src[:, :, LOC:ACT]

        @pl.when(chip == 1)
        def _():
            put_tail(tail_o)

        @pl.when(chip == 0)
        def _():
            put_tail(tail_r)
        t_copies = []
        for b in range(2):
            ts = tails.at[l, :, :, pl.ds(pl.multiple_of(LOC * b + HALF * core, 128), HALF)]
            t_copies.append(remote(ts, ts, tsend.at[l, b], trecv.at[l, b], partner))
        for c in t_copies:
            c.start()

        def gate_body(p, c):
            y_copy(p).wait()
            total = jnp.zeros((SEG, 1), F32)
            for b in range(2):
                for own in range(2):
                    cols = pl.ds(pl.multiple_of(LOC * b + HALF * (core if own else 1 - core), 128), HALF)
                    if own:
                        y = ybuf[p, pl.ds(pl.multiple_of(SEG * core, 16), SEG), HALF * b:HALF * (b + 1)]
                    else:
                        y = yrecv[lb + p, :, HALF * b:HALF * (b + 1)]
                    g = y.astype(F32) * sz[p, :, cols]
                    sz[p, :, cols] = g
                    total = total + jnp.sum(g * g, axis=-1, keepdims=True)
            scale = lax.rsqrt(total * (1.0 / D_INNER) + EPSILON)
            for b in range(4):
                cols = slice(HALF * b, HALF * (b + 1))
                gn[p, :, cols] = (sz[p, :, cols] * scale * gw_ref[l, :, cols]).astype(BF16)
            return c
        lax.fori_loop(0, NB, gate_body, 0)

        oc.wait()

        def out_body(n, c):
            cols = pl.ds(pl.multiple_of(512 * n, 512), 512)
            o = dot(gn[...].reshape(NB * SEG, D_INNER), wout[:, cols])
            r_out[:, :, cols] = r_out[:, :, cols] + o.reshape(NB, SEG, 512)
            return c
        lax.fori_loop(0, 3, out_body, 0)

        @pl.when(l == 0)
        def _():
            onx.start()

        for c in [c_par, c_tail, c_r0, c_r1, f_tail, f_r0, f_r1]:
            c.wait_send()
        for c in t_copies:
            c.wait()
        return carry

    lax.fori_loop(0, LAYERS, layer, 0)
    for p in range(NB):
        pltpu.make_async_copy(stg.at[p], ssm_out.at[p, LAYERS - 1], osem.at[p]).wait()
    tail_out[...] = tails[...]


def solution(mesh):
    vmem = pl.BlockSpec(memory_space=pltpu.VMEM)
    hbm = pl.BlockSpec(memory_space=pl.ANY)
    smem = pl.BlockSpec(memory_space=pltpu.SMEM)

    def forward(resid, pre_norm, w_in, conv_w, conv_b, dt_bias, a_log, d_skip, gate_norm, w_out):
        r, ssm, tails = pl.pallas_call(
            kernel,
            out_shape=(
                jax.ShapeDtypeStruct((NB, SEG, D_MODEL), F32),
                jax.ShapeDtypeStruct((NB, LAYERS, 12, 64, 128), F32),
                jax.ShapeDtypeStruct((LAYERS, NB, 16, CONV_DIM), BF16),
            ),
            in_specs=[vmem, vmem, hbm, vmem, vmem, vmem, vmem, smem, vmem, hbm],
            out_specs=(vmem, hbm, vmem),
            scratch_shapes=[
                pltpu.VMEM((LAYERS * NB, ROWS, D_MODEL), BF16),
                pltpu.VMEM((NB, SEG, D_INNER), F32),
                pltpu.VMEM((D_INNER, D_MODEL), BF16),
                pltpu.VMEM((LOC, D_MODEL), BF16),
                pltpu.VMEM((384, D_MODEL), BF16),
                pltpu.VMEM((D_INNER, D_MODEL), BF16),
                pltpu.VMEM((NB, EXT, 512), F32),
                pltpu.VMEM((NB, BLK, ACT), BF16),
                pltpu.VMEM((NB, BLK, ACT), BF16),
                pltpu.VMEM((NB, BLK, LOC), F32),
                pltpu.VMEM((NB, BLK, LOC), BF16),
                pltpu.VMEM((LAYERS * NB, SEG, LOC), BF16),
                pltpu.VMEM((NB, SEG, D_INNER), BF16),
                pltpu.VMEM((NB, 12, 64, 128), F32),
                pltpu.VMEM((LAYERS, NB, 16, CONV_DIM), BF16),
                pltpu.VMEM((NB, 16, ACT), BF16),
                pltpu.VMEM((NB, 16, ACT), BF16),
                pltpu.VMEM((NB, BLK, BLK), F32),
                pltpu.VMEM((NB, 40, BLK), F32),
                pltpu.VMEM((NB, 40, BLK), F32),
                pltpu.VMEM((NB, 40, BLK), F32),
                pltpu.VMEM((NB, 40, BLK), F32),
                pltpu.VMEM((8, ACT), F32),
                pltpu.VMEM((8, 128), F32),
                pltpu.SemaphoreType.DMA((8,)),
                pltpu.SemaphoreType.DMA((LAYERS, 7)),
                pltpu.SemaphoreType.DMA((LAYERS, 7)),
                pltpu.SemaphoreType.DMA((LAYERS, NB)),
                pltpu.SemaphoreType.DMA((LAYERS, NB)),
                pltpu.SemaphoreType.DMA((LAYERS, 2)),
                pltpu.SemaphoreType.DMA((LAYERS, 2)),
                pltpu.SemaphoreType.DMA((NB,)),
            ],
            compiler_params=pltpu.CompilerParams(collective_id=0, has_side_effects=True, vmem_limit_bytes=67043328),
        )(resid, pre_norm.reshape(LAYERS, 1, D_MODEL), jnp.swapaxes(w_in, 1, 2), jnp.swapaxes(conv_w, 1, 2), conv_b.reshape(LAYERS, 1, CONV_DIM),
          dt_bias.reshape(LAYERS, 1, HEADS), a_log.reshape(LAYERS, 1, HEADS), d_skip, gate_norm, w_out)
        conv_state = jnp.transpose(tails[:, :, 13:16, :], (1, 0, 3, 2))
        return r, ssm, conv_state

    return jax.shard_map(forward, mesh=mesh, in_specs=(P('dp', 'sp', None), P(), P(), P(), P(), P(), P(), P(), P(), P()), out_specs=(P('dp', 'sp', None), P('dp', None, 'sp', None, None), P('dp', None, None, None)), check_vma=False)
```

time: 448 us -> 121 us (0.27); the launches traced: 441 us -> 120 us
  local copies, waits for them, and re-layouts: 151 us -> 9.08 us
  waiting for transfers between devices: 121 us -> 0 us
  Pallas kernels: 0 us -> 111 us
  matrix products: 62.4 us -> 0 us
  other arithmetic: 51.2 us -> 0 us
  starting transfers between devices: 40.3 us -> 0 us
  between operations: 15.2 us -> 0.65 us
    pallas_call x0 -> x1, Pallas kernels: none -> 111 us  [forward(): pl.pallas_call(kernel, out_shape=(jax.ShapeDtypeStruct((NB, SEG, D_MODEL)...]
    dot_general x12 -> x0, matrix products: 62.4 us -> none  [the longest x2 29.2 us: layer(): jnp.einsum('bld,de->ble', normed, w_in_l, preferred_element_type=jnp.floa...]
    all_to_all x8 -> x0, waiting for transfers between devices: 61.6 us -> none  [the longest x2 43 us: layer(): x_local = lax.all_to_all(activated[..., :d_inner], 'sp', 2, 1, tiled=True)]
    psum x1 -> x0, waiting for transfers between devices: 59.8 us -> none  [layer(): conv_state = lax.psum(tail_rows, 'sp')]
    convert_element_type x18 -> x0, local copies, waits for them, and re-layouts: 45.6 us -> none  [the longest x6 36.3 us: body(): x_float = x_chunk.astype(jnp.float32)]
    slice x25 -> x0, local copies, waits for them, and re-layouts: 42.6 us -> none  [the longest x6 32 us: layer(): x_local = lax.all_to_all(activated[..., :d_inner], 'sp', 2, 1, tiled=True)]
    all_to_all x8 -> x0, starting transfers between devices: 34.6 us -> none  [the longest x2 9.1 us: layer(): x_local = lax.all_to_all(activated[..., :d_inner], 'sp', 2, 1, tiled=True)]
    unnamed x66 -> x5, local copies, waits for them, and re-layouts: 32.4 us -> 5.13 us
  transfers between devices with their start and end apart: 11 -> 0, of which waited for: 4 -> 0; matrix products, arithmetic and copies ran while one was open for 34% -> 0% of each run, Pallas kernels for 0% -> 0%
where the time goes in v1:
time: 121 us; the launch traced here: 120 us
  Pallas kernels  111 us (92%)
  local copies, waits for them, and re-layouts  9.08 us (8%)
    pallas_call x1, Pallas kernels, forward(): pl.pallas_call(kernel, out_shape=(jax.ShapeDtypeStruct((NB, SEG, D_MODEL)...  111 us
    unnamed x5, local copies, waits for them, and re-layouts  5.13 us

profile of v1, /device:TPU:0, one launch (start us, length us, event | category | flops | bytes accessed | tf_op | source)
XLA Modules:
  0.0 120.5 jit_solution(11758478659897493425)
XLA Ops:
  0.6 1.3 %reshape.18.pre_ref = f32[2,1,1536]{2,1,0:T(1,128)} reshape(f32[2,1536]{1,0:T(2,128)} %param.11) | data formatting | bytes 24576 | tf_op jit(solution)/shard_map/reshape | solution.py:403
  1.9 1.4 %reshape.19.cb_ref = f32[2,1,3328]{2,1,0:T(1,128)} reshape(f32[2,3328]{1,0:T(2,128)} %param.14) | data formatting | bytes 53248 | tf_op jit(solution)/shard_map/reshape | solution.py:403
  3.3 110.7 %shard_map.121 = (f32[4,64,1536]{2,1,0:T(8,128)}, f32[4,2,12,64,128]{4,3,2,1,0:T(8,128)}, bf16[2,4,16,3328]{3,2,1,0:T(8,128)(2,1)}) custom-call(f32[4,64,1536]{2,1,0:T(8,128)} %resid_ref.1, f32[2,1,1536]{2,1,0:T(1,128)} %reshape.18.pre_ref, bf16[2,6448,1536]{2,1,0:T(8,128)(2,1)} %bitcast.10, f32[2,4,3328]{2,1,0:T(4,128)} %bitcast.11, ...), custom_call_target="tpu_custom_call" | custom-call | tf_op jit(solution)/shard_map/pallas_call | solution.py:359
  114.1 0.0 copy-start
  114.1 1.3 %slice_bitcast_fusion = bf16[4,2,3328,3]{2,3,0,1:T(4,128)(2,1)S(1)} fusion(bf16[2,4,16,3328]{3,2,1,0:T(8,128)(2,1)} %get-tuple-element.8), kind=kLoop, calls=%fused_computation | loop fusion | bytes 319488 | tf_op jit(solution)/shard_map/transpose | solution.py:405
  115.4 0.8 copy.15
  116.2 2.7 %copy.18 = f32[4,64,1536]{2,1,0:T(8,128)} copy(f32[4,64,1536]{2,1,0:T(8,128)} %get-tuple-element.15) | data formatting | bytes 3145728
  118.8 0.0 copy-done
  118.8 1.7 %copy.19 = f32[4,2,12,64,128]{4,3,2,1,0:T(8,128)} copy(f32[4,2,12,64,128]{4,3,2,1,0:T(8,128)S(1)} %copy-done) | data formatting | bytes 6291456
Async XLA Ops:
  114.1 4.7 %copy-start = (f32[4,2,12,64,128]{4,3,2,1,0:T(8,128)S(1)}, f32[4,2,12,64,128]{4,3,2,1,0:T(8,128)}, u32[]{:S(2)}) copy-start(f32[4,2,12,64,128]{4,3,2,1,0:T(8,128)} %get-tuple-element.16) | copy-start | bytes 9437188

commit v2 on v1

--- a/solution.py
+++ b/solution.py
@@ -61,15 +61,18 @@
     core_f = core.astype(F32)
 
     def weight_copies(l):
-        zc = [pltpu.make_async_copy(w_in_ref.at[l, pl.ds(HALF * j, HALF), :], wz.at[pl.ds(HALF * j, HALF), :], wsem.at[j]) for j in range(4)]
-        xc = [pltpu.make_async_copy(w_in_ref.at[l, pl.ds(pl.multiple_of(D_INNER + LOC * b + HALF * core, 16), HALF), :], wx.at[pl.ds(HALF * b, HALF), :], wsem.at[4 + b]) for b in range(2)]
-        bc = pltpu.make_async_copy(w_in_ref.at[l, pl.ds(2 * D_INNER, 304), :], wbc.at[pl.ds(0, 304), :], wsem.at[6])
-        oc = pltpu.make_async_copy(w_out_ref.at[l], wout, wsem.at[7])
-        return zc, xc, bc, oc
-
-    zc0, xc0, bc0, oc0 = weight_copies(0)
-    for c in zc0 + xc0 + [bc0, oc0]:
-        c.start()
+        xc = [pltpu.make_async_copy(w_in_ref.at[l, pl.ds(pl.multiple_of(D_INNER + LOC * b + HALF * core, 16), HALF), :], wx.at[pl.ds(HALF * b, HALF), :], wsem.at[6 + b]) for b in range(2)]
+        bc = pltpu.make_async_copy(w_in_ref.at[l, pl.ds(2 * D_INNER, 304), :], wbc.at[pl.ds(0, 304), :], wsem.at[8])
+        oc = pltpu.make_async_copy(w_out_ref.at[l], wout, wsem.at[9])
+        return xc, bc, oc
+
+    def z_copy(l, n):
+        rows = pl.ds(pl.multiple_of(512 * n, 16), 512)
+        return pltpu.make_async_copy(w_in_ref.at[l, rows, :], wz.at[rows, :], wsem.at[n])
+
+    xc0, bc0, oc0 = weight_copies(0)
+    for n in range(6):
+        z_copy(0, n).start()
 
     barrier = pltpu.get_barrier_semaphore()
     for step in range(1, 4):
@@ -79,7 +82,10 @@
     wbc[304:384, :] = jnp.zeros((80, D_MODEL), BF16)
     prm[...] = jnp.zeros((8, 128), F32)
     r_out[...] = resid_ref[...]
-    pl.semaphore_wait(barrier, 3)
+    for c in [bc0] + xc0:
+        c.start()
+    with jax.named_scope('barrier'):
+        pl.semaphore_wait(barrier, 3)
 
     own_row = pl.multiple_of(HALO + BLK * chip + SEG * core, 16)
     oth_row = pl.multiple_of(HALO + BLK * (1 - chip) + SEG * core, 16)
@@ -100,9 +106,10 @@
         def norm_body(p, c):
             v = r_out[p]
             ms = jnp.mean(v * v, axis=-1, keepdims=True)
-            hbuf[lb + p, pl.ds(own_row, SEG), :] = (v * lax.rsqrt(ms + EPSILON) * pre_ref[l]).astype(BF16)
-            return c
-        lax.fori_loop(0, NB, norm_body, 0)
+            hbuf[lb + p, pl.ds(own_row, SEG), :] = (v * lax.rsqrt(ms + EPSILON) * pre_ref[pl.ds(l, 1), :]).astype(BF16)
+            return c
+        with jax.named_scope('norm'):
+            lax.fori_loop(0, NB, norm_body, 0)
 
         def hslice(p0, n, row, size):
             return hbuf.at[pl.ds(lb + p0, n), pl.ds(row, size), :]
@@ -123,32 +130,32 @@
         c_r0.start()
         c_r1.start()
 
-        zc, xc, bc, oc = weight_copies(l)
-        znx, xnx, bnx, onx = weight_copies(1)
+        xc, bc, oc = weight_copies(l)
+        xnx, bnx, onx = weight_copies(1)
 
         for b in range(2):
             src = pl.multiple_of(LOC * b + HALF * core, 128)
             cwl[0:4, HALF * b:HALF * (b + 1)] = cw_ref[l, :, pl.ds(src, HALF)]
-            cwl[4:5, HALF * b:HALF * (b + 1)] = cb_ref[l, :, pl.ds(src, HALF)]
+            cwl[4:5, HALF * b:HALF * (b + 1)] = cb_ref[pl.ds(l, 1), pl.ds(src, HALF)]
         cwl[0:4, LOC:ACT] = cw_ref[l, :, D_INNER:CONV_DIM]
-        cwl[4:5, LOC:ACT] = cb_ref[l, :, D_INNER:CONV_DIM]
-        prm[0:1, 0:HEADS] = dtb_ref[l]
-        prm[1:2, 0:HEADS] = -jnp.exp(alog_ref[l])
-
-        for c in zc:
-            c.wait()
+        cwl[4:5, LOC:ACT] = cb_ref[pl.ds(l, 1), D_INNER:CONV_DIM]
+        prm[0:1, 0:HEADS] = dtb_ref[pl.ds(l, 1), :]
+        prm[1:2, 0:HEADS] = -jnp.exp(alog_ref[pl.ds(l, 1), :])
 
         def z_body(n, c):
+            z_copy(l, n).wait()
             lhs = hbuf[pl.ds(lb, NB), pl.ds(own_row, SEG), :].reshape(NB * SEG, D_MODEL)
             z = round_bf16(dot_nt(lhs, wz[pl.ds(pl.multiple_of(512 * n, 512), 512), :]))
             sz[:, :, pl.ds(pl.multiple_of(512 * n, 512), 512)] = silu(z).reshape(NB, SEG, 512)
             return c
-        lax.fori_loop(0, 6, z_body, 0)
+        with jax.named_scope('zproj'):
+            lax.fori_loop(0, 6, z_body, 0)
 
         @pl.when(l == 0)
         def _():
-            for c in znx:
-                c.start()
+            oc.start()
+            for n in range(6):
+                z_copy(1, n).start()
 
         def conv_chunk(act, i, p, src_col, dst_col, width):
             for s in range(width // 128):
@@ -194,16 +201,21 @@
                 return c
             lax.fori_loop(0, 3, x_body, 0)
 
-        c_par.wait_recv()
-        c_tail.wait_recv()
-        f_tail.start()
-        bc.wait()
-        for c in xc:
-            c.wait()
-        f_tail.wait_recv()
-        block(0, NB, own_blk, act_o, tail_o, cumt_o, dtt_o, cum_o)
-        c_r0.wait_recv()
-        f_r0.start()
+        with jax.named_scope('wait_h'):
+            c_par.wait_recv()
+            c_tail.wait_recv()
+            f_tail.start()
+        with jax.named_scope('wait_wx'):
+            bc.wait()
+            for c in xc:
+                c.wait()
+        with jax.named_scope('wait_tail'):
+            f_tail.wait_recv()
+        with jax.named_scope('own_block'):
+            block(0, NB, own_blk, act_o, tail_o, cumt_o, dtt_o, cum_o)
+        with jax.named_scope('wait_r0'):
+            c_r0.wait_recv()
+            f_r0.start()
 
         def intra_body(p, c):
             cb = act_o[p, :, LOC + 128:ACT]
@@ -220,7 +232,8 @@
                 dv = jnp.where(low[0:1], dskip_ref[l, blk], dskip_ref[l, blk + 1])
                 yloc[p, :, 128 * j:128 * (j + 1)] = dot(jnp.concatenate(mats, axis=1), rhs) + dv * xp
             return c
-        lax.fori_loop(0, NB, intra_body, 0)
+        with jax.named_scope('intra'):
+            lax.fori_loop(0, NB, intra_body, 0)
 
         def y_copy(p):
             src = ybuf.at[p, pl.ds(pl.multiple_of(SEG * (1 - core), 16), SEG), :]
@@ -272,14 +285,20 @@
             out_copy(p, l).start()
             return c
 
-        c_r1.wait_recv()
-        f_r1.start()
-        f_r0.wait_recv()
-        block(0, 2, oth_blk, act_r, tail_r, cumt_r, dtt_r, None)
-        lax.fori_loop(0, 2, inter_body, 0)
-        f_r1.wait_recv()
-        block(2, 2, oth_blk, act_r, tail_r, cumt_r, dtt_r, None)
-        lax.fori_loop(2, NB, inter_body, 0)
+        with jax.named_scope('wait_f0'):
+            f_r0.wait_recv()
+        with jax.named_scope('oth_block0'):
+            block(0, 2, oth_blk, act_r, tail_r, cumt_r, dtt_r, None)
+        with jax.named_scope('inter0'):
+            lax.fori_loop(0, 2, inter_body, 0)
+        with jax.named_scope('wait_r1'):
+            c_r1.wait_recv()
+            f_r1.start()
+            f_r1.wait_recv()
+        with jax.named_scope('oth_block1'):
+            block(2, 2, oth_blk, act_r, tail_r, cumt_r, dtt_r, None)
+        with jax.named_scope('inter1'):
+            lax.fori_loop(2, NB, inter_body, 0)
 
         @pl.when(l == 0)
         def _():
@@ -323,25 +342,29 @@
                 cols = slice(HALF * b, HALF * (b + 1))
                 gn[p, :, cols] = (sz[p, :, cols] * scale * gw_ref[l, :, cols]).astype(BF16)
             return c
-        lax.fori_loop(0, NB, gate_body, 0)
-
-        oc.wait()
+        with jax.named_scope('gate'):
+            lax.fori_loop(0, NB, gate_body, 0)
+
+        with jax.named_scope('wait_wout'):
+            oc.wait()
 
         def out_body(n, c):
             cols = pl.ds(pl.multiple_of(512 * n, 512), 512)
             o = dot(gn[...].reshape(NB * SEG, D_INNER), wout[:, cols])
             r_out[:, :, cols] = r_out[:, :, cols] + o.reshape(NB, SEG, 512)
             return c
-        lax.fori_loop(0, 3, out_body, 0)
+        with jax.named_scope('outproj'):
+            lax.fori_loop(0, 3, out_body, 0)
 
         @pl.when(l == 0)
         def _():
             onx.start()
 
-        for c in [c_par, c_tail, c_r0, c_r1, f_tail, f_r0, f_r1]:
-            c.wait_send()
-        for c in t_copies:
-            c.wait()
+        with jax.named_scope('wait_end'):
+            for c in [c_par, c_tail, c_r0, c_r1, f_tail, f_r0, f_r1]:
+                c.wait_send()
+            for c in t_copies:
+                c.wait()
         return carry
 
     lax.fori_loop(0, LAYERS, layer, 0)
@@ -390,7 +413,7 @@
                 pltpu.VMEM((NB, 40, BLK), F32),
                 pltpu.VMEM((8, ACT), F32),
                 pltpu.VMEM((8, 128), F32),
-                pltpu.SemaphoreType.DMA((8,)),
+                pltpu.SemaphoreType.DMA((10,)),
                 pltpu.SemaphoreType.DMA((LAYERS, 7)),
                 pltpu.SemaphoreType.DMA((LAYERS, 7)),
                 pltpu.SemaphoreType.DMA((LAYERS, NB)),
@@ -400,8 +423,7 @@
                 pltpu.SemaphoreType.DMA((NB,)),
             ],
             compiler_params=pltpu.CompilerParams(collective_id=0, has_side_effects=True, vmem_limit_bytes=67043328),
-        )(resid, pre_norm.reshape(LAYERS, 1, D_MODEL), jnp.swapaxes(w_in, 1, 2), jnp.swapaxes(conv_w, 1, 2), conv_b.reshape(LAYERS, 1, CONV_DIM),
-          dt_bias.reshape(LAYERS, 1, HEADS), a_log.reshape(LAYERS, 1, HEADS), d_skip, gate_norm, w_out)
+        )(resid, pre_norm, jnp.swapaxes(w_in, 1, 2), jnp.swapaxes(conv_w, 1, 2), conv_b, dt_bias, a_log, d_skip, gate_norm, w_out)
         conv_state = jnp.transpose(tails[:, :, 13:16, :], (1, 0, 3, 2))
         return r, ssm, conv_state
 

time: 121 us -> 121 us (level)
  Pallas kernels: 111 us -> 114 us
  local copies, waits for them, and re-layouts: 9.08 us -> 6.4 us
    pallas_call x1, Pallas kernels: 111 us -> 114 us  [forward(): pl.pallas_call(kernel, out_shape=(jax.ShapeDtypeStruct((NB, SEG, D_MODEL)...]
    reshape x2 -> x0, local copies, waits for them, and re-layouts: 2.68 us -> none  [the longest x1 1.37 us: forward(): conv_b.reshape(LAYERS, 1, CONV_DIM)]
where the time goes in v2:
time: 121 us
  Pallas kernels  114 us (94%)
  local copies, waits for them, and re-layouts  6.4 us (5%)
    pallas_call x1, Pallas kernels, forward(): pl.pallas_call(kernel, out_shape=(jax.ShapeDtypeStruct((NB, SEG, D_MODEL)...  114 us
    unnamed x5, local copies, waits for them, and re-layouts  5.13 us

profile of v2, /device:TPU:0, one launch (start us, length us, event | category | flops | bytes accessed | tf_op | source)
XLA Modules:
  0.0 121.1 jit_solution(4135601657378503251)
XLA Ops:
  0.6 114.1 %shard_map.121 = (f32[4,64,1536]{2,1,0:T(8,128)}, f32[4,2,12,64,128]{4,3,2,1,0:T(8,128)}, bf16[2,4,16,3328]{3,2,1,0:T(8,128)(2,1)}) custom-call(f32[4,64,1536]{2,1,0:T(8,128)} %resid_ref.1, f32[2,1536]{1,0:T(2,128)} %pre_ref.1, bf16[2,6448,1536]{2,1,0:T(8,128)(2,1)} %bitcast.4, f32[2,4,3328]{2,1,0:T(4,128)} %bitcast.5, f32[2,3328]{1,0:T(2,128)} %cb_ref.1, ...), custom_call_target="tpu_custom_call" | custom-call | tf_op jit(solution)/shard_map/pallas_call | solution.py:382
  114.7 0.0 copy-start
  114.7 1.3 %slice_bitcast_fusion = bf16[4,2,3328,3]{2,3,0,1:T(4,128)(2,1)S(1)} fusion(bf16[2,4,16,3328]{3,2,1,0:T(8,128)(2,1)} %get-tuple-element.8), kind=kLoop, calls=%fused_computation | loop fusion | bytes 319488 | tf_op jit(solution)/shard_map/transpose | solution.py:427
  116.0 0.8 copy.13
  116.8 2.7 %copy.16 = f32[4,64,1536]{2,1,0:T(8,128)} copy(f32[4,64,1536]{2,1,0:T(8,128)} %get-tuple-element.15) | data formatting | bytes 3145728
  119.4 0.0 copy-done
  119.4 1.7 %copy.17 = f32[4,2,12,64,128]{4,3,2,1,0:T(8,128)} copy(f32[4,2,12,64,128]{4,3,2,1,0:T(8,128)S(1)} %copy-done) | data formatting | bytes 6291456
Async XLA Ops:
  114.7 4.7 %copy-start = (f32[4,2,12,64,128]{4,3,2,1,0:T(8,128)S(1)}, f32[4,2,12,64,128]{4,3,2,1,0:T(8,128)}, u32[]{:S(2)}) copy-start(f32[4,2,12,64,128]{4,3,2,1,0:T(8,128)} %get-tuple-element.16) | copy-start | bytes 9437188

commit v3 on v2

v3 whole, which is shorter than its diff:
```python
import jax
import jax.numpy as jnp
from jax import lax
from jax.experimental import pallas as pl
from jax.experimental.pallas import tpu as pltpu
from jax.sharding import PartitionSpec as P

F32 = jnp.float32
BF16 = jnp.bfloat16
EPSILON = 1e-5
LAYERS = 2
NB = 4
SEG = 64
BLK = 128
HALO = 16
EXT = BLK + HALO
ROWS = HALO + 2 * BLK
D_MODEL = 1536
D_INNER = 3072
CONV_DIM = 3328
HEADS = 48
HALF = 768
LOC = 1536
ACT = LOC + 256
PAIRS = 12
NT = (((1,), (1,)), ((), ()))


def dot(a, b):
    return jnp.dot(a, b, preferred_element_type=F32)


def dot_nt(a, b):
    return lax.dot_general(a, b, NT, preferred_element_type=F32)


def round_bf16(v):
    return v.astype(BF16).astype(F32)


def silu(v):
    half = 0.5 * v
    return half * jnp.tanh(half) + half


def head_row(i):
    return i if i < 12 else i + 12


def kernel(resid_ref, pre_ref, w_in_ref, cw_ref, cb_ref, dtb_ref, alog_ref, dskip_ref, gw_ref, w_out_ref,
           r_out, ssm_out, tail_out,
           hbuf, sz, wz, wx, wbc, wout, rawa, rawb, states, act_o, act_r, yloc, ybuf, yrecv, gn, stg, tails, tail_o, tail_r,
           cum_o, cumt_o, cumt_r, dtt_o, dtt_r, cwl, prm,
           wsem, hsend, hrecv, ysend, yrecv_sem, tsend, trecv, osem):
    me = lax.axis_index('sp')
    chip = me // 2
    core = me % 2
    partner = chip * 2 + (1 - core)
    other = (1 - chip) * 2 + core
    chip_f = chip.astype(F32)
    core_f = core.astype(F32)

    def weight_copies(l):
        xc = [pltpu.make_async_copy(w_in_ref.at[l, pl.ds(pl.multiple_of(D_INNER + LOC * b + HALF * core, 16), HALF), :], wx.at[pl.ds(HALF * b, HALF), :], wsem.at[6 + b]) for b in range(2)]
        bc = pltpu.make_async_copy(w_in_ref.at[l, pl.ds(2 * D_INNER, 304), :], wbc.at[pl.ds(0, 304), :], wsem.at[8])
        oc = pltpu.make_async_copy(w_out_ref.at[l], wout, wsem.at[9])
        return xc, bc, oc

    def z_copy(l, n):
        rows = pl.ds(pl.multiple_of(512 * n, 16), 512)
        return pltpu.make_async_copy(w_in_ref.at[l, rows, :], wz.at[rows, :], wsem.at[n])

    xc0, bc0, oc0 = weight_copies(0)
    for n in range(6):
        z_copy(0, n).start()

    barrier = pltpu.get_barrier_semaphore()
    for step in range(1, 4):
        pl.semaphore_signal(barrier, inc=1, device_id={'sp': (me + step) % 4}, device_id_type=pl.DeviceIdType.MESH)

    hbuf[:, 0:HALO, :] = jnp.zeros((LAYERS * NB, HALO, D_MODEL), BF16)
    wbc[304:384, :] = jnp.zeros((80, D_MODEL), BF16)
    prm[...] = jnp.zeros((8, 128), F32)
    r_out[...] = resid_ref[...]
    for c in [bc0] + xc0:
        c.start()
    with jax.named_scope('barrier'):
        pl.semaphore_wait(barrier, 3)

    own_row = pl.multiple_of(HALO + BLK * chip + SEG * core, 16)
    oth_row = pl.multiple_of(HALO + BLK * (1 - chip) + SEG * core, 16)
    own_blk = pl.multiple_of(BLK * chip, 16)
    oth_blk = pl.multiple_of(BLK * (1 - chip), 16)

    iota_r = lax.broadcasted_iota(jnp.int32, (BLK, BLK), 0)
    iota_c = lax.broadcasted_iota(jnp.int32, (BLK, BLK), 1)

    def remote(src, dst, ssem, rsem, dev):
        return pltpu.make_async_remote_copy(src_ref=src, dst_ref=dst, send_sem=ssem, recv_sem=rsem, device_id={'sp': dev}, device_id_type=pl.DeviceIdType.MESH)

    tri = (iota_r >= iota_c).astype(F32)
    low = iota_c < 64

    def hslice(l, p0, n, row, size):
        return hbuf.at[pl.ds(NB * l + p0, n), pl.ds(row, size), :]

    def same(l, idx, p0, n, row, size, dev):
        ref = hslice(l, p0, n, row, size)
        return remote(ref, ref, hsend.at[l, idx], hrecv.at[l, idx], dev)

    def c_par(l):
        return same(l, 0, 0, NB, own_row, SEG, partner)

    def c_tail(l):
        return same(l, 1, 0, NB, own_row + 48, 16, other)

    def c_half(l, half):
        return same(l, 2 + half, 2 * half, 2, own_row, 48, other)

    def f_tail(l):
        return same(l, 4, 0, NB, oth_row + 48, 16, partner)

    def f_half(l, half):
        return same(l, 5 + half, 2 * half, 2, oth_row, 48, partner)

    def y_copy(l, p):
        src = ybuf.at[p, pl.ds(pl.multiple_of(SEG * (1 - core), 16), SEG), :]
        return remote(src, yrecv.at[NB * l + p], ysend.at[l, p], yrecv_sem.at[l, p], partner)

    def out_copy(l, p):
        return pltpu.make_async_copy(stg.at[p], ssm_out.at[p, l], osem.at[p])

    def tail_copies(l):
        res = []
        for b in range(2):
            ref = tails.at[l, :, :, pl.ds(pl.multiple_of(LOC * b + HALF * core, 128), HALF)]
            res.append(remote(ref, ref, tsend.at[l, b], trecv.at[l, b], partner))
        return res

    def conv_chunk(act, src, groups, i, p, dst):
        for g in range(groups):
            cols = slice(dst + 128 * g, dst + 128 * (g + 1))
            acc = cwl[0:1, cols] * src[g, i, 13:141, :]
            for k in range(1, 4):
                acc = acc + cwl[k:k + 1, cols] * src[g, i, 13 + k:141 + k, :]
            act[p, :, cols] = silu(acc + cwl[4:5, cols]).astype(BF16)

    def block(l, p0, np_, row, act, tail, cumt, dtt, cum):
        def project(w, rows, dst):
            lhs = hbuf[pl.ds(NB * l + p0, np_), pl.ds(row, EXT), :].reshape(np_ * EXT, D_MODEL)
            res = round_bf16(dot_nt(lhs, w[rows, :]))
            for g in range((rows.stop - rows.start) // 128):
                dst[g, 0:np_] = res[:, 128 * g:128 * (g + 1)].reshape(np_, EXT, 128)

        def finish_bc(src):
            for i in range(np_):
                p = p0 + i
                for g in range(2):
                    tail[p, :, LOC + 128 * g:LOC + 128 * (g + 1)] = src[g, i, BLK:EXT, :].astype(BF16)
                conv_chunk(act, src, 2, i, p, LOC)
                v = src[2, i, HALO:EXT, :] + prm[0:1, :]
                dt = round_bf16(jnp.maximum(v, 0.0) + jnp.log1p(jnp.exp(-jnp.abs(v))))
                logs = dt * prm[1:2, :]
                dt = dt * (1.0 - core_f) + pltpu.roll(dt, 116, 1) * core_f
                logs = logs * (1.0 - core_f) + pltpu.roll(logs, 116, 1) * core_f
                cums = jnp.dot(tri, logs, precision=lax.Precision.HIGHEST, preferred_element_type=F32)
                cumt[p] = cums.T[0:40]
                dtt[p] = dt.T[0:40]
                if cum is not None:
                    cum[p] = cums

        def finish_x(src, n):
            for i in range(np_):
                for g in range(4):
                    tail[p0 + i, :, 512 * n + 128 * g:512 * n + 128 * (g + 1)] = src[g, i, BLK:EXT, :].astype(BF16)
                conv_chunk(act, src, 4, i, p0 + i, 512 * n)

        project(wbc, slice(0, 384), rawa)
        project(wx, slice(0, 512), rawb)
        finish_bc(rawa)
        project(wx, slice(512, 1024), rawa)
        finish_x(rawb, 0)
        project(wx, slice(1024, 1536), rawb)
        finish_x(rawa, 1)
        finish_x(rawb, 2)

    zero = jnp.zeros((), BF16)

    def split_pair(xp):
        return [jnp.where(low, xp, zero), jnp.where(low, zero, xp)]

    def decays(p, h, cumt, dtt, extra):
        row = cumt[p, pl.ds(h, 1), :]
        return dtt[p, pl.ds(h, 1), :] * jnp.exp(row[:, 127:128] - row + extra)

    def intra_body(l, p):
        cb = act_o[p, :, LOC + 128:ACT]
        scores = dot_nt(cb, act_o[p, :, LOC:LOC + 128]) * tri
        for j in range(PAIRS):
            mats = []
            for i in (2 * j, 2 * j + 1):
                h = head_row(i)
                col = jnp.broadcast_to(cum_o[p, :, h:h + 1], (BLK, BLK))
                mats.append((jnp.exp(jnp.minimum(col - cumt_o[p, h:h + 1, :], 0.0)) * (scores * dtt_o[p, h:h + 1, :])).astype(BF16))
            xp = act_o[p, :, 128 * j:128 * (j + 1)]
            blk = (0 if j < 6 else 24) + 12 * core + (2 * j) % 12
            dv = jnp.where(low[0:1], dskip_ref[l, blk], dskip_ref[l, blk + 1])
            y = dot(jnp.concatenate(mats, axis=1), jnp.concatenate(split_pair(xp), axis=0)) + dv * xp.astype(F32)
            yloc[p, :, 128 * j:128 * (j + 1)] = y
            ybuf[p, :, 128 * j:128 * (j + 1)] = y.astype(BF16)

        @pl.when(chip == 0)
        def _():
            y_copy(l, p).start()

    def inter_body(l, p):
        bt = act_r[p, :, LOC:LOC + 128].astype(F32).T
        cf = act_o[p, :, LOC + 128:ACT]
        for j in range(PAIRS):
            lhs = jnp.concatenate([(bt * decays(p, h, cumt_r, dtt_r, 0.0)).astype(BF16) for h in (head_row(2 * j), head_row(2 * j + 1))], axis=1)
            states[:, 128 * j:128 * (j + 1)] = dot(lhs, jnp.concatenate(split_pair(act_r[p, :, 128 * j:128 * (j + 1)]), axis=0))
        for jj in range(PAIRS // 2):
            o = dot(cf, states[:, 256 * jj:256 * (jj + 1)].astype(BF16))
            for s in range(2):
                j = 2 * jj + s
                ha, hb = head_row(2 * j), head_row(2 * j + 1)
                ca = jnp.broadcast_to(cum_o[p, :, ha:ha + 1], (BLK, BLK))
                cb = jnp.broadcast_to(cum_o[p, :, hb:hb + 1], (BLK, BLK))
                y = yloc[p, :, 128 * j:128 * (j + 1)] + o[:, 128 * s:128 * (s + 1)] * jnp.exp(jnp.where(low, ca, cb))
                ybuf[p, :, 128 * j:128 * (j + 1)] = y.astype(BF16)
        y_copy(l, p).start()

    def final_body(l, p):
        @pl.when(l > 0)
        def _():
            out_copy(0, p).wait()
        bto = act_o[p, :, LOC:LOC + 128].astype(F32).T
        btr = act_r[p, :, LOC:LOC + 128].astype(F32).T
        for q in range(6):
            h = 24 * chip + 2 * q
            cols = pl.ds(pl.multiple_of(128 * (6 * chip + q), 128), 128)
            left, right = [], []
            for hh in (h, h + 1):
                end_o = cumt_o[p, pl.ds(hh, 1), :][:, 127:128]
                end_r = cumt_r[p, pl.ds(hh, 1), :][:, 127:128]
                left.append((bto * decays(p, hh, cumt_o, dtt_o, end_r * (1.0 - chip_f))).astype(BF16))
                right.append((btr * decays(p, hh, cumt_r, dtt_r, end_o * chip_f)).astype(BF16))
            rhs = jnp.concatenate(split_pair(act_o[p, :, cols]) + split_pair(act_r[p, :, cols]), axis=0)
            state = dot(jnp.concatenate(left + right, axis=1), rhs)
            stg[p, 2 * q:2 * q + 2] = state.T.reshape(2, 64, 128)
        out_copy(l, p).start()

    def early_tail(l):
        @pl.when(core == 1)
        def _():
            c_tail(l).wait_recv()
            f_tail(l).start()

        @pl.when(core == 0)
        def _():
            f_tail(l).wait_recv()

    def late_tail(l):
        @pl.when(core == 0)
        def _():
            c_tail(l).wait_recv()
            f_tail(l).start()

        @pl.when(core == 1)
        def _():
            f_tail(l).wait_recv()

    def after_other(l, tail):
        for b in range(2):
            tails[l, :, :, pl.ds(pl.multiple_of(LOC * b + HALF * core, 128), HALF)] = tail[:, :, HALF * b:HALF * (b + 1)]
        tails[l, :, :, D_INNER:CONV_DIM] = tail[:, :, LOC:ACT]
        for c in tail_copies(l):
            c.start()

        @pl.when(l == 0)
        def _():
            xnx, bnx, _ = weight_copies(1)
            for c in xnx + [bnx]:
                c.start()

    def begin(l):
        def norm_body(p, c):
            v = r_out[p]
            ms = jnp.mean(v * v, axis=-1, keepdims=True)
            hbuf[NB * l + p, pl.ds(own_row, SEG), :] = (v * lax.rsqrt(ms + EPSILON) * pre_ref[pl.ds(l, 1), :]).astype(BF16)
            return c
        with jax.named_scope('norm'):
            lax.fori_loop(0, NB, norm_body, 0)

        c_par(l).start()

        @pl.when(core == 1)
        def _():
            c_tail(l).start()
        c_half(l, 0).start()

        @pl.when(core == 0)
        def _():
            c_tail(l).start()
        c_half(l, 1).start()

    def main(l):
        xc, bc, oc = weight_copies(l)

        for b in range(2):
            src = pl.multiple_of(LOC * b + HALF * core, 128)
            cwl[0:4, HALF * b:HALF * (b + 1)] = cw_ref[l, :, pl.ds(src, HALF)]
            cwl[4:5, HALF * b:HALF * (b + 1)] = cb_ref[pl.ds(l, 1), pl.ds(src, HALF)]
        cwl[0:4, LOC:ACT] = cw_ref[l, :, D_INNER:CONV_DIM]
        cwl[4:5, LOC:ACT] = cb_ref[pl.ds(l, 1), D_INNER:CONV_DIM]
        prm[0:1, 0:HEADS] = dtb_ref[pl.ds(l, 1), :]
        prm[1:2, 0:HEADS] = -jnp.exp(alog_ref[pl.ds(l, 1), :])

        def z_body(n, c):
            z_copy(l, n).wait()
            lhs = hbuf[pl.ds(NB * l, NB), pl.ds(own_row, SEG), :].reshape(NB * SEG, D_MODEL)
            z = round_bf16(dot_nt(lhs, wz[pl.ds(pl.multiple_of(512 * n, 512), 512), :]))
            sz[:, :, pl.ds(pl.multiple_of(512 * n, 512), 512)] = silu(z).reshape(NB, SEG, 512)
            return c
        with jax.named_scope('zproj'):
            lax.fori_loop(0, 6, z_body, 0)
        oc.start()

        @pl.when(l == 0)
        def _():
            for n in range(6):
                z_copy(1, n).start()

        with jax.named_scope('wait_h'):
            c_par(l).wait_recv()
            bc.wait()
            for c in xc:
                c.wait()

            @pl.when(chip == 1)
            def _():
                early_tail(l)
        with jax.named_scope('own_block'):
            block(l, 0, NB, own_blk, act_o, tail_o, cumt_o, dtt_o, cum_o)
        with jax.named_scope('intra'):
            lax.fori_loop(0, NB, lambda p, c: (intra_body(l, p), c)[1], 0)

        @pl.when(chip == 1)
        def _():
            with jax.named_scope('wait_r0'):
                c_half(l, 0).wait_recv()
                f_half(l, 0).start()
                late_tail(l)
                f_half(l, 0).wait_recv()

            def half_body(half, c):
                with jax.named_scope('oth_block'):
                    block(l, 2 * half, 2, oth_blk, act_r, tail_r, cumt_r, dtt_r, None)

                @pl.when(half == 0)
                def _():
                    with jax.named_scope('wait_c1'):
                        c_half(l, 1).wait_recv()
                        f_half(l, 1).start()
                with jax.named_scope('inter'):
                    lax.fori_loop(2 * half, 2 * half + 2, lambda p, c: (inter_body(l, p), c)[1], 0)

                @pl.when(half == 0)
                def _():
                    with jax.named_scope('wait_f1'):
                        f_half(l, 1).wait_recv()
                return c
            lax.fori_loop(0, 2, half_body, 0)
            with jax.named_scope('final'):
                lax.fori_loop(0, NB, lambda p, c: (final_body(l, p), c)[1], 0)
            after_other(l, tail_o)

        def gate_body(p, c):
            y_copy(l, p).wait()
            total = jnp.zeros((SEG, 1), F32)
            for b in range(2):
                for own in range(2):
                    cols = pl.ds(pl.multiple_of(LOC * b + HALF * (core if own else 1 - core), 128), HALF)
                    if own:
                        y = ybuf[p, pl.ds(pl.multiple_of(SEG * core, 16), SEG), HALF * b:HALF * (b + 1)]
                    else:
                        y = yrecv[NB * l + p, :, HALF * b:HALF * (b + 1)]
                    g = y.astype(F32) * sz[p, :, cols]
                    sz[p, :, cols] = g
                    total = total + jnp.sum(g * g, axis=-1, keepdims=True)
            scale = lax.rsqrt(total * (1.0 / D_INNER) + EPSILON)
            for b in range(4):
                cols = slice(HALF * b, HALF * (b + 1))
                gn[p, :, cols] = (sz[p, :, cols] * scale * gw_ref[l, :, cols]).astype(BF16)
            return c
        with jax.named_scope('gate'):
            lax.fori_loop(0, NB, gate_body, 0)
            oc.wait()

        def out_body(n, c):
            cols = pl.ds(pl.multiple_of(512 * n, 512), 512)
            o = dot(gn[...].reshape(NB * SEG, D_INNER), wout[:, cols])
            r_out[:, :, cols] = r_out[:, :, cols] + o.reshape(NB, SEG, 512)
            return c
        with jax.named_scope('outproj'):
            lax.fori_loop(0, 3, out_body, 0)

    def deferred(l):
        with jax.named_scope('wait_d'):
            early_tail(l)
            late_tail(l)

        def half_body(half, c):
            with jax.named_scope('wait_dh'):
                c_half(l, half).wait_recv()
                f_half(l, half).start()
                f_half(l, half).wait_recv()
            with jax.named_scope('oth_block'):
                block(l, 2 * half, 2, oth_blk, act_r, tail_r, cumt_r, dtt_r, None)
            with jax.named_scope('final'):
                lax.fori_loop(2 * half, 2 * half + 2, lambda p, c: (final_body(l, p), c)[1], 0)
            return c
        lax.fori_loop(0, 2, half_body, 0)
        after_other(l, tail_r)

    def step(l, carry):
        @pl.when(l < LAYERS)
        def _():
            begin(l)

        @pl.when(jnp.logical_and(chip == 0, l > 0))
        def _():
            deferred(l - 1)

        @pl.when(l < LAYERS)
        def _():
            main(l)
        return carry

    lax.fori_loop(0, LAYERS + 1, step, 0)
    for l in range(LAYERS):
        for c in [c_par(l), c_tail(l), c_half(l, 0), c_half(l, 1), f_tail(l), f_half(l, 0), f_half(l, 1)]:
            c.wait_send()
        for c in tail_copies(l):
            c.wait()
    for p in range(NB):
        pltpu.make_async_copy(stg.at[p], ssm_out.at[p, LAYERS - 1], osem.at[p]).wait()
    tail_out[...] = tails[...]


def solution(mesh):
    vmem = pl.BlockSpec(memory_space=pltpu.VMEM)
    hbm = pl.BlockSpec(memory_space=pl.ANY)
    smem = pl.BlockSpec(memory_space=pltpu.SMEM)

    def forward(resid, pre_norm, w_in, conv_w, conv_b, dt_bias, a_log, d_skip, gate_norm, w_out):
        r, ssm, tails = pl.pallas_call(
            kernel,
            out_shape=(
                jax.ShapeDtypeStruct((NB, SEG, D_MODEL), F32),
                jax.ShapeDtypeStruct((NB, LAYERS, 12, 64, 128), F32),
                jax.ShapeDtypeStruct((LAYERS, NB, 16, CONV_DIM), BF16),
            ),
            in_specs=[vmem, vmem, hbm, vmem, vmem, vmem, vmem, smem, vmem, hbm],
            out_specs=(vmem, hbm, vmem),
            scratch_shapes=[
                pltpu.VMEM((LAYERS * NB, ROWS, D_MODEL), BF16),
                pltpu.VMEM((NB, SEG, D_INNER), F32),
                pltpu.VMEM((D_INNER, D_MODEL), BF16),
                pltpu.VMEM((LOC, D_MODEL), BF16),
                pltpu.VMEM((384, D_MODEL), BF16),
                pltpu.VMEM((D_INNER, D_MODEL), BF16),
                pltpu.VMEM((4, NB, EXT, 128), F32),
                pltpu.VMEM((4, NB, EXT, 128), F32),
                pltpu.VMEM((BLK, LOC), F32),
                pltpu.VMEM((NB, BLK, ACT), BF16),
                pltpu.VMEM((NB, BLK, ACT), BF16),
                pltpu.VMEM((NB, BLK, LOC), F32),
                pltpu.VMEM((NB, BLK, LOC), BF16),
                pltpu.VMEM((LAYERS * NB, SEG, LOC), BF16),
                pltpu.VMEM((NB, SEG, D_INNER), BF16),
                pltpu.VMEM((NB, 12, 64, 128), F32),
                pltpu.VMEM((LAYERS, NB, 16, CONV_DIM), BF16),
                pltpu.VMEM((NB, 16, ACT), BF16),
                pltpu.VMEM((NB, 16, ACT), BF16),
                pltpu.VMEM((NB, BLK, BLK), F32),
                pltpu.VMEM((NB, 40, BLK), F32),
                pltpu.VMEM((NB, 40, BLK), F32),
                pltpu.VMEM((NB, 40, BLK), F32),
                pltpu.VMEM((NB, 40, BLK), F32),
                pltpu.VMEM((8, ACT), F32),
                pltpu.VMEM((8, 128), F32),
                pltpu.SemaphoreType.DMA((10,)),
                pltpu.SemaphoreType.DMA((LAYERS, 7)),
                pltpu.SemaphoreType.DMA((LAYERS, 7)),
                pltpu.SemaphoreType.DMA((LAYERS, NB)),
                pltpu.SemaphoreType.DMA((LAYERS, NB)),
                pltpu.SemaphoreType.DMA((LAYERS, 2)),
                pltpu.SemaphoreType.DMA((LAYERS, 2)),
                pltpu.SemaphoreType.DMA((NB,)),
            ],
            compiler_params=pltpu.CompilerParams(collective_id=0, has_side_effects=True, vmem_limit_bytes=67043328),
        )(resid, pre_norm, jnp.swapaxes(w_in, 1, 2), jnp.swapaxes(conv_w, 1, 2), conv_b, dt_bias, a_log, d_skip, gate_norm, w_out)
        conv_state = jnp.transpose(tails[:, :, 13:16, :], (1, 0, 3, 2))
        return r, ssm, conv_state

    return jax.shard_map(forward, mesh=mesh, in_specs=(P('dp', 'sp', None), P(), P(), P(), P(), P(), P(), P(), P(), P()), out_specs=(P('dp', 'sp', None), P('dp', None, 'sp', None, None), P('dp', None, None, None)), check_vma=False)
```

time: 121 us -> 77.8 us (0.64)
  Pallas kernels: 114 us -> 70.6 us
    pallas_call x1, Pallas kernels: 114 us -> 70.6 us  [forward(): pl.pallas_call(kernel, out_shape=(jax.ShapeDtypeStruct((NB, SEG, D_MODEL)...]
where the time goes in v3:
time: 77.8 us; the launch traced here: 77.6 us
  Pallas kernels  70.6 us (91%)
  local copies, waits for them, and re-layouts  6.4 us (8%)
    pallas_call x1, Pallas kernels, forward(): pl.pallas_call(kernel, out_shape=(jax.ShapeDtypeStruct((NB, SEG, D_MODEL)...  70.6 us
    unnamed x5, local copies, waits for them, and re-layouts  5.13 us

profile of v3, /device:TPU:0, one launch (start us, length us, event | category | flops | bytes accessed | tf_op | source)
XLA Modules:
  0.0 77.6 jit_solution(5871393500834760545)
XLA Ops:
  0.6 70.6 %shard_map.121 = (f32[4,64,1536]{2,1,0:T(8,128)}, f32[4,2,12,64,128]{4,3,2,1,0:T(8,128)}, bf16[2,4,16,3328]{3,2,1,0:T(8,128)(2,1)}) custom-call(f32[4,64,1536]{2,1,0:T(8,128)} %resid_ref.1, f32[2,1536]{1,0:T(2,128)} %pre_ref.1, bf16[2,6448,1536]{2,1,0:T(8,128)(2,1)} %bitcast.4, f32[2,4,3328]{2,1,0:T(4,128)} %bitcast.5, f32[2,3328]{1,0:T(2,128)} %cb_ref.1, ...), custom_call_target="tpu_custom_call" | custom-call | tf_op jit(solution)/shard_map/pallas_call | solution.py:457
  71.2 0.0 copy-start
  71.2 1.3 %slice_bitcast_fusion = bf16[4,2,3328,3]{2,3,0,1:T(4,128)(2,1)S(1)} fusion(bf16[2,4,16,3328]{3,2,1,0:T(8,128)(2,1)} %get-tuple-element.8), kind=kLoop, calls=%fused_computation | loop fusion | bytes 319488 | tf_op jit(solution)/shard_map/transpose | solution.py:504
  72.5 0.8 %copy.13 = bf16[4,2,3328,3]{2,1,3,0:T(2,128)(2,1)} copy(bf16[4,2,3328,3]{2,3,0,1:T(4,128)(2,1)S(1)} %slice_bitcast_fusion) | data formatting | bytes 319488
  73.3 2.7 %copy.16 = f32[4,64,1536]{2,1,0:T(8,128)} copy(f32[4,64,1536]{2,1,0:T(8,128)} %get-tuple-element.15) | data formatting | bytes 3145728
  75.9 0.0 copy-done
  75.9 1.7 %copy.17 = f32[4,2,12,64,128]{4,3,2,1,0:T(8,128)} copy(f32[4,2,12,64,128]{4,3,2,1,0:T(8,128)S(1)} %copy-done) | data formatting | bytes 6291456
Async XLA Ops:
  71.2 4.7 %copy-start = (f32[4,2,12,64,128]{4,3,2,1,0:T(8,128)S(1)}, f32[4,2,12,64,128]{4,3,2,1,0:T(8,128)}, u32[]{:S(2)}) copy-start(f32[4,2,12,64,128]{4,3,2,1,0:T(8,128)} %get-tuple-element.16) | copy-start | bytes 9437188

commit v4 on v3

--- a/solution.py
+++ b/solution.py
@@ -49,7 +49,7 @@
 
 def kernel(resid_ref, pre_ref, w_in_ref, cw_ref, cb_ref, dtb_ref, alog_ref, dskip_ref, gw_ref, w_out_ref,
            r_out, ssm_out, tail_out,
-           hbuf, sz, wz, wx, wbc, wout, rawa, rawb, states, act_o, act_r, yloc, ybuf, yrecv, gn, stg, tails, tail_o, tail_r,
+           hbuf, sz, wz, wx, wbc, wout, rawa, rawb, states, bt_o, bt_r, act_o, act_r, yloc, ybuf, yrecv, gn, stg, tails, tail_o, tail_r,
            cum_o, cumt_o, cumt_r, dtt_o, dtt_r, cwl, prm,
            wsem, hsend, hrecv, ysend, yrecv_sem, tsend, trecv, osem):
     me = lax.axis_index('sp')
@@ -62,8 +62,8 @@
 
     def weight_copies(l):
         xc = [pltpu.make_async_copy(w_in_ref.at[l, pl.ds(pl.multiple_of(D_INNER + LOC * b + HALF * core, 16), HALF), :], wx.at[pl.ds(HALF * b, HALF), :], wsem.at[6 + b]) for b in range(2)]
-        bc = pltpu.make_async_copy(w_in_ref.at[l, pl.ds(2 * D_INNER, 304), :], wbc.at[pl.ds(0, 304), :], wsem.at[8])
-        oc = pltpu.make_async_copy(w_out_ref.at[l], wout, wsem.at[9])
+        bc = [pltpu.make_async_copy(w_in_ref.at[l, pl.ds(src, n), :], wbc.at[pl.ds(dst, n), :], wsem.at[sem]) for src, n, dst, sem in ((2 * D_INNER, 128, 0, 8), (2 * D_INNER + 256, HEADS, 128, 9), (2 * D_INNER + 128, 128, 256, 10))]
+        oc = pltpu.make_async_copy(w_out_ref.at[l], wout, wsem.at[11])
         return xc, bc, oc
 
     def z_copy(l, n):
@@ -79,10 +79,10 @@
         pl.semaphore_signal(barrier, inc=1, device_id={'sp': (me + step) % 4}, device_id_type=pl.DeviceIdType.MESH)
 
     hbuf[:, 0:HALO, :] = jnp.zeros((LAYERS * NB, HALO, D_MODEL), BF16)
-    wbc[304:384, :] = jnp.zeros((80, D_MODEL), BF16)
+    wbc[176:256, :] = jnp.zeros((80, D_MODEL), BF16)
     prm[...] = jnp.zeros((8, 128), F32)
     r_out[...] = resid_ref[...]
-    for c in [bc0] + xc0:
+    for c in bc0 + xc0:
         c.start()
     with jax.named_scope('barrier'):
         pl.semaphore_wait(barrier, 3)
@@ -137,15 +137,15 @@
             res.append(remote(ref, ref, tsend.at[l, b], trecv.at[l, b], partner))
         return res
 
-    def conv_chunk(act, src, groups, i, p, dst):
+    def conv_chunk(act, src, first, groups, i, p, dst):
         for g in range(groups):
             cols = slice(dst + 128 * g, dst + 128 * (g + 1))
-            acc = cwl[0:1, cols] * src[g, i, 13:141, :]
+            acc = cwl[0:1, cols] * src[first + g, i, 13:141, :]
             for k in range(1, 4):
-                acc = acc + cwl[k:k + 1, cols] * src[g, i, 13 + k:141 + k, :]
+                acc = acc + cwl[k:k + 1, cols] * src[first + g, i, 13 + k:141 + k, :]
             act[p, :, cols] = silu(acc + cwl[4:5, cols]).astype(BF16)
 
-    def block(l, p0, np_, row, act, tail, cumt, dtt, cum):
+    def block(l, p0, np_, row, act, tail, cumt, dtt, cum, with_c):
         def project(w, rows, dst):
             lhs = hbuf[pl.ds(NB * l + p0, np_), pl.ds(row, EXT), :].reshape(np_ * EXT, D_MODEL)
             res = round_bf16(dot_nt(lhs, w[rows, :]))
@@ -155,10 +155,10 @@
         def finish_bc(src):
             for i in range(np_):
                 p = p0 + i
-                for g in range(2):
-                    tail[p, :, LOC + 128 * g:LOC + 128 * (g + 1)] = src[g, i, BLK:EXT, :].astype(BF16)
-                conv_chunk(act, src, 2, i, p, LOC)
-                v = src[2, i, HALO:EXT, :] + prm[0:1, :]
+                for g, dst in ((0, LOC), (2, LOC + 128))[:2 if with_c else 1]:
+                    tail[p, :, dst:dst + 128] = src[g, i, BLK:EXT, :].astype(BF16)
+                    conv_chunk(act, src, g, 1, i, p, dst)
+                v = src[1, i, HALO:EXT, :] + prm[0:1, :]
                 dt = round_bf16(jnp.maximum(v, 0.0) + jnp.log1p(jnp.exp(-jnp.abs(v))))
                 logs = dt * prm[1:2, :]
                 dt = dt * (1.0 - core_f) + pltpu.roll(dt, 116, 1) * core_f
@@ -173,9 +173,9 @@
             for i in range(np_):
                 for g in range(4):
                     tail[p0 + i, :, 512 * n + 128 * g:512 * n + 128 * (g + 1)] = src[g, i, BLK:EXT, :].astype(BF16)
-                conv_chunk(act, src, 4, i, p0 + i, 512 * n)
-
-        project(wbc, slice(0, 384), rawa)
+                conv_chunk(act, src, 0, 4, i, p0 + i, 512 * n)
+
+        project(wbc, slice(0, 384 if with_c else 256), rawa)
         project(wx, slice(0, 512), rawb)
         finish_bc(rawa)
         project(wx, slice(512, 1024), rawa)
@@ -194,6 +194,7 @@
         return dtt[p, pl.ds(h, 1), :] * jnp.exp(row[:, 127:128] - row + extra)
 
     def intra_body(l, p):
+        bt_o[p] = act_o[p, :, LOC:LOC + 128].astype(F32).T
         cb = act_o[p, :, LOC + 128:ACT]
         scores = dot_nt(cb, act_o[p, :, LOC:LOC + 128]) * tri
         for j in range(PAIRS):
@@ -209,12 +210,9 @@
             yloc[p, :, 128 * j:128 * (j + 1)] = y
             ybuf[p, :, 128 * j:128 * (j + 1)] = y.astype(BF16)
 
-        @pl.when(chip == 0)
-        def _():
-            y_copy(l, p).start()
-
     def inter_body(l, p):
         bt = act_r[p, :, LOC:LOC + 128].astype(F32).T
+        bt_r[p] = bt
         cf = act_o[p, :, LOC + 128:ACT]
         for j in range(PAIRS):
             lhs = jnp.concatenate([(bt * decays(p, h, cumt_r, dtt_r, 0.0)).astype(BF16) for h in (head_row(2 * j), head_row(2 * j + 1))], axis=1)
@@ -230,45 +228,37 @@
                 ybuf[p, :, 128 * j:128 * (j + 1)] = y.astype(BF16)
         y_copy(l, p).start()
 
-    def final_body(l, p):
+    def final_pair(p, q):
+        h = 24 * chip + 2 * q
+        cols = pl.ds(pl.multiple_of(128 * (6 * chip + q), 128), 128)
+        left, right = [], []
+        for hh in (h, h + 1):
+            end_o = cumt_o[p, pl.ds(hh, 1), :][:, 127:128]
+            end_r = cumt_r[p, pl.ds(hh, 1), :][:, 127:128]
+            left.append((bt_o[p] * decays(p, hh, cumt_o, dtt_o, end_r * (1.0 - chip_f))).astype(BF16))
+            right.append((bt_r[p] * decays(p, hh, cumt_r, dtt_r, end_o * chip_f)).astype(BF16))
+        rhs = jnp.concatenate(split_pair(act_o[p, :, cols]) + split_pair(act_r[p, :, cols]), axis=0)
+        state = dot(jnp.concatenate(left + right, axis=1), rhs)
+        stg[p, pl.ds(2 * q, 2)] = state.T.reshape(2, 64, 128)
+
+    def wait_out(l):
         @pl.when(l > 0)
         def _():
-            out_copy(0, p).wait()
-        bto = act_o[p, :, LOC:LOC + 128].astype(F32).T
-        btr = act_r[p, :, LOC:LOC + 128].astype(F32).T
-        for q in range(6):
-            h = 24 * chip + 2 * q
-            cols = pl.ds(pl.multiple_of(128 * (6 * chip + q), 128), 128)
-            left, right = [], []
-            for hh in (h, h + 1):
-                end_o = cumt_o[p, pl.ds(hh, 1), :][:, 127:128]
-                end_r = cumt_r[p, pl.ds(hh, 1), :][:, 127:128]
-                left.append((bto * decays(p, hh, cumt_o, dtt_o, end_r * (1.0 - chip_f))).astype(BF16))
-                right.append((btr * decays(p, hh, cumt_r, dtt_r, end_o * chip_f)).astype(BF16))
-            rhs = jnp.concatenate(split_pair(act_o[p, :, cols]) + split_pair(act_r[p, :, cols]), axis=0)
-            state = dot(jnp.concatenate(left + right, axis=1), rhs)
-            stg[p, 2 * q:2 * q + 2] = state.T.reshape(2, 64, 128)
-        out_copy(l, p).start()
-
-    def early_tail(l):
-        @pl.when(core == 1)
-        def _():
-            c_tail(l).wait_recv()
-            f_tail(l).start()
-
-        @pl.when(core == 0)
-        def _():
-            f_tail(l).wait_recv()
-
-    def late_tail(l):
-        @pl.when(core == 0)
-        def _():
-            c_tail(l).wait_recv()
-            f_tail(l).start()
-
-        @pl.when(core == 1)
-        def _():
-            f_tail(l).wait_recv()
+            for p in range(NB):
+                out_copy(0, p).wait()
+
+    def pass_tail(l):
+        c_tail(l).wait_recv()
+        f_tail(l).start()
+
+    def pass_half(l, half):
+        c_half(l, half).wait_recv()
+        f_half(l, half).start()
+
+    def bulk(l):
+        c_half(l, 0).start()
+        c_tail(l).start()
+        c_half(l, 1).start()
 
     def after_other(l, tail):
         for b in range(2):
@@ -280,7 +270,7 @@
         @pl.when(l == 0)
         def _():
             xnx, bnx, _ = weight_copies(1)
-            for c in xnx + [bnx]:
+            for c in xnx + bnx:
                 c.start()
 
     def begin(l):
@@ -297,12 +287,12 @@
         @pl.when(core == 1)
         def _():
             c_tail(l).start()
-        c_half(l, 0).start()
-
-        @pl.when(core == 0)
-        def _():
-            c_tail(l).start()
-        c_half(l, 1).start()
+            c_half(l, 0).start()
+            c_half(l, 1).start()
+
+        @pl.when(jnp.logical_and(core == 0, l > 0))
+        def _():
+            bulk(l)
 
     def main(l):
         xc, bc, oc = weight_copies(l)
@@ -316,14 +306,23 @@
         prm[0:1, 0:HEADS] = dtb_ref[pl.ds(l, 1), :]
         prm[1:2, 0:HEADS] = -jnp.exp(alog_ref[pl.ds(l, 1), :])
 
-        def z_body(n, c):
+        def z_chunk(n):
             z_copy(l, n).wait()
             lhs = hbuf[pl.ds(NB * l, NB), pl.ds(own_row, SEG), :].reshape(NB * SEG, D_MODEL)
-            z = round_bf16(dot_nt(lhs, wz[pl.ds(pl.multiple_of(512 * n, 512), 512), :]))
-            sz[:, :, pl.ds(pl.multiple_of(512 * n, 512), 512)] = silu(z).reshape(NB, SEG, 512)
-            return c
+            cols = pl.ds(pl.multiple_of(512 * n, 512), 512)
+            z = round_bf16(dot_nt(lhs, wz[cols, :]))
+            sz[:, :, cols] = silu(z).reshape(NB, SEG, 512)
+
+        def z_loop(lo, hi):
+            lax.fori_loop(lo, hi, lambda n, c: (z_chunk(n), c)[1], 0)
+
         with jax.named_scope('zproj'):
-            lax.fori_loop(0, 6, z_body, 0)
+            z_loop(0, 2)
+
+            @pl.when(jnp.logical_and(core == 0, l == 0))
+            def _():
+                bulk(l)
+            z_loop(2, jnp.where(l == 0, 6, 2))
         oc.start()
 
         @pl.when(l == 0)
@@ -333,35 +332,69 @@
 
         with jax.named_scope('wait_h'):
             c_par(l).wait_recv()
-            bc.wait()
-            for c in xc:
+            for c in bc + xc:
                 c.wait()
 
-            @pl.when(chip == 1)
-            def _():
-                early_tail(l)
+            @pl.when(jnp.logical_and(chip == 1, core == 1))
+            def _():
+                pass_tail(l)
+
+            @pl.when(jnp.logical_and(chip == 1, core == 0))
+            def _():
+                f_tail(l).wait_recv()
         with jax.named_scope('own_block'):
-            block(l, 0, NB, own_blk, act_o, tail_o, cumt_o, dtt_o, cum_o)
+            block(l, 0, NB, own_blk, act_o, tail_o, cumt_o, dtt_o, cum_o, True)
+
+        def intra_end(p):
+            @pl.when(chip == 0)
+            def _():
+                y_copy(l, p).start()
+
+            @pl.when(jnp.logical_and(chip == 1, p == 1))
+            def _():
+                pass_half(l, 0)
+
+                @pl.when(core == 0)
+                def _():
+                    pass_tail(l)
+
+        def intra_plain(p, c):
+            intra_body(l, p)
+            intra_end(p)
+            return c
+
+        def intra_z(p, c):
+            z_chunk(2 + p)
+            intra_body(l, p)
+            intra_end(p)
+            return c
+
         with jax.named_scope('intra'):
-            lax.fori_loop(0, NB, lambda p, c: (intra_body(l, p), c)[1], 0)
+            @pl.when(l == 0)
+            def _():
+                lax.fori_loop(0, NB, intra_plain, 0)
+
+            @pl.when(l > 0)
+            def _():
+                lax.fori_loop(0, NB, intra_z, 0)
 
         @pl.when(chip == 1)
         def _():
             with jax.named_scope('wait_r0'):
-                c_half(l, 0).wait_recv()
-                f_half(l, 0).start()
-                late_tail(l)
                 f_half(l, 0).wait_recv()
+
+                @pl.when(core == 1)
+                def _():
+                    f_tail(l).wait_recv()
 
             def half_body(half, c):
                 with jax.named_scope('oth_block'):
-                    block(l, 2 * half, 2, oth_blk, act_r, tail_r, cumt_r, dtt_r, None)
+                    block(l, 2 * half, 2, oth_blk, act_r, tail_r, cumt_r, dtt_r, None, False)
 
                 @pl.when(half == 0)
                 def _():
                     with jax.named_scope('wait_c1'):
-                        c_half(l, 1).wait_recv()
-                        f_half(l, 1).start()
+                        pass_half(l, 1)
                 with jax.named_scope('inter'):
                     lax.fori_loop(2 * half, 2 * half + 2, lambda p, c: (inter_body(l, p), c)[1], 0)
 
@@ -371,8 +404,6 @@
                         f_half(l, 1).wait_recv()
                 return c
             lax.fori_loop(0, 2, half_body, 0)
-            with jax.named_scope('final'):
-                lax.fori_loop(0, NB, lambda p, c: (final_body(l, p), c)[1], 0)
             after_other(l, tail_o)
 
         def gate_body(p, c):
@@ -397,28 +428,66 @@
             lax.fori_loop(0, NB, gate_body, 0)
             oc.wait()
 
-        def out_body(n, c):
+        def out_chunk(n):
             cols = pl.ds(pl.multiple_of(512 * n, 512), 512)
             o = dot(gn[...].reshape(NB * SEG, D_INNER), wout[:, cols])
             r_out[:, :, cols] = r_out[:, :, cols] + o.reshape(NB, SEG, 512)
+
+        def out_final(n, c):
+            out_chunk(n)
+            for q in range(2):
+                for p in range(NB):
+                    final_pair(p, 2 * n + q)
             return c
+
         with jax.named_scope('outproj'):
-            lax.fori_loop(0, 3, out_body, 0)
+            @pl.when(chip == 0)
+            def _():
+                lax.fori_loop(0, 3, lambda n, c: (out_chunk(n), c)[1], 0)
+
+            @pl.when(chip == 1)
+            def _():
+                wait_out(l)
+                lax.fori_loop(0, 3, out_final, 0)
+                for p in range(NB):
+                    out_copy(l, p).start()
+
+        @pl.when(chip == 0)
+        def _():
+            with jax.named_scope('pass_d'):
+                @pl.when(core == 1)
+                def _():
+                    pass_tail(l)
+                pass_half(l, 0)
+
+                @pl.when(core == 0)
+                def _():
+                    pass_tail(l)
 
     def deferred(l):
         with jax.named_scope('wait_d'):
-            early_tail(l)
-            late_tail(l)
+            f_tail(l).wait_recv()
+            wait_out(l)
 
         def half_body(half, c):
             with jax.named_scope('wait_dh'):
-                c_half(l, half).wait_recv()
-                f_half(l, half).start()
                 f_half(l, half).wait_recv()
             with jax.named_scope('oth_block'):
-                block(l, 2 * half, 2, oth_blk, act_r, tail_r, cumt_r, dtt_r, None)
+                block(l, 2 * half, 2, oth_blk, act_r, tail_r, cumt_r, dtt_r, None, True)
+
+            @pl.when(half == 0)
+            def _():
+                with jax.named_scope('wait_c1'):
+                    pass_half(l, 1)
+
+            def final_body(p, cc):
+                bt_r[p] = act_r[p, :, LOC:LOC + 128].astype(F32).T
+                for q in range(6):
+                    final_pair(p, q)
+                out_copy(l, p).start()
+                return cc
             with jax.named_scope('final'):
-                lax.fori_loop(2 * half, 2 * half + 2, lambda p, c: (final_body(l, p), c)[1], 0)
+                lax.fori_loop(2 * half, 2 * half + 2, final_body, 0)
             return c
         lax.fori_loop(0, 2, half_body, 0)
         after_other(l, tail_r)
@@ -446,6 +515,15 @@
     for p in range(NB):
         pltpu.make_async_copy(stg.at[p], ssm_out.at[p, LAYERS - 1], osem.at[p]).wait()
     tail_out[...] = tails[...]
+
+
+def copy_kernel(r_ref, ssm_ref, tail_ref, r_out, ssm_out, conv_out):
+    r_out[...] = r_ref[...]
+    ssm_out[...] = ssm_ref[...]
+    for l in range(LAYERS):
+        rows = tail_ref[l, 0].astype(F32)
+        for k in range(3):
+            conv_out[0, k, l:l + 1, :] = rows[13 + k:14 + k, :].astype(BF16)
 
 
 def solution(mesh):
@@ -473,6 +551,8 @@
                 pltpu.VMEM((4, NB, EXT, 128), F32),
                 pltpu.VMEM((4, NB, EXT, 128), F32),
                 pltpu.VMEM((BLK, LOC), F32),
+                pltpu.VMEM((NB, BLK, BLK), F32),
+                pltpu.VMEM((NB, BLK, BLK), F32),
                 pltpu.VMEM((NB, BLK, ACT), BF16),
                 pltpu.VMEM((NB, BLK, ACT), BF16),
                 pltpu.VMEM((NB, BLK, LOC), F32),
@@ -490,7 +570,7 @@
                 pltpu.VMEM((NB, 40, BLK), F32),
                 pltpu.VMEM((8, ACT), F32),
                 pltpu.VMEM((8, 128), F32),
-                pltpu.SemaphoreType.DMA((10,)),
+                pltpu.SemaphoreType.DMA((12,)),
                 pltpu.SemaphoreType.DMA((LAYERS, 7)),
                 pltpu.SemaphoreType.DMA((LAYERS, 7)),
                 pltpu.SemaphoreType.DMA((LAYERS, NB)),
@@ -501,7 +581,21 @@
             ],
             compiler_params=pltpu.CompilerParams(collective_id=0, has_side_effects=True, vmem_limit_bytes=67043328),
         )(resid, pre_norm, jnp.swapaxes(w_in, 1, 2), jnp.swapaxes(conv_w, 1, 2), conv_b, dt_bias, a_log, d_skip, gate_norm, w_out)
-        conv_state = jnp.transpose(tails[:, :, 13:16, :], (1, 0, 3, 2))
-        return r, ssm, conv_state
+        specs = (
+            pl.BlockSpec((1, SEG, D_MODEL), lambda p: (p, 0, 0)),
+            pl.BlockSpec((1, LAYERS, 12, 64, 128), lambda p: (p, 0, 0, 0, 0)),
+        )
+        r, ssm, conv = pl.pallas_call(
+            copy_kernel,
+            grid=(NB,),
+            out_shape=(
+                jax.ShapeDtypeStruct(r.shape, F32),
+                jax.ShapeDtypeStruct(ssm.shape, F32),
+                jax.ShapeDtypeStruct((NB, 3, LAYERS, CONV_DIM), BF16),
+            ),
+            in_specs=list(specs) + [pl.BlockSpec((LAYERS, 1, 16, CONV_DIM), lambda p: (0, p, 0, 0))],
+            out_specs=specs + (pl.BlockSpec((1, 3, LAYERS, CONV_DIM), lambda p: (p, 0, 0, 0)),),
+        )(r, ssm, tails)
+        return r, ssm, jnp.transpose(conv, (0, 2, 3, 1))
 
     return jax.shard_map(forward, mesh=mesh, in_specs=(P('dp', 'sp', None), P(), P(), P(), P(), P(), P(), P(), P(), P()), out_specs=(P('dp', 'sp', None), P('dp', None, 'sp', None, None), P('dp', None, None, None)), check_vma=False)

time: 77.8 us -> 69.6 us (0.89)
  the two profiles are of different devices: /device:TPU:0 before, /device:TPU:11 now
where the time goes in v4:
time: 69.6 us; the launch traced here: 69.4 us
  Pallas kernels  68.8 us (99%)
    pallas_call x1, Pallas kernels, forward(): pl.pallas_call(kernel, out_shape=(jax.ShapeDtypeStruct((NB, SEG, D_MODEL)...  63.7 us
    pallas_call x1, Pallas kernels, forward(): pl.pallas_call(copy_kernel, grid=(NB,), out_shape=(jax.ShapeDtypeStruct(r...  5.07 us

profile of v4, /device:TPU:11, one launch (start us, length us, event | category | flops | bytes accessed | tf_op | source)
XLA Modules:
  0.0 69.4 jit_solution(15900335752084159599)
XLA Ops:
  0.6 63.7 %shard_map.121 = (f32[4,64,1536]{2,1,0:T(8,128)}, f32[4,2,12,64,128]{4,3,2,1,0:T(8,128)}, bf16[2,4,16,3328]{3,2,1,0:T(8,128)(2,1)}) custom-call(f32[4,64,1536]{2,1,0:T(8,128)} %resid_ref.1, f32[2,1536]{1,0:T(2,128)} %pre_ref.1, bf16[2,6448,1536]{2,1,0:T(8,128)(2,1)} %bitcast.3, f32[2,4,3328]{2,1,0:T(4,128)} %bitcast.4, f32[2,3328]{1,0:T(2,128)} %cb_ref.1, ...), custom_call_target="tpu_custom_call" | custom-call | tf_op jit(solution)/shard_map/pallas_call | solution.py:535
  64.3 5.1 %shard_map.122 = (f32[4,64,1536]{2,1,0:T(8,128)}, f32[4,2,12,64,128]{4,3,2,1,0:T(8,128)}, bf16[4,3,2,3328]{3,2,1,0:T(2,128)(2,1)}) custom-call(f32[4,64,1536]{2,1,0:T(8,128)} %get-tuple-element.9.r_ref, f32[4,2,12,64,128]{4,3,2,1,0:T(8,128)} %get-tuple-element.10.ssm_ref, bf16[2,4,16,3328]{3,2,1,0:T(8,128)(2,1)} %get-tuple-element.11.tail_ref), custom_call_target="tpu_custom_call" | custom-call | tf_op jit(solution)/shard_map/pallas_call | solution.py:588

commit v5 on v4

--- a/solution.py
+++ b/solution.py
@@ -47,11 +47,11 @@
     return i if i < 12 else i + 12
 
 
-def kernel(resid_ref, pre_ref, w_in_ref, cw_ref, cb_ref, dtb_ref, alog_ref, dskip_ref, gw_ref, w_out_ref,
-           r_out, ssm_out, tail_out,
-           hbuf, sz, wz, wx, wbc, wout, rawa, rawb, states, bt_o, bt_r, act_o, act_r, yloc, ybuf, yrecv, gn, stg, tails, tail_o, tail_r,
+def kernel(resid_hbm, pre_hbm, w_in_ref, cw_hbm, cb_hbm, dtb_hbm, alog_hbm, dskip_hbm, gw_hbm, w_out_ref,
+           r_hbm, ssm_out, tail_out,
+           r_out, pre_ref, cw_ref, cb_ref, dtb_ref, alog_ref, dskip_ref, gw_ref, hbuf, sz, wz, wx, wbc, wout, rawa, rawb, states, bt_o, bt_r, act_o, act_r, yloc, ybuf, yrecv, gn, stg, tails, tail_o, tail_r,
            cum_o, cumt_o, cumt_r, dtt_o, dtt_r, cwl, prm,
-           wsem, hsend, hrecv, ysend, yrecv_sem, tsend, trecv, osem):
+           wsem, hsend, hrecv, ysend, yrecv_sem, tsend, trecv, osem, psem, rsem, tout):
     me = lax.axis_index('sp')
     chip = me // 2
     core = me % 2
@@ -70,8 +70,14 @@
         rows = pl.ds(pl.multiple_of(512 * n, 16), 512)
         return pltpu.make_async_copy(w_in_ref.at[l, rows, :], wz.at[rows, :], wsem.at[n])
 
+    params = [pltpu.make_async_copy(src, dst, psem.at[i]) for i, (src, dst) in enumerate(((resid_hbm, r_out), (pre_hbm, pre_ref), (cw_hbm, cw_ref), (cb_hbm, cb_ref), (dtb_hbm, dtb_ref), (alog_hbm, alog_ref), (dskip_hbm, dskip_ref), (gw_hbm, gw_ref)))]
     xc0, bc0, oc0 = weight_copies(0)
-    for n in range(6):
+    params[0].start()
+    params[1].start()
+    z_copy(0, 0).start()
+    for c in params[2:]:
+        c.start()
+    for n in range(1, 6):
         z_copy(0, n).start()
 
     barrier = pltpu.get_barrier_semaphore()
@@ -81,9 +87,11 @@
     hbuf[:, 0:HALO, :] = jnp.zeros((LAYERS * NB, HALO, D_MODEL), BF16)
     wbc[176:256, :] = jnp.zeros((80, D_MODEL), BF16)
     prm[...] = jnp.zeros((8, 128), F32)
-    r_out[...] = resid_ref[...]
     for c in bc0 + xc0:
         c.start()
+    with jax.named_scope('params'):
+        for c in params:
+            c.wait()
     with jax.named_scope('barrier'):
         pl.semaphore_wait(barrier, 3)
 
@@ -114,21 +122,43 @@
     def c_tail(l):
         return same(l, 1, 0, NB, own_row + 48, 16, other)
 
-    def c_half(l, half):
-        return same(l, 2 + half, 2 * half, 2, own_row, 48, other)
+    def c_half(l, half, size):
+        return same(l, 2 + half, 2 * half, 2, own_row, size, other)
 
     def f_tail(l):
         return same(l, 4, 0, NB, oth_row + 48, 16, partner)
 
-    def f_half(l, half):
-        return same(l, 5 + half, 2 * half, 2, oth_row, 48, partner)
+    def f_half(l, half, size):
+        return same(l, 5 + half, 2 * half, 2, oth_row, size, partner)
+
+    def by_core(fn):
+        @pl.when(core == 0)
+        def _():
+            fn(64)
+
+        @pl.when(core == 1)
+        def _():
+            fn(48)
+
+    def wait_half(l, half):
+        by_core(lambda n: f_half(l, half, 112 - n).wait_recv())
 
     def y_copy(l, p):
         src = ybuf.at[p, pl.ds(pl.multiple_of(SEG * (1 - core), 16), SEG), :]
         return remote(src, yrecv.at[NB * l + p], ysend.at[l, p], yrecv_sem.at[l, p], partner)
 
-    def out_copy(l, p):
+    def out_prompt(l, p):
         return pltpu.make_async_copy(stg.at[p], ssm_out.at[p, l], osem.at[p])
+
+    def out_heads(l, n):
+        return pltpu.make_async_copy(stg.at[:, pl.ds(4 * n, 4)], ssm_out.at[:, l, pl.ds(4 * n, 4)], osem.at[n])
+
+    def r_copy(n):
+        cols = pl.ds(pl.multiple_of(512 * n, 512), 512)
+        return pltpu.make_async_copy(r_out.at[:, :, cols], r_hbm.at[:, :, cols], rsem.at[n])
+
+    def tail_copy(l):
+        return pltpu.make_async_copy(tails.at[l], tail_out.at[l], tout.at[l])
 
     def tail_copies(l):
         res = []
@@ -241,24 +271,19 @@
         state = dot(jnp.concatenate(left + right, axis=1), rhs)
         stg[p, pl.ds(2 * q, 2)] = state.T.reshape(2, 64, 128)
 
-    def wait_out(l):
-        @pl.when(l > 0)
-        def _():
-            for p in range(NB):
-                out_copy(0, p).wait()
-
     def pass_tail(l):
         c_tail(l).wait_recv()
         f_tail(l).start()
 
     def pass_half(l, half):
-        c_half(l, half).wait_recv()
-        f_half(l, half).start()
+        def go(n):
+            c_half(l, half, n).wait_recv()
+            f_half(l, half, n).start()
+        by_core(go)
 
     def bulk(l):
-        c_half(l, 0).start()
-        c_tail(l).start()
-        c_half(l, 1).start()
+        c_half(l, 0, 64).start()
+        c_half(l, 1, 64).start()
 
     def after_other(l, tail):
         for b in range(2):
@@ -287,12 +312,16 @@
         @pl.when(core == 1)
         def _():
             c_tail(l).start()
-            c_half(l, 0).start()
-            c_half(l, 1).start()
+            c_half(l, 0, 48).start()
+            c_half(l, 1, 48).start()
 
         @pl.when(jnp.logical_and(core == 0, l > 0))
         def _():
             bulk(l)
+
+        @pl.when(jnp.logical_and(jnp.logical_and(core == 1, chip == 1), l > 0))
+        def _():
+            pass_tail(l)
 
     def main(l):
         xc, bc, oc = weight_copies(l)
@@ -335,7 +364,7 @@
             for c in bc + xc:
                 c.wait()
 
-            @pl.when(jnp.logical_and(chip == 1, core == 1))
+            @pl.when(jnp.logical_and(jnp.logical_and(core == 1, chip == 1), l == 0))
             def _():
                 pass_tail(l)
 
@@ -353,10 +382,6 @@
             @pl.when(jnp.logical_and(chip == 1, p == 1))
             def _():
                 pass_half(l, 0)
-
-                @pl.when(core == 0)
-                def _():
-                    pass_tail(l)
 
         def intra_plain(p, c):
             intra_body(l, p)
@@ -381,11 +406,7 @@
         @pl.when(chip == 1)
         def _():
             with jax.named_scope('wait_r0'):
-                f_half(l, 0).wait_recv()
-
-                @pl.when(core == 1)
-                def _():
-                    f_tail(l).wait_recv()
+                wait_half(l, 0)
 
             def half_body(half, c):
                 with jax.named_scope('oth_block'):
@@ -401,7 +422,7 @@
                 @pl.when(half == 0)
                 def _():
                     with jax.named_scope('wait_f1'):
-                        f_half(l, 1).wait_recv()
+                        wait_half(l, 1)
                 return c
             lax.fori_loop(0, 2, half_body, 0)
             after_other(l, tail_o)
@@ -433,24 +454,37 @@
             o = dot(gn[...].reshape(NB * SEG, D_INNER), wout[:, cols])
             r_out[:, :, cols] = r_out[:, :, cols] + o.reshape(NB, SEG, 512)
 
+        def send_r(n):
+            @pl.when(l == LAYERS - 1)
+            def _():
+                r_copy(n).start()
+
         def out_final(n, c):
             out_chunk(n)
             for q in range(2):
                 for p in range(NB):
                     final_pair(p, 2 * n + q)
+            out_heads(l, n).start()
+            send_r(n)
+            return c
+
+        def out_plain(n, c):
+            out_chunk(n)
+            send_r(n)
             return c
 
         with jax.named_scope('outproj'):
             @pl.when(chip == 0)
             def _():
-                lax.fori_loop(0, 3, lambda n, c: (out_chunk(n), c)[1], 0)
+                lax.fori_loop(0, 3, out_plain, 0)
 
             @pl.when(chip == 1)
             def _():
-                wait_out(l)
+                @pl.when(l > 0)
+                def _():
+                    for n in range(3):
+                        out_heads(0, n).wait()
                 lax.fori_loop(0, 3, out_final, 0)
-                for p in range(NB):
-                    out_copy(l, p).start()
 
         @pl.when(chip == 0)
         def _():
@@ -460,18 +494,20 @@
                     pass_tail(l)
                 pass_half(l, 0)
 
-                @pl.when(core == 0)
-                def _():
-                    pass_tail(l)
-
     def deferred(l):
         with jax.named_scope('wait_d'):
-            f_tail(l).wait_recv()
-            wait_out(l)
+            @pl.when(core == 0)
+            def _():
+                f_tail(l).wait_recv()
+
+            @pl.when(l > 0)
+            def _():
+                for p in range(NB):
+                    out_prompt(0, p).wait()
 
         def half_body(half, c):
             with jax.named_scope('wait_dh'):
-                f_half(l, half).wait_recv()
+                wait_half(l, half)
             with jax.named_scope('oth_block'):
                 block(l, 2 * half, 2, oth_blk, act_r, tail_r, cumt_r, dtt_r, None, True)
 
@@ -479,18 +515,21 @@
             def _():
                 with jax.named_scope('wait_c1'):
                     pass_half(l, 1)
+
+            @pl.when(half == 1)
+            def _():
+                after_other(l, tail_r)
 
             def final_body(p, cc):
                 bt_r[p] = act_r[p, :, LOC:LOC + 128].astype(F32).T
                 for q in range(6):
                     final_pair(p, q)
-                out_copy(l, p).start()
+                out_prompt(l, p).start()
                 return cc
             with jax.named_scope('final'):
                 lax.fori_loop(2 * half, 2 * half + 2, final_body, 0)
             return c
         lax.fori_loop(0, 2, half_body, 0)
-        after_other(l, tail_r)
 
     def step(l, carry):
         @pl.when(l < LAYERS)
@@ -508,28 +547,68 @@
 
     lax.fori_loop(0, LAYERS + 1, step, 0)
     for l in range(LAYERS):
-        for c in [c_par(l), c_tail(l), c_half(l, 0), c_half(l, 1), f_tail(l), f_half(l, 0), f_half(l, 1)]:
-            c.wait_send()
         for c in tail_copies(l):
             c.wait()
+        tail_copy(l).start()
+    for l in range(LAYERS):
+        c_par(l).wait_send()
+
+        @pl.when(core == 1)
+        def _():
+            c_tail(l).wait_send()
+            f_tail(l).wait_send()
+
+        def sent(n):
+            for half in range(2):
+                c_half(l, half, n).wait_send()
+                f_half(l, half, n).wait_send()
+        by_core(sent)
+        tail_copy(l).wait()
+
+    @pl.when(chip == 0)
+    def _():
+        for p in range(NB):
+            out_prompt(LAYERS - 1, p).wait()
+
+    @pl.when(chip == 1)
+    def _():
+        for n in range(3):
+            out_heads(LAYERS - 1, n).wait()
+    for n in range(3):
+        r_copy(n).wait()
+
+
+def copy_kernel(r_ref, ssm_ref, tail_ref, r_out, ssm_out, conv_out, rbuf, sbuf, tbuf, cbuf, isem, osem):
+    def copies(p):
+        srcs = (r_ref.at[p], ssm_ref.at[p], tail_ref.at[:, p])
+        bufs = (rbuf.at[p], sbuf.at[p], tbuf.at[p])
+        dsts = (r_out.at[p], ssm_out.at[p], conv_out.at[p])
+        outs = (rbuf.at[p], sbuf.at[p], cbuf.at[p])
+        ins = [pltpu.make_async_copy(srcs[i], bufs[i], isem.at[p, i]) for i in range(3)]
+        res = [pltpu.make_async_copy(outs[i], dsts[i], osem.at[p, i]) for i in range(3)]
+        return ins, res
+
     for p in range(NB):
-        pltpu.make_async_copy(stg.at[p], ssm_out.at[p, LAYERS - 1], osem.at[p]).wait()
-    tail_out[...] = tails[...]
-
-
-def copy_kernel(r_ref, ssm_ref, tail_ref, r_out, ssm_out, conv_out):
-    r_out[...] = r_ref[...]
-    ssm_out[...] = ssm_ref[...]
-    for l in range(LAYERS):
-        rows = tail_ref[l, 0].astype(F32)
-        for k in range(3):
-            conv_out[0, k, l:l + 1, :] = rows[13 + k:14 + k, :].astype(BF16)
+        for c in copies(p)[0]:
+            c.start()
+    for p in range(NB):
+        ins, res = copies(p)
+        for i in range(2):
+            ins[i].wait()
+            res[i].start()
+        ins[2].wait()
+        for l in range(LAYERS):
+            rows = tbuf[p, l].astype(F32)
+            for k in range(3):
+                cbuf[p, k, l:l + 1, :] = rows[13 + k:14 + k, :].astype(BF16)
+        res[2].start()
+    for p in range(NB):
+        for c in copies(p)[1]:
+            c.wait()
 
 
 def solution(mesh):
-    vmem = pl.BlockSpec(memory_space=pltpu.VMEM)
     hbm = pl.BlockSpec(memory_space=pl.ANY)
-    smem = pl.BlockSpec(memory_space=pltpu.SMEM)
 
     def forward(resid, pre_norm, w_in, conv_w, conv_b, dt_bias, a_log, d_skip, gate_norm, w_out):
         r, ssm, tails = pl.pallas_call(
@@ -539,9 +618,17 @@
                 jax.ShapeDtypeStruct((NB, LAYERS, 12, 64, 128), F32),
                 jax.ShapeDtypeStruct((LAYERS, NB, 16, CONV_DIM), BF16),
             ),
-            in_specs=[vmem, vmem, hbm, vmem, vmem, vmem, vmem, smem, vmem, hbm],
-            out_specs=(vmem, hbm, vmem),
+            in_specs=[hbm] * 10,
+            out_specs=(hbm, hbm, hbm),
             scratch_shapes=[
+                pltpu.VMEM((NB, SEG, D_MODEL), F32),
+                pltpu.VMEM((LAYERS, D_MODEL), F32),
+                pltpu.VMEM((LAYERS, 4, CONV_DIM), F32),
+                pltpu.VMEM((LAYERS, CONV_DIM), F32),
+                pltpu.VMEM((LAYERS, HEADS), F32),
+                pltpu.VMEM((LAYERS, HEADS), F32),
+                pltpu.SMEM((LAYERS, HEADS), F32),
+                pltpu.VMEM((LAYERS, 1, D_INNER), F32),
                 pltpu.VMEM((LAYERS * NB, ROWS, D_MODEL), BF16),
                 pltpu.VMEM((NB, SEG, D_INNER), F32),
                 pltpu.VMEM((D_INNER, D_MODEL), BF16),
@@ -578,23 +665,29 @@
                 pltpu.SemaphoreType.DMA((LAYERS, 2)),
                 pltpu.SemaphoreType.DMA((LAYERS, 2)),
                 pltpu.SemaphoreType.DMA((NB,)),
+                pltpu.SemaphoreType.DMA((8,)),
+                pltpu.SemaphoreType.DMA((3,)),
+                pltpu.SemaphoreType.DMA((LAYERS,)),
             ],
             compiler_params=pltpu.CompilerParams(collective_id=0, has_side_effects=True, vmem_limit_bytes=67043328),
         )(resid, pre_norm, jnp.swapaxes(w_in, 1, 2), jnp.swapaxes(conv_w, 1, 2), conv_b, dt_bias, a_log, d_skip, gate_norm, w_out)
-        specs = (
-            pl.BlockSpec((1, SEG, D_MODEL), lambda p: (p, 0, 0)),
-            pl.BlockSpec((1, LAYERS, 12, 64, 128), lambda p: (p, 0, 0, 0, 0)),
-        )
         r, ssm, conv = pl.pallas_call(
             copy_kernel,
-            grid=(NB,),
             out_shape=(
                 jax.ShapeDtypeStruct(r.shape, F32),
                 jax.ShapeDtypeStruct(ssm.shape, F32),
                 jax.ShapeDtypeStruct((NB, 3, LAYERS, CONV_DIM), BF16),
             ),
-            in_specs=list(specs) + [pl.BlockSpec((LAYERS, 1, 16, CONV_DIM), lambda p: (0, p, 0, 0))],
-            out_specs=specs + (pl.BlockSpec((1, 3, LAYERS, CONV_DIM), lambda p: (p, 0, 0, 0)),),
+            in_specs=[hbm] * 3,
+            out_specs=(hbm, hbm, hbm),
+            scratch_shapes=[
+                pltpu.VMEM((NB, SEG, D_MODEL), F32),
+                pltpu.VMEM((NB, LAYERS, 12, 64, 128), F32),
+                pltpu.VMEM((NB, LAYERS, 16, CONV_DIM), BF16),
+                pltpu.VMEM((NB, 3, LAYERS, CONV_DIM), BF16),
+                pltpu.SemaphoreType.DMA((NB, 3)),
+                pltpu.SemaphoreType.DMA((NB, 3)),
+            ],
         )(r, ssm, tails)
         return r, ssm, jnp.transpose(conv, (0, 2, 3, 1))
 

time: 69.6 us -> 67.6 us (0.971)
  Pallas kernels: 68.8 us -> 66.8 us
    pallas_call x1, Pallas kernels: 63.7 us -> 61.9 us  [forward(): pl.pallas_call(kernel, out_shape=(jax.ShapeDtypeStruct((NB, SEG, D_MODEL)...]
where the time goes in v5:
time: 67.6 us; the launch traced here: 67.4 us
  Pallas kernels  66.8 us (99%)
    pallas_call x1, Pallas kernels, forward(): pl.pallas_call(kernel, out_shape=(jax.ShapeDtypeStruct((NB, SEG, D_MODEL)...  61.9 us
    pallas_call x1, Pallas kernels, forward(): pl.pallas_call(copy_kernel, out_shape=(jax.ShapeDtypeStruct(r.shape, F32)...  4.93 us

profile of v5, /device:TPU:11, one launch (start us, length us, event | category | flops | bytes accessed | tf_op | source)
XLA Modules:
  0.0 67.4 jit_solution(1080192364574151993)
XLA Ops:
  0.6 61.9 %shard_map.121 = (f32[4,64,1536]{2,1,0:T(8,128)}, f32[4,2,12,64,128]{4,3,2,1,0:T(8,128)}, bf16[2,4,16,3328]{3,2,1,0:T(8,128)(2,1)}) custom-call(f32[4,64,1536]{2,1,0:T(8,128)} %resid_hbm.1, f32[2,1536]{1,0:T(2,128)} %pre_hbm.1, bf16[2,6448,1536]{2,1,0:T(8,128)(2,1)} %bitcast.3, f32[2,4,3328]{2,1,0:T(4,128)} %bitcast.4, f32[2,3328]{1,0:T(2,128)} %cb_hbm.1, ...), custom_call_target="tpu_custom_call" | custom-call | tf_op jit(solution)/shard_map/pallas_call | solution.py:614
  62.5 4.9 %shard_map.122 = (f32[4,64,1536]{2,1,0:T(8,128)}, f32[4,2,12,64,128]{4,3,2,1,0:T(8,128)}, bf16[4,3,2,3328]{3,2,1,0:T(2,128)(2,1)}) custom-call(f32[4,64,1536]{2,1,0:T(8,128)} %get-tuple-element.9.r_ref, f32[4,2,12,64,128]{4,3,2,1,0:T(8,128)} %get-tuple-element.10.ssm_ref, bf16[2,4,16,3328]{3,2,1,0:T(8,128)(2,1)} %get-tuple-element.11.tail_ref), custom_call_target="tpu_custom_call" | custom-call | tf_op jit(solution)/shard_map/pallas_call | solution.py:674

commit v6 on v5

--- a/solution.py
+++ b/solution.py
@@ -1,3 +1,5 @@
+import functools
+
 import jax
 import jax.numpy as jnp
 from jax import lax
@@ -23,6 +25,7 @@
 LOC = 1536
 ACT = LOC + 256
 PAIRS = 12
+VMEM_LIMIT = 57200000
 NT = (((1,), (1,)), ((), ()))
 
 
@@ -90,7 +93,7 @@
     for c in bc0 + xc0:
         c.start()
     with jax.named_scope('params'):
-        for c in params:
+        for c in params[:2]:
             c.wait()
     with jax.named_scope('barrier'):
         pl.semaphore_wait(barrier, 3)
@@ -175,7 +178,7 @@
                 acc = acc + cwl[k:k + 1, cols] * src[first + g, i, 13 + k:141 + k, :]
             act[p, :, cols] = silu(acc + cwl[4:5, cols]).astype(BF16)
 
-    def block(l, p0, np_, row, act, tail, cumt, dtt, cum, with_c):
+    def block(l, p0, np_, row, act, tail, cumt, dtt, cum, with_c, width):
         def project(w, rows, dst):
             lhs = hbuf[pl.ds(NB * l + p0, np_), pl.ds(row, EXT), :].reshape(np_ * EXT, D_MODEL)
             res = round_bf16(dot_nt(lhs, w[rows, :]))
@@ -186,7 +189,8 @@
             for i in range(np_):
                 p = p0 + i
                 for g, dst in ((0, LOC), (2, LOC + 128))[:2 if with_c else 1]:
-                    tail[p, :, dst:dst + 128] = src[g, i, BLK:EXT, :].astype(BF16)
+                    if tail is not None:
+                        tail[p, :, dst:dst + 128] = src[g, i, BLK:EXT, :].astype(BF16)
                     conv_chunk(act, src, g, 1, i, p, dst)
                 v = src[1, i, HALO:EXT, :] + prm[0:1, :]
                 dt = round_bf16(jnp.maximum(v, 0.0) + jnp.log1p(jnp.exp(-jnp.abs(v))))
@@ -199,20 +203,30 @@
                 if cum is not None:
                     cum[p] = cums
 
-        def finish_x(src, n):
+        def finish_x(src, col, n):
             for i in range(np_):
-                for g in range(4):
-                    tail[p0 + i, :, 512 * n + 128 * g:512 * n + 128 * (g + 1)] = src[g, i, BLK:EXT, :].astype(BF16)
-                conv_chunk(act, src, 0, 4, i, p0 + i, 512 * n)
+                if tail is not None:
+                    for g in range(n // 128):
+                        tail[p0 + i, :, col + 128 * g:col + 128 * (g + 1)] = src[g, i, BLK:EXT, :].astype(BF16)
+                conv_chunk(act, src, 0, n // 128, i, p0 + i, col)
 
         project(wbc, slice(0, 384 if with_c else 256), rawa)
-        project(wx, slice(0, 512), rawb)
-        finish_bc(rawa)
-        project(wx, slice(512, 1024), rawa)
-        finish_x(rawb, 0)
-        project(wx, slice(1024, 1536), rawb)
-        finish_x(rawa, 1)
-        finish_x(rawb, 2)
+        pending, nxt = (lambda: finish_bc(rawa)), rawb
+        for col in range(0, width, 512):
+            n = min(512, width - col)
+            project(wx, slice(col, col + n), nxt)
+            pending()
+            pending = functools.partial(finish_x, nxt, col, n)
+            nxt = rawa if nxt is rawb else rawb
+        pending()
+
+    def last_rows(l, tail):
+        lhs = hbuf[pl.ds(NB * l, NB), ROWS - 16:ROWS, :].reshape(NB * 16, D_MODEL)
+        for col in range(0, LOC, 512):
+            tail[:, :, col:col + 512] = dot_nt(lhs, wx[col:col + 512, :]).astype(BF16).reshape(NB, 16, 512)
+        res = dot_nt(lhs, wbc[...]).astype(BF16).reshape(NB, 16, 384)
+        tail[:, :, LOC:LOC + 128] = res[:, :, 0:128]
+        tail[:, :, LOC + 128:ACT] = res[:, :, 256:384]
 
     zero = jnp.zeros((), BF16)
 
@@ -292,6 +306,7 @@
         for c in tail_copies(l):
             c.start()
 
+    def next_weights(l):
         @pl.when(l == 0)
         def _():
             xnx, bnx, _ = weight_copies(1)
@@ -326,6 +341,40 @@
     def main(l):
         xc, bc, oc = weight_copies(l)
 
+        def z_chunk(n):
+            lhs = hbuf[pl.ds(NB * l, NB), pl.ds(own_row, SEG), :].reshape(NB * SEG, D_MODEL)
+            cols = slice(512 * n, 512 * (n + 1)) if isinstance(n, int) else pl.ds(pl.multiple_of(512 * n, 512), 512)
+            z = round_bf16(dot_nt(lhs, wz[cols, :]))
+            sz[:, :, cols] = silu(z).reshape(NB, SEG, 512)
+
+        def z_group(lo):
+            for n in range(lo, lo + 3):
+                z_copy(l, n).wait()
+            for n in range(lo, lo + 3):
+                z_chunk(n)
+
+        with jax.named_scope('zproj'):
+            z_group(0)
+
+            @pl.when(jnp.logical_and(core == 0, l == 0))
+            def _():
+                bulk(l)
+
+            @pl.when(l == 0)
+            def _():
+                z_group(3)
+        oc.start()
+
+        @pl.when(l == 0)
+        def _():
+            for n in range(6):
+                z_copy(1, n).start()
+
+        @pl.when(l == 0)
+        def _():
+            for c in params[2:]:
+                c.wait()
+
         for b in range(2):
             src = pl.multiple_of(LOC * b + HALF * core, 128)
             cwl[0:4, HALF * b:HALF * (b + 1)] = cw_ref[l, :, pl.ds(src, HALF)]
@@ -335,30 +384,6 @@
         prm[0:1, 0:HEADS] = dtb_ref[pl.ds(l, 1), :]
         prm[1:2, 0:HEADS] = -jnp.exp(alog_ref[pl.ds(l, 1), :])
 
-        def z_chunk(n):
-            z_copy(l, n).wait()
-            lhs = hbuf[pl.ds(NB * l, NB), pl.ds(own_row, SEG), :].reshape(NB * SEG, D_MODEL)
-            cols = pl.ds(pl.multiple_of(512 * n, 512), 512)
-            z = round_bf16(dot_nt(lhs, wz[cols, :]))
-            sz[:, :, cols] = silu(z).reshape(NB, SEG, 512)
-
-        def z_loop(lo, hi):
-            lax.fori_loop(lo, hi, lambda n, c: (z_chunk(n), c)[1], 0)
-
-        with jax.named_scope('zproj'):
-            z_loop(0, 2)
-
-            @pl.when(jnp.logical_and(core == 0, l == 0))
-            def _():
-                bulk(l)
-            z_loop(2, jnp.where(l == 0, 6, 2))
-        oc.start()
-
-        @pl.when(l == 0)
-        def _():
-            for n in range(6):
-                z_copy(1, n).start()
-
         with jax.named_scope('wait_h'):
             c_par(l).wait_recv()
             for c in bc + xc:
@@ -372,7 +397,7 @@
             def _():
                 f_tail(l).wait_recv()
         with jax.named_scope('own_block'):
-            block(l, 0, NB, own_blk, act_o, tail_o, cumt_o, dtt_o, cum_o, True)
+            block(l, 0, NB, own_blk, act_o, tail_o, cumt_o, dtt_o, cum_o, True, LOC)
 
         def intra_end(p):
             @pl.when(chip == 0)
@@ -389,19 +414,19 @@
             return c
 
         def intra_z(p, c):
-            z_chunk(2 + p)
+            z_chunk(3 + p)
             intra_body(l, p)
             intra_end(p)
             return c
 
         with jax.named_scope('intra'):
-            @pl.when(l == 0)
-            def _():
-                lax.fori_loop(0, NB, intra_plain, 0)
-
             @pl.when(l > 0)
             def _():
-                lax.fori_loop(0, NB, intra_z, 0)
+                for n in range(3, 6):
+                    z_copy(l, n).wait()
+            split = jnp.where(l == 0, 0, 3)
+            lax.fori_loop(0, split, intra_z, 0)
+            lax.fori_loop(split, NB, intra_plain, 0)
 
         @pl.when(chip == 1)
         def _():
@@ -410,7 +435,7 @@
 
             def half_body(half, c):
                 with jax.named_scope('oth_block'):
-                    block(l, 2 * half, 2, oth_blk, act_r, tail_r, cumt_r, dtt_r, None, False)
+                    block(l, 2 * half, 2, oth_blk, act_r, None, cumt_r, dtt_r, None, False, LOC)
 
                 @pl.when(half == 0)
                 def _():
@@ -426,6 +451,7 @@
                 return c
             lax.fori_loop(0, 2, half_body, 0)
             after_other(l, tail_o)
+            next_weights(l)
 
         def gate_body(p, c):
             y_copy(l, p).wait()
@@ -504,12 +530,15 @@
             def _():
                 for p in range(NB):
                     out_prompt(0, p).wait()
+        with jax.named_scope('last_rows'):
+            last_rows(l, tail_r)
+            after_other(l, tail_r)
 
         def half_body(half, c):
             with jax.named_scope('wait_dh'):
                 wait_half(l, half)
             with jax.named_scope('oth_block'):
-                block(l, 2 * half, 2, oth_blk, act_r, tail_r, cumt_r, dtt_r, None, True)
+                block(l, 2 * half, 2, oth_blk, act_r, None, cumt_r, dtt_r, None, False, HALF)
 
             @pl.when(half == 0)
             def _():
@@ -518,7 +547,7 @@
 
             @pl.when(half == 1)
             def _():
-                after_other(l, tail_r)
+                next_weights(l)
 
             def final_body(p, cc):
                 bt_r[p] = act_r[p, :, LOC:LOC + 128].astype(F32).T
@@ -578,33 +607,22 @@
         r_copy(n).wait()
 
 
-def copy_kernel(r_ref, ssm_ref, tail_ref, r_out, ssm_out, conv_out, rbuf, sbuf, tbuf, cbuf, isem, osem):
-    def copies(p):
-        srcs = (r_ref.at[p], ssm_ref.at[p], tail_ref.at[:, p])
-        bufs = (rbuf.at[p], sbuf.at[p], tbuf.at[p])
-        dsts = (r_out.at[p], ssm_out.at[p], conv_out.at[p])
-        outs = (rbuf.at[p], sbuf.at[p], cbuf.at[p])
-        ins = [pltpu.make_async_copy(srcs[i], bufs[i], isem.at[p, i]) for i in range(3)]
-        res = [pltpu.make_async_copy(outs[i], dsts[i], osem.at[p, i]) for i in range(3)]
-        return ins, res
-
+def copy_kernel(r_ref, ssm_ref, tail_ref, r_out, ssm_out, conv_out, tbuf, cbuf, sems):
+    whole = [pltpu.make_async_copy(r_ref, r_out, sems.at[0]), pltpu.make_async_copy(ssm_ref, ssm_out, sems.at[1])]
+    load = pltpu.make_async_copy(tail_ref, tbuf, sems.at[2])
+    load.start()
+    for c in whole:
+        c.start()
+    load.wait()
     for p in range(NB):
-        for c in copies(p)[0]:
-            c.start()
-    for p in range(NB):
-        ins, res = copies(p)
-        for i in range(2):
-            ins[i].wait()
-            res[i].start()
-        ins[2].wait()
         for l in range(LAYERS):
-            rows = tbuf[p, l].astype(F32)
+            rows = tbuf[l, p].astype(F32)
             for k in range(3):
                 cbuf[p, k, l:l + 1, :] = rows[13 + k:14 + k, :].astype(BF16)
-        res[2].start()
-    for p in range(NB):
-        for c in copies(p)[1]:
-            c.wait()
+    store = pltpu.make_async_copy(cbuf, conv_out, sems.at[3])
+    store.start()
+    for c in whole + [store]:
+        c.wait()
 
 
 def solution(mesh):
@@ -614,9 +632,9 @@
         r, ssm, tails = pl.pallas_call(
             kernel,
             out_shape=(
-                jax.ShapeDtypeStruct((NB, SEG, D_MODEL), F32),
-                jax.ShapeDtypeStruct((NB, LAYERS, 12, 64, 128), F32),
-                jax.ShapeDtypeStruct((LAYERS, NB, 16, CONV_DIM), BF16),
+                pltpu.VMEM((NB, SEG, D_MODEL), F32),
+                pltpu.VMEM((NB, LAYERS, 12, 64, 128), F32),
+                pltpu.VMEM((LAYERS, NB, 16, CONV_DIM), BF16),
             ),
             in_specs=[hbm] * 10,
             out_specs=(hbm, hbm, hbm),
@@ -669,7 +687,7 @@
                 pltpu.SemaphoreType.DMA((3,)),
                 pltpu.SemaphoreType.DMA((LAYERS,)),
             ],
-            compiler_params=pltpu.CompilerParams(collective_id=0, has_side_effects=True, vmem_limit_bytes=67043328),
+            compiler_params=pltpu.CompilerParams(collective_id=0, has_side_effects=True, vmem_limit_bytes=VMEM_LIMIT),
         )(resid, pre_norm, jnp.swapaxes(w_in, 1, 2), jnp.swapaxes(conv_w, 1, 2), conv_b, dt_bias, a_log, d_skip, gate_norm, w_out)
         r, ssm, conv = pl.pallas_call(
             copy_kernel,
@@ -681,13 +699,11 @@
             in_specs=[hbm] * 3,
             out_specs=(hbm, hbm, hbm),
             scratch_shapes=[
-                pltpu.VMEM((NB, SEG, D_MODEL), F32),
-                pltpu.VMEM((NB, LAYERS, 12, 64, 128), F32),
-                pltpu.VMEM((NB, LAYERS, 16, CONV_DIM), BF16),
+                pltpu.VMEM((LAYERS, NB, 16, CONV_DIM), BF16),
                 pltpu.VMEM((NB, 3, LAYERS, CONV_DIM), BF16),
-                pltpu.SemaphoreType.DMA((NB, 3)),
-                pltpu.SemaphoreType.DMA((NB, 3)),
+                pltpu.SemaphoreType.DMA((4,)),
             ],
+            compiler_params=pltpu.CompilerParams(vmem_limit_bytes=4 * 1024 * 1024),
         )(r, ssm, tails)
         return r, ssm, jnp.transpose(conv, (0, 2, 3, 1))
 

time: 67.6 us -> 62.8 us (0.929)
  Pallas kernels: 66.8 us -> 62 us
    pallas_call x1, Pallas kernels: 4.93 us -> 2.39 us  [forward(): pl.pallas_call(copy_kernel, out_shape=(jax.ShapeDtypeStruct(r.shape, F32)...]
    pallas_call x1, Pallas kernels: 61.9 us -> 59.6 us  [forward(): pl.pallas_call(kernel, out_shape=(pltpu.VMEM((NB, SEG, D_MODEL), F32), pl...]
where the time goes in v6:
time: 62.8 us; the launch traced here: 62.7 us
  Pallas kernels  62 us (99%)
  between operations  0.64 us (1%)
    pallas_call x1, Pallas kernels, forward(): pl.pallas_call(kernel, out_shape=(pltpu.VMEM((NB, SEG, D_MODEL), F32), pl...  59.6 us
    pallas_call x1, Pallas kernels, forward(): pl.pallas_call(copy_kernel, out_shape=(jax.ShapeDtypeStruct(r.shape, F32)...  2.39 us

profile of v6, /device:TPU:11, one launch (start us, length us, event | category | flops | bytes accessed | tf_op | source)
XLA Modules:
  0.0 62.7 jit_solution(17774167865108663293)
XLA Ops:
  0.6 59.6 %shard_map.121 = (f32[4,64,1536]{2,1,0:T(8,128)S(1)}, f32[4,2,12,64,128]{4,3,2,1,0:T(8,128)S(1)}, bf16[2,4,16,3328]{3,2,1,0:T(8,128)(2,1)S(1)}) custom-call(f32[4,64,1536]{2,1,0:T(8,128)} %resid_hbm.1, f32[2,1536]{1,0:T(2,128)} %pre_hbm.1, bf16[2,6448,1536]{2,1,0:T(8,128)(2,1)} %bitcast.3, f32[2,4,3328]{2,1,0:T(4,128)} %bitcast.4, f32[2,3328]{1,0:T(2,128)} %cb_hbm.1, ...), custom_call_target="tpu_custom_call" | custom-call | tf_op jit(solution)/shard_map/pallas_call | solution.py:632
  60.3 2.4 %shard_map.122 = (f32[4,64,1536]{2,1,0:T(8,128)}, f32[4,2,12,64,128]{4,3,2,1,0:T(8,128)}, bf16[4,3,2,3328]{3,2,1,0:T(2,128)(2,1)}) custom-call(f32[4,64,1536]{2,1,0:T(8,128)S(1)} %get-tuple-element.9.r_ref, f32[4,2,12,64,128]{4,3,2,1,0:T(8,128)S(1)} %get-tuple-element.10.ssm_ref, bf16[2,4,16,3328]{3,2,1,0:T(8,128)(2,1)S(1)} %get-tuple-element.11.tail_ref), custom_call_target="tpu_custom_call" | custom-call | tf_op jit(solution)/shard_map/pallas_call | solution.py:692

commit v7 on v6

--- a/solution.py
+++ b/solution.py
@@ -25,7 +25,7 @@
 LOC = 1536
 ACT = LOC + 256
 PAIRS = 12
-VMEM_LIMIT = 57200000
+VMEM_LIMIT = 58400000
 NT = (((1,), (1,)), ((), ()))
 
 
@@ -52,8 +52,8 @@
 
 def kernel(resid_hbm, pre_hbm, w_in_ref, cw_hbm, cb_hbm, dtb_hbm, alog_hbm, dskip_hbm, gw_hbm, w_out_ref,
            r_hbm, ssm_out, tail_out,
-           r_out, pre_ref, cw_ref, cb_ref, dtb_ref, alog_ref, dskip_ref, gw_ref, hbuf, sz, wz, wx, wbc, wout, rawa, rawb, states, bt_o, bt_r, act_o, act_r, yloc, ybuf, yrecv, gn, stg, tails, tail_o, tail_r,
-           cum_o, cumt_o, cumt_r, dtt_o, dtt_r, cwl, prm,
+           r_out, pre_ref, cw_ref, cb_ref, dtb_ref, alog_ref, dskip_ref, gw_ref, hbuf, sz, wz, wx, wbc, wout, rawa, rawb, spread, scaled, act_o, act_r, yloc, ybuf, yrecv, gn, stg, tails, tail_o, tail_r,
+           cum_o, cum_r, dt_o, dt_r, cumt_o, dtt_o, cwl, prm,
            wsem, hsend, hrecv, ysend, yrecv_sem, tsend, trecv, osem, psem, rsem, tout):
     me = lax.axis_index('sp')
     chip = me // 2
@@ -92,6 +92,12 @@
     prm[...] = jnp.zeros((8, 128), F32)
     for c in bc0 + xc0:
         c.start()
+    rows_i = lax.broadcasted_iota(jnp.int32, (BLK, 64), 0)
+    for i in range(24):
+        h = head_row(i)
+        hit = (rows_i == h) | (rows_i == h + 40) | (rows_i == h + 80)
+        spread[:, 64 * i:64 * (i + 1)] = jnp.where(hit, 1.0, 0.0).astype(BF16)
+
     with jax.named_scope('params'):
         for c in params[:2]:
             c.wait()
@@ -152,9 +158,6 @@
 
     def out_prompt(l, p):
         return pltpu.make_async_copy(stg.at[p], ssm_out.at[p, l], osem.at[p])
-
-    def out_heads(l, n):
-        return pltpu.make_async_copy(stg.at[:, pl.ds(4 * n, 4)], ssm_out.at[:, l, pl.ds(4 * n, 4)], osem.at[n])
 
     def r_copy(n):
         cols = pl.ds(pl.multiple_of(512 * n, 512), 512)
@@ -178,7 +181,7 @@
                 acc = acc + cwl[k:k + 1, cols] * src[first + g, i, 13 + k:141 + k, :]
             act[p, :, cols] = silu(acc + cwl[4:5, cols]).astype(BF16)
 
-    def block(l, p0, np_, row, act, tail, cumt, dtt, cum, with_c, width):
+    def block(l, p0, np_, row, act, tail, cum, dts, trans, with_c, widths):
         def project(w, rows, dst):
             lhs = hbuf[pl.ds(NB * l + p0, np_), pl.ds(row, EXT), :].reshape(np_ * EXT, D_MODEL)
             res = round_bf16(dot_nt(lhs, w[rows, :]))
@@ -198,10 +201,11 @@
                 dt = dt * (1.0 - core_f) + pltpu.roll(dt, 116, 1) * core_f
                 logs = logs * (1.0 - core_f) + pltpu.roll(logs, 116, 1) * core_f
                 cums = jnp.dot(tri, logs, precision=lax.Precision.HIGHEST, preferred_element_type=F32)
-                cumt[p] = cums.T[0:40]
-                dtt[p] = dt.T[0:40]
-                if cum is not None:
-                    cum[p] = cums
+                cum[p] = cums
+                dts[p] = dt
+                if trans is not None:
+                    trans[0][p] = cums.T[0:40]
+                    trans[1][p] = dt.T[0:40]
 
         def finish_x(src, col, n):
             for i in range(np_):
@@ -212,11 +216,12 @@
 
         project(wbc, slice(0, 384 if with_c else 256), rawa)
         pending, nxt = (lambda: finish_bc(rawa)), rawb
-        for col in range(0, width, 512):
-            n = min(512, width - col)
+        col = 0
+        for n in widths:
             project(wx, slice(col, col + n), nxt)
             pending()
             pending = functools.partial(finish_x, nxt, col, n)
+            col += n
             nxt = rawa if nxt is rawb else rawb
         pending()
 
@@ -233,12 +238,18 @@
     def split_pair(xp):
         return [jnp.where(low, xp, zero), jnp.where(low, zero, xp)]
 
-    def decays(p, h, cumt, dtt, extra):
-        row = cumt[p, pl.ds(h, 1), :]
-        return dtt[p, pl.ds(h, 1), :] * jnp.exp(row[:, 127:128] - row + extra)
+    lane = lax.broadcasted_iota(jnp.int32, (BLK, BLK), 1)
+
+    def three_terms(v):
+        v = jnp.where(lane < 40, v, 0.0)
+        hi = round_bf16(v)
+        mid = round_bf16(v - hi)
+        return (hi + pltpu.roll(mid, 40, 1) + pltpu.roll((v - hi) - mid, 80, 1)).astype(BF16)
+
+    def weighted(act, p, cols, terms):
+        return (act[p, :, cols].astype(F32) * dot(terms, spread[:, cols])).astype(BF16)
 
     def intra_body(l, p):
-        bt_o[p] = act_o[p, :, LOC:LOC + 128].astype(F32).T
         cb = act_o[p, :, LOC + 128:ACT]
         scores = dot_nt(cb, act_o[p, :, LOC:LOC + 128]) * tri
         for j in range(PAIRS):
@@ -254,36 +265,54 @@
             yloc[p, :, 128 * j:128 * (j + 1)] = y
             ybuf[p, :, 128 * j:128 * (j + 1)] = y.astype(BF16)
 
-    def inter_body(l, p):
-        bt = act_r[p, :, LOC:LOC + 128].astype(F32).T
-        bt_r[p] = bt
-        cf = act_o[p, :, LOC + 128:ACT]
-        for j in range(PAIRS):
-            lhs = jnp.concatenate([(bt * decays(p, h, cumt_r, dtt_r, 0.0)).astype(BF16) for h in (head_row(2 * j), head_row(2 * j + 1))], axis=1)
-            states[:, 128 * j:128 * (j + 1)] = dot(lhs, jnp.concatenate(split_pair(act_r[p, :, 128 * j:128 * (j + 1)]), axis=0))
-        for jj in range(PAIRS // 2):
-            o = dot(cf, states[:, 256 * jj:256 * (jj + 1)].astype(BF16))
-            for s in range(2):
-                j = 2 * jj + s
-                ha, hb = head_row(2 * j), head_row(2 * j + 1)
-                ca = jnp.broadcast_to(cum_o[p, :, ha:ha + 1], (BLK, BLK))
-                cb = jnp.broadcast_to(cum_o[p, :, hb:hb + 1], (BLK, BLK))
-                y = yloc[p, :, 128 * j:128 * (j + 1)] + o[:, 128 * s:128 * (s + 1)] * jnp.exp(jnp.where(low, ca, cb))
-                ybuf[p, :, 128 * j:128 * (j + 1)] = y.astype(BF16)
-        y_copy(l, p).start()
-
-    def final_pair(p, q):
-        h = 24 * chip + 2 * q
-        cols = pl.ds(pl.multiple_of(128 * (6 * chip + q), 128), 128)
-        left, right = [], []
-        for hh in (h, h + 1):
-            end_o = cumt_o[p, pl.ds(hh, 1), :][:, 127:128]
-            end_r = cumt_r[p, pl.ds(hh, 1), :][:, 127:128]
-            left.append((bt_o[p] * decays(p, hh, cumt_o, dtt_o, end_r * (1.0 - chip_f))).astype(BF16))
-            right.append((bt_r[p] * decays(p, hh, cumt_r, dtt_r, end_o * chip_f)).astype(BF16))
-        rhs = jnp.concatenate(split_pair(act_o[p, :, cols]) + split_pair(act_r[p, :, cols]), axis=0)
-        state = dot(jnp.concatenate(left + right, axis=1), rhs)
-        stg[p, pl.ds(2 * q, 2)] = state.T.reshape(2, 64, 128)
+    def inter_half(l, half):
+        prompts = [(0, 2 * half, rawa), (1, 2 * half + 1, rawb)]
+        bts, ends = [], []
+        for i, p, _ in prompts:
+            cum = cum_r[p]
+            bts.append(act_r[p, :, LOC:LOC + 128].astype(F32).T.astype(BF16))
+            ends.append(three_terms(dt_r[p] * jnp.exp(cum[127:128, :] - cum)))
+        for i, p, _ in prompts:
+            for j in range(6):
+                cols = slice(256 * j, 256 * (j + 1))
+                scaled[i, :, cols] = weighted(act_r, p, cols, ends[i])
+        for i, p, states in prompts:
+            for j in range(6):
+                state = dot(bts[i], scaled[i, :, 256 * j:256 * (j + 1)])
+                for k in range(2):
+                    states[(2 * j + k) // 4, (2 * j + k) % 4, 0:BLK, :] = state[:, 128 * k:128 * (k + 1)]
+        for i, p, states in prompts:
+            cf = act_o[p, :, LOC + 128:ACT]
+            start = three_terms(jnp.exp(cum_o[p]))
+            for j in range(6):
+                cols = slice(256 * j, 256 * (j + 1))
+                state = jnp.concatenate([states[(2 * j + k) // 4, (2 * j + k) % 4, 0:BLK, :].astype(BF16) for k in range(2)], axis=1)
+                y = yloc[p, :, cols] + dot(cf, state) * dot(start, spread[:, cols])
+                ybuf[p, :, cols] = y.astype(BF16)
+        for i, p, _ in prompts:
+            y_copy(l, p).start()
+
+    def final_inputs(p):
+        co, cr = cum_o[p], cum_r[p]
+        eo, er = co[127:128, :], cr[127:128, :]
+        fo = three_terms(dt_o[p] * jnp.exp(eo - co + er * (1.0 - chip_f)))
+        fr = three_terms(dt_r[p] * jnp.exp(er - cr + eo * chip_f))
+        for j in range(3):
+            cols = pl.ds(pl.multiple_of(HALF * chip + 256 * j, 256), 256)
+            ybuf[p, :, 256 * j:256 * (j + 1)] = weighted(act_o, p, cols, fo)
+            ybuf[p, :, HALF + 256 * j:HALF + 256 * (j + 1)] = weighted(act_r, p, cols, fr)
+
+    def final_states(p):
+        bts = jnp.concatenate([act[p, :, LOC:LOC + 128].astype(F32).T.astype(BF16) for act in (act_o, act_r)], axis=1)
+        for j in range(3):
+            state = dot(bts, jnp.concatenate([ybuf[p, :, 256 * j:256 * (j + 1)], ybuf[p, :, HALF + 256 * j:HALF + 256 * (j + 1)]], axis=0))
+            stg[p, 4 * j:4 * j + 4] = state.T.reshape(4, 64, 128)
+
+    def wait_states(l):
+        @pl.when(l > 0)
+        def _():
+            for p in range(NB):
+                out_prompt(0, p).wait()
 
     def pass_tail(l):
         c_tail(l).wait_recv()
@@ -397,7 +426,7 @@
             def _():
                 f_tail(l).wait_recv()
         with jax.named_scope('own_block'):
-            block(l, 0, NB, own_blk, act_o, tail_o, cumt_o, dtt_o, cum_o, True, LOC)
+            block(l, 0, NB, own_blk, act_o, tail_o, cum_o, dt_o, (cumt_o, dtt_o), True, (512, 512, 256, 256))
 
         def intra_end(p):
             @pl.when(chip == 0)
@@ -435,14 +464,14 @@
 
             def half_body(half, c):
                 with jax.named_scope('oth_block'):
-                    block(l, 2 * half, 2, oth_blk, act_r, None, cumt_r, dtt_r, None, False, LOC)
+                    block(l, 2 * half, 2, oth_blk, act_r, None, cum_r, dt_r, None, False, (512, 512, 256, 256))
 
                 @pl.when(half == 0)
                 def _():
                     with jax.named_scope('wait_c1'):
                         pass_half(l, 1)
                 with jax.named_scope('inter'):
-                    lax.fori_loop(2 * half, 2 * half + 2, lambda p, c: (inter_body(l, p), c)[1], 0)
+                    inter_half(l, half)
 
                 @pl.when(half == 0)
                 def _():
@@ -476,41 +505,37 @@
             oc.wait()
 
         def out_chunk(n):
-            cols = pl.ds(pl.multiple_of(512 * n, 512), 512)
+            cols = slice(512 * n, 512 * (n + 1))
             o = dot(gn[...].reshape(NB * SEG, D_INNER), wout[:, cols])
             r_out[:, :, cols] = r_out[:, :, cols] + o.reshape(NB, SEG, 512)
 
-        def send_r(n):
-            @pl.when(l == LAYERS - 1)
-            def _():
-                r_copy(n).start()
-
-        def out_final(n, c):
-            out_chunk(n)
-            for q in range(2):
-                for p in range(NB):
-                    final_pair(p, 2 * n + q)
-            out_heads(l, n).start()
-            send_r(n)
-            return c
-
-        def out_plain(n, c):
-            out_chunk(n)
-            send_r(n)
-            return c
-
         with jax.named_scope('outproj'):
             @pl.when(chip == 0)
             def _():
-                lax.fori_loop(0, 3, out_plain, 0)
+                for n in range(3):
+                    out_chunk(n)
 
             @pl.when(chip == 1)
             def _():
-                @pl.when(l > 0)
-                def _():
-                    for n in range(3):
-                        out_heads(0, n).wait()
-                lax.fori_loop(0, 3, out_final, 0)
+                wait_states(l)
+                final_inputs(0)
+                final_inputs(1)
+                out_chunk(0)
+                final_states(0)
+                final_states(1)
+                final_inputs(2)
+                final_inputs(3)
+                out_chunk(1)
+                final_states(2)
+                final_states(3)
+                out_chunk(2)
+                for p in range(NB):
+                    out_prompt(l, p).start()
+
+            @pl.when(l == LAYERS - 1)
+            def _():
+                for n in range(3):
+                    r_copy(n).start()
 
         @pl.when(chip == 0)
         def _():
@@ -526,10 +551,7 @@
             def _():
                 f_tail(l).wait_recv()
 
-            @pl.when(l > 0)
-            def _():
-                for p in range(NB):
-                    out_prompt(0, p).wait()
+            wait_states(l)
         with jax.named_scope('last_rows'):
             last_rows(l, tail_r)
             after_other(l, tail_r)
@@ -538,25 +560,28 @@
             with jax.named_scope('wait_dh'):
                 wait_half(l, half)
             with jax.named_scope('oth_block'):
-                block(l, 2 * half, 2, oth_blk, act_r, None, cumt_r, dtt_r, None, False, HALF)
-
-            @pl.when(half == 0)
+                block(l, 2 * half, 2, oth_blk, act_r, None, cum_r, dt_r, None, False, (512, 256))
+
+            @pl.when(jnp.logical_and(half == 0, l == 0))
+            def _():
+                pass_half(l, 1)
+
+            @pl.when(half == 1)
+            def _():
+                next_weights(l)
+
+            with jax.named_scope('final'):
+                for i in range(2):
+                    final_inputs(2 * half + i)
+                for i in range(2):
+                    final_states(2 * half + i)
+                for i in range(2):
+                    out_prompt(l, 2 * half + i).start()
+
+            @pl.when(jnp.logical_and(half == 0, l > 0))
             def _():
                 with jax.named_scope('wait_c1'):
                     pass_half(l, 1)
-
-            @pl.when(half == 1)
-            def _():
-                next_weights(l)
-
-            def final_body(p, cc):
-                bt_r[p] = act_r[p, :, LOC:LOC + 128].astype(F32).T
-                for q in range(6):
-                    final_pair(p, q)
-                out_prompt(l, p).start()
-                return cc
-            with jax.named_scope('final'):
-                lax.fori_loop(2 * half, 2 * half + 2, final_body, 0)
             return c
         lax.fori_loop(0, 2, half_body, 0)
 
@@ -594,15 +619,8 @@
         by_core(sent)
         tail_copy(l).wait()
 
-    @pl.when(chip == 0)
-    def _():
-        for p in range(NB):
-            out_prompt(LAYERS - 1, p).wait()
-
-    @pl.when(chip == 1)
-    def _():
-        for n in range(3):
-            out_heads(LAYERS - 1, n).wait()
+    for p in range(NB):
+        out_prompt(LAYERS - 1, p).wait()
     for n in range(3):
         r_copy(n).wait()
 
@@ -655,9 +673,8 @@
                 pltpu.VMEM((D_INNER, D_MODEL), BF16),
                 pltpu.VMEM((4, NB, EXT, 128), F32),
                 pltpu.VMEM((4, NB, EXT, 128), F32),
-                pltpu.VMEM((BLK, LOC), F32),
-                pltpu.VMEM((NB, BLK, BLK), F32),
-                pltpu.VMEM((NB, BLK, BLK), F32),
+                pltpu.VMEM((BLK, LOC), BF16),
+                pltpu.VMEM((2, BLK, LOC), BF16),
                 pltpu.VMEM((NB, BLK, ACT), BF16),
                 pltpu.VMEM((NB, BLK, ACT), BF16),
                 pltpu.VMEM((NB, BLK, LOC), F32),
@@ -669,8 +686,9 @@
                 pltpu.VMEM((NB, 16, ACT), BF16),
                 pltpu.VMEM((NB, 16, ACT), BF16),
                 pltpu.VMEM((NB, BLK, BLK), F32),
-                pltpu.VMEM((NB, 40, BLK), F32),
-                pltpu.VMEM((NB, 40, BLK), F32),
+                pltpu.VMEM((NB, BLK, BLK), F32),
+                pltpu.VMEM((NB, BLK, BLK), F32),
+                pltpu.VMEM((NB, BLK, BLK), F32),
                 pltpu.VMEM((NB, 40, BLK), F32),
                 pltpu.VMEM((NB, 40, BLK), F32),
                 pltpu.VMEM((8, ACT), F32),

time: 62.8 us -> 63.3 us (level)
  no operation moved by 1% of the time
where the time goes in v7:
time: 63.3 us; the launch traced here: 63 us
  Pallas kernels  62.3 us (98%)
  between operations  0.64 us (1%)
    pallas_call x1, Pallas kernels, forward(): pl.pallas_call(kernel, out_shape=(pltpu.VMEM((NB, SEG, D_MODEL), F32), pl...  59.9 us
    pallas_call x1, Pallas kernels, forward(): pl.pallas_call(copy_kernel, out_shape=(jax.ShapeDtypeStruct(r.shape, F32)...  2.39 us

profile of v7, /device:TPU:11, one launch (start us, length us, event | category | flops | bytes accessed | tf_op | source)
XLA Modules:
  0.0 63.0 jit_solution(422685937085476018)
XLA Ops:
  0.6 59.9 %shard_map.121 = (f32[4,64,1536]{2,1,0:T(8,128)S(1)}, f32[4,2,12,64,128]{4,3,2,1,0:T(8,128)S(1)}, bf16[2,4,16,3328]{3,2,1,0:T(8,128)(2,1)S(1)}) custom-call(f32[4,64,1536]{2,1,0:T(8,128)} %resid_hbm.1, f32[2,1536]{1,0:T(2,128)} %pre_hbm.1, bf16[2,6448,1536]{2,1,0:T(8,128)(2,1)} %bitcast.3, f32[2,4,3328]{2,1,0:T(4,128)} %bitcast.4, f32[2,3328]{1,0:T(2,128)} %cb_hbm.1, ...), custom_call_target="tpu_custom_call" | custom-call | tf_op jit(solution)/shard_map/pallas_call | solution.py:650
  60.6 2.4 %shard_map.122 = (f32[4,64,1536]{2,1,0:T(8,128)}, f32[4,2,12,64,128]{4,3,2,1,0:T(8,128)}, bf16[4,3,2,3328]{3,2,1,0:T(2,128)(2,1)}) custom-call(f32[4,64,1536]{2,1,0:T(8,128)S(1)} %get-tuple-element.9.r_ref, f32[4,2,12,64,128]{4,3,2,1,0:T(8,128)S(1)} %get-tuple-element.10.ssm_ref, bf16[2,4,16,3328]{3,2,1,0:T(8,128)(2,1)S(1)} %get-tuple-element.11.tail_ref), custom_call_target="tpu_custom_call" | custom-call | tf_op jit(solution)/shard_map/pallas_call | solution.py:710

commit v8 on v7

--- a/solution.py
+++ b/solution.py
@@ -51,10 +51,10 @@
 
 
 def kernel(resid_hbm, pre_hbm, w_in_ref, cw_hbm, cb_hbm, dtb_hbm, alog_hbm, dskip_hbm, gw_hbm, w_out_ref,
-           r_hbm, ssm_out, tail_out,
-           r_out, pre_ref, cw_ref, cb_ref, dtb_ref, alog_ref, dskip_ref, gw_ref, hbuf, sz, wz, wx, wbc, wout, rawa, rawb, spread, scaled, act_o, act_r, yloc, ybuf, yrecv, gn, stg, tails, tail_o, tail_r,
+           r_out, ssm_out, tail_out,
+           pre_ref, cw_ref, cb_ref, dtb_ref, alog_ref, dskip_ref, gw_ref, hbuf, sz, wz, wx, wbc, wout, rawa, rawb, spread, scaled, act_o, act_r, yloc, ybuf, yrecv, gn, tails, tail_o, tail_r,
            cum_o, cum_r, dt_o, dt_r, cumt_o, dtt_o, cwl, prm,
-           wsem, hsend, hrecv, ysend, yrecv_sem, tsend, trecv, osem, psem, rsem, tout):
+           wsem, hsend, hrecv, ysend, yrecv_sem, tsend, trecv, psem, tout):
     me = lax.axis_index('sp')
     chip = me // 2
     core = me % 2
@@ -155,13 +155,6 @@
     def y_copy(l, p):
         src = ybuf.at[p, pl.ds(pl.multiple_of(SEG * (1 - core), 16), SEG), :]
         return remote(src, yrecv.at[NB * l + p], ysend.at[l, p], yrecv_sem.at[l, p], partner)
-
-    def out_prompt(l, p):
-        return pltpu.make_async_copy(stg.at[p], ssm_out.at[p, l], osem.at[p])
-
-    def r_copy(n):
-        cols = pl.ds(pl.multiple_of(512 * n, 512), 512)
-        return pltpu.make_async_copy(r_out.at[:, :, cols], r_hbm.at[:, :, cols], rsem.at[n])
 
     def tail_copy(l):
         return pltpu.make_async_copy(tails.at[l], tail_out.at[l], tout.at[l])
@@ -289,7 +282,6 @@
                 state = jnp.concatenate([states[(2 * j + k) // 4, (2 * j + k) % 4, 0:BLK, :].astype(BF16) for k in range(2)], axis=1)
                 y = yloc[p, :, cols] + dot(cf, state) * dot(start, spread[:, cols])
                 ybuf[p, :, cols] = y.astype(BF16)
-        for i, p, _ in prompts:
             y_copy(l, p).start()
 
     def final_inputs(p):
@@ -302,17 +294,11 @@
             ybuf[p, :, 256 * j:256 * (j + 1)] = weighted(act_o, p, cols, fo)
             ybuf[p, :, HALF + 256 * j:HALF + 256 * (j + 1)] = weighted(act_r, p, cols, fr)
 
-    def final_states(p):
+    def final_states(l, p):
         bts = jnp.concatenate([act[p, :, LOC:LOC + 128].astype(F32).T.astype(BF16) for act in (act_o, act_r)], axis=1)
         for j in range(3):
             state = dot(bts, jnp.concatenate([ybuf[p, :, 256 * j:256 * (j + 1)], ybuf[p, :, HALF + 256 * j:HALF + 256 * (j + 1)]], axis=0))
-            stg[p, 4 * j:4 * j + 4] = state.T.reshape(4, 64, 128)
-
-    def wait_states(l):
-        @pl.when(l > 0)
-        def _():
-            for p in range(NB):
-                out_prompt(0, p).wait()
+            ssm_out[p, l, 4 * j:4 * j + 4] = state.T.reshape(4, 64, 128)
 
     def pass_tail(l):
         c_tail(l).wait_recv()
@@ -464,7 +450,7 @@
 
             def half_body(half, c):
                 with jax.named_scope('oth_block'):
-                    block(l, 2 * half, 2, oth_blk, act_r, None, cum_r, dt_r, None, False, (512, 512, 256, 256))
+                    block(l, 2 * half, 2, oth_blk, act_r, None, cum_r, dt_r, None, False, (512, 512, 512))
 
                 @pl.when(half == 0)
                 def _():
@@ -517,25 +503,17 @@
 
             @pl.when(chip == 1)
             def _():
-                wait_states(l)
                 final_inputs(0)
                 final_inputs(1)
                 out_chunk(0)
-                final_states(0)
-                final_states(1)
+                final_states(l, 0)
+                final_states(l, 1)
                 final_inputs(2)
                 final_inputs(3)
                 out_chunk(1)
-                final_states(2)
-                final_states(3)
+                final_states(l, 2)
+                final_states(l, 3)
                 out_chunk(2)
-                for p in range(NB):
-                    out_prompt(l, p).start()
-
-            @pl.when(l == LAYERS - 1)
-            def _():
-                for n in range(3):
-                    r_copy(n).start()
 
         @pl.when(chip == 0)
         def _():
@@ -551,7 +529,6 @@
             def _():
                 f_tail(l).wait_recv()
 
-            wait_states(l)
         with jax.named_scope('last_rows'):
             last_rows(l, tail_r)
             after_other(l, tail_r)
@@ -574,9 +551,7 @@
                 for i in range(2):
                     final_inputs(2 * half + i)
                 for i in range(2):
-                    final_states(2 * half + i)
-                for i in range(2):
-                    out_prompt(l, 2 * half + i).start()
+                    final_states(l, 2 * half + i)
 
             @pl.when(jnp.logical_and(half == 0, l > 0))
             def _():
@@ -618,11 +593,6 @@
                 f_half(l, half, n).wait_send()
         by_core(sent)
         tail_copy(l).wait()
-
-    for p in range(NB):
-        out_prompt(LAYERS - 1, p).wait()
-    for n in range(3):
-        r_copy(n).wait()
 
 
 def copy_kernel(r_ref, ssm_ref, tail_ref, r_out, ssm_out, conv_out, tbuf, cbuf, sems):
@@ -645,6 +615,7 @@
 
 def solution(mesh):
     hbm = pl.BlockSpec(memory_space=pl.ANY)
+    vmem = pl.BlockSpec(memory_space=pltpu.VMEM)
 
     def forward(resid, pre_norm, w_in, conv_w, conv_b, dt_bias, a_log, d_skip, gate_norm, w_out):
         r, ssm, tails = pl.pallas_call(
@@ -655,9 +626,8 @@
                 pltpu.VMEM((LAYERS, NB, 16, CONV_DIM), BF16),
             ),
             in_specs=[hbm] * 10,
-            out_specs=(hbm, hbm, hbm),
+            out_specs=(vmem, vmem, hbm),
             scratch_shapes=[
-                pltpu.VMEM((NB, SEG, D_MODEL), F32),
                 pltpu.VMEM((LAYERS, D_MODEL), F32),
                 pltpu.VMEM((LAYERS, 4, CONV_DIM), F32),
                 pltpu.VMEM((LAYERS, CONV_DIM), F32),
@@ -681,7 +651,6 @@
                 pltpu.VMEM((NB, BLK, LOC), BF16),
                 pltpu.VMEM((LAYERS * NB, SEG, LOC), BF16),
                 pltpu.VMEM((NB, SEG, D_INNER), BF16),
-                pltpu.VMEM((NB, 12, 64, 128), F32),
                 pltpu.VMEM((LAYERS, NB, 16, CONV_DIM), BF16),
                 pltpu.VMEM((NB, 16, ACT), BF16),
                 pltpu.VMEM((NB, 16, ACT), BF16),
@@ -700,9 +669,7 @@
                 pltpu.SemaphoreType.DMA((LAYERS, NB)),
                 pltpu.SemaphoreType.DMA((LAYERS, 2)),
                 pltpu.SemaphoreType.DMA((LAYERS, 2)),
-                pltpu.SemaphoreType.DMA((NB,)),
                 pltpu.SemaphoreType.DMA((8,)),
-                pltpu.SemaphoreType.DMA((3,)),
                 pltpu.SemaphoreType.DMA((LAYERS,)),
             ],
             compiler_params=pltpu.CompilerParams(collective_id=0, has_side_effects=True, vmem_limit_bytes=VMEM_LIMIT),

time: 63.3 us -> 61.6 us (0.973)
  Pallas kernels: 62.3 us -> 60.6 us
    pallas_call x1, Pallas kernels: 59.9 us -> 58.2 us  [forward(): pl.pallas_call(kernel, out_shape=(pltpu.VMEM((NB, SEG, D_MODEL), F32), pl...]
where the time goes in v8:
time: 61.6 us; the launch traced here: 61.3 us
  Pallas kernels  60.6 us (98%)
  between operations  0.64 us (1%)
    pallas_call x1, Pallas kernels, forward(): pl.pallas_call(kernel, out_shape=(pltpu.VMEM((NB, SEG, D_MODEL), F32), pl...  58.2 us
    pallas_call x1, Pallas kernels, forward(): pl.pallas_call(copy_kernel, out_shape=(jax.ShapeDtypeStruct(r.shape, F32)...  2.39 us

profile of v8, /device:TPU:11, one launch (start us, length us, event | category | flops | bytes accessed | tf_op | source)
XLA Modules:
  0.0 61.3 jit_solution(2899763770784741708)
XLA Ops:
  0.6 58.2 %shard_map.121 = (f32[4,64,1536]{2,1,0:T(8,128)S(1)}, f32[4,2,12,64,128]{4,3,2,1,0:T(8,128)S(1)}, bf16[2,4,16,3328]{3,2,1,0:T(8,128)(2,1)S(1)}) custom-call(f32[4,64,1536]{2,1,0:T(8,128)} %resid_hbm.1, f32[2,1536]{1,0:T(2,128)} %pre_hbm.1, bf16[2,6448,1536]{2,1,0:T(8,128)(2,1)} %bitcast.3, f32[2,4,3328]{2,1,0:T(4,128)} %bitcast.4, f32[2,3328]{1,0:T(2,128)} %cb_hbm.1, ...), custom_call_target="tpu_custom_call" | custom-call | tf_op jit(solution)/shard_map/pallas_call | solution.py:621
  58.9 2.4 %shard_map.122 = (f32[4,64,1536]{2,1,0:T(8,128)}, f32[4,2,12,64,128]{4,3,2,1,0:T(8,128)}, bf16[4,3,2,3328]{3,2,1,0:T(2,128)(2,1)}) custom-call(f32[4,64,1536]{2,1,0:T(8,128)S(1)} %get-tuple-element.9.r_ref, f32[4,2,12,64,128]{4,3,2,1,0:T(8,128)S(1)} %get-tuple-element.10.ssm_ref, bf16[2,4,16,3328]{3,2,1,0:T(8,128)(2,1)S(1)} %get-tuple-element.11.tail_ref), custom_call_target="tpu_custom_call" | custom-call | tf_op jit(solution)/shard_map/pallas_call | solution.py:677

commit v9 on v8

--- a/solution.py
+++ b/solution.py
@@ -284,20 +284,20 @@
                 ybuf[p, :, cols] = y.astype(BF16)
             y_copy(l, p).start()
 
-    def final_inputs(p):
+    def final_inputs(p, buf):
         co, cr = cum_o[p], cum_r[p]
         eo, er = co[127:128, :], cr[127:128, :]
         fo = three_terms(dt_o[p] * jnp.exp(eo - co + er * (1.0 - chip_f)))
         fr = three_terms(dt_r[p] * jnp.exp(er - cr + eo * chip_f))
         for j in range(3):
             cols = pl.ds(pl.multiple_of(HALF * chip + 256 * j, 256), 256)
-            ybuf[p, :, 256 * j:256 * (j + 1)] = weighted(act_o, p, cols, fo)
-            ybuf[p, :, HALF + 256 * j:HALF + 256 * (j + 1)] = weighted(act_r, p, cols, fr)
-
-    def final_states(l, p):
+            buf[:, 256 * j:256 * (j + 1)] = weighted(act_o, p, cols, fo)
+            buf[:, HALF + 256 * j:HALF + 256 * (j + 1)] = weighted(act_r, p, cols, fr)
+
+    def final_states(l, p, buf):
         bts = jnp.concatenate([act[p, :, LOC:LOC + 128].astype(F32).T.astype(BF16) for act in (act_o, act_r)], axis=1)
         for j in range(3):
-            state = dot(bts, jnp.concatenate([ybuf[p, :, 256 * j:256 * (j + 1)], ybuf[p, :, HALF + 256 * j:HALF + 256 * (j + 1)]], axis=0))
+            state = dot(bts, jnp.concatenate([buf[:, 256 * j:256 * (j + 1)], buf[:, HALF + 256 * j:HALF + 256 * (j + 1)]], axis=0))
             ssm_out[p, l, 4 * j:4 * j + 4] = state.T.reshape(4, 64, 128)
 
     def pass_tail(l):
@@ -320,6 +320,11 @@
         tails[l, :, :, D_INNER:CONV_DIM] = tail[:, :, LOC:ACT]
         for c in tail_copies(l):
             c.start()
+
+    def finish_tails(l):
+        for c in tail_copies(l):
+            c.wait()
+        tail_copy(l).start()
 
     def next_weights(l):
         @pl.when(l == 0)
@@ -452,12 +457,24 @@
                 with jax.named_scope('oth_block'):
                     block(l, 2 * half, 2, oth_blk, act_r, None, cum_r, dt_r, None, False, (512, 512, 512))
 
-                @pl.when(half == 0)
+                @pl.when(jnp.logical_and(half == 0, jnp.logical_or(core == 1, l > 0)))
                 def _():
                     with jax.named_scope('wait_c1'):
                         pass_half(l, 1)
                 with jax.named_scope('inter'):
                     inter_half(l, half)
+
+                @pl.when(jnp.logical_and(half == 0, l == 0))
+                def _():
+                    with jax.named_scope('final0'):
+                        for i in range(2):
+                            final_inputs(i, scaled.at[i])
+                        for i in range(2):
+                            final_states(l, i, scaled.at[i])
+
+                    @pl.when(core == 0)
+                    def _():
+                        pass_half(l, 1)
 
                 @pl.when(half == 0)
                 def _():
@@ -490,6 +507,10 @@
             lax.fori_loop(0, NB, gate_body, 0)
             oc.wait()
 
+            @pl.when(chip == 1)
+            def _():
+                finish_tails(l)
+
         def out_chunk(n):
             cols = slice(512 * n, 512 * (n + 1))
             o = dot(gn[...].reshape(NB * SEG, D_INNER), wout[:, cols])
@@ -503,17 +524,29 @@
 
             @pl.when(chip == 1)
             def _():
-                final_inputs(0)
-                final_inputs(1)
-                out_chunk(0)
-                final_states(l, 0)
-                final_states(l, 1)
-                final_inputs(2)
-                final_inputs(3)
-                out_chunk(1)
-                final_states(l, 2)
-                final_states(l, 3)
-                out_chunk(2)
+                @pl.when(l == 0)
+                def _():
+                    final_inputs(2, ybuf.at[2])
+                    final_inputs(3, ybuf.at[3])
+                    out_chunk(0)
+                    final_states(l, 2, ybuf.at[2])
+                    final_states(l, 3, ybuf.at[3])
+                    out_chunk(1)
+                    out_chunk(2)
+
+                @pl.when(l > 0)
+                def _():
+                    final_inputs(0, ybuf.at[0])
+                    final_inputs(1, ybuf.at[1])
+                    out_chunk(0)
+                    final_states(l, 0, ybuf.at[0])
+                    final_states(l, 1, ybuf.at[1])
+                    final_inputs(2, ybuf.at[2])
+                    final_inputs(3, ybuf.at[3])
+                    out_chunk(1)
+                    final_states(l, 2, ybuf.at[2])
+                    final_states(l, 3, ybuf.at[3])
+                    out_chunk(2)
 
         @pl.when(chip == 0)
         def _():
@@ -546,12 +579,13 @@
             @pl.when(half == 1)
             def _():
                 next_weights(l)
+                finish_tails(l)
 
             with jax.named_scope('final'):
                 for i in range(2):
-                    final_inputs(2 * half + i)
+                    final_inputs(2 * half + i, ybuf.at[2 * half + i])
                 for i in range(2):
-                    final_states(l, 2 * half + i)
+                    final_states(l, 2 * half + i, ybuf.at[2 * half + i])
 
             @pl.when(jnp.logical_and(half == 0, l > 0))
             def _():
@@ -575,10 +609,6 @@
         return carry
 
     lax.fori_loop(0, LAYERS + 1, step, 0)
-    for l in range(LAYERS):
-        for c in tail_copies(l):
-            c.wait()
-        tail_copy(l).start()
     for l in range(LAYERS):
         c_par(l).wait_send()
 
@@ -595,19 +625,16 @@
         tail_copy(l).wait()
 
 
-def copy_kernel(r_ref, ssm_ref, tail_ref, r_out, ssm_out, conv_out, tbuf, cbuf, sems):
+def copy_kernel(r_ref, ssm_ref, tail_ref, r_out, ssm_out, conv_out, cbuf, sems):
     whole = [pltpu.make_async_copy(r_ref, r_out, sems.at[0]), pltpu.make_async_copy(ssm_ref, ssm_out, sems.at[1])]
-    load = pltpu.make_async_copy(tail_ref, tbuf, sems.at[2])
-    load.start()
     for c in whole:
         c.start()
-    load.wait()
     for p in range(NB):
         for l in range(LAYERS):
-            rows = tbuf[l, p].astype(F32)
+            rows = tail_ref[l, p].astype(F32)
             for k in range(3):
                 cbuf[p, k, l:l + 1, :] = rows[13 + k:14 + k, :].astype(BF16)
-    store = pltpu.make_async_copy(cbuf, conv_out, sems.at[3])
+    store = pltpu.make_async_copy(cbuf, conv_out, sems.at[2])
     store.start()
     for c in whole + [store]:
         c.wait()
@@ -681,12 +708,11 @@
                 jax.ShapeDtypeStruct(ssm.shape, F32),
                 jax.ShapeDtypeStruct((NB, 3, LAYERS, CONV_DIM), BF16),
             ),
-            in_specs=[hbm] * 3,
+            in_specs=[hbm, hbm, vmem],
             out_specs=(hbm, hbm, hbm),
             scratch_shapes=[
-                pltpu.VMEM((LAYERS, NB, 16, CONV_DIM), BF16),
                 pltpu.VMEM((NB, 3, LAYERS, CONV_DIM), BF16),
-                pltpu.SemaphoreType.DMA((4,)),
+                pltpu.SemaphoreType.DMA((3,)),
             ],
             compiler_params=pltpu.CompilerParams(vmem_limit_bytes=4 * 1024 * 1024),
         )(r, ssm, tails)

time: 61.6 us -> 61.7 us (level)
  no operation moved by 1% of the time
where the time goes in v9:
time: 61.7 us; the launch traced here: 61.6 us
  Pallas kernels  60.9 us (99%)
  between operations  0.64 us (1%)
    pallas_call x1, Pallas kernels, forward(): pl.pallas_call(kernel, out_shape=(pltpu.VMEM((NB, SEG, D_MODEL), F32), pl...  58.7 us
    pallas_call x1, Pallas kernels, forward(): pl.pallas_call(copy_kernel, out_shape=(jax.ShapeDtypeStruct(r.shape, F32)...  2.25 us

profile of v9, /device:TPU:11, one launch (start us, length us, event | category | flops | bytes accessed | tf_op | source)
XLA Modules:
  0.0 61.6 jit_solution(4683999398034231512)
XLA Ops:
  0.6 58.7 %shard_map.121 = (f32[4,64,1536]{2,1,0:T(8,128)S(1)}, f32[4,2,12,64,128]{4,3,2,1,0:T(8,128)S(1)}, bf16[2,4,16,3328]{3,2,1,0:T(8,128)(2,1)S(1)}) custom-call(f32[4,64,1536]{2,1,0:T(8,128)} %resid_hbm.1, f32[2,1536]{1,0:T(2,128)} %pre_hbm.1, bf16[2,6448,1536]{2,1,0:T(8,128)(2,1)} %bitcast.3, f32[2,4,3328]{2,1,0:T(4,128)} %bitcast.4, f32[2,3328]{1,0:T(2,128)} %cb_hbm.1, ...), custom_call_target="tpu_custom_call" | custom-call | tf_op jit(solution)/shard_map/pallas_call | solution.py:648
  59.3 2.2 %shard_map.122 = (f32[4,64,1536]{2,1,0:T(8,128)}, f32[4,2,12,64,128]{4,3,2,1,0:T(8,128)}, bf16[4,3,2,3328]{3,2,1,0:T(2,128)(2,1)}) custom-call(f32[4,64,1536]{2,1,0:T(8,128)S(1)} %get-tuple-element.9.r_ref, f32[4,2,12,64,128]{4,3,2,1,0:T(8,128)S(1)} %get-tuple-element.10.ssm_ref, bf16[2,4,16,3328]{3,2,1,0:T(8,128)(2,1)S(1)} %get-tuple-element.11.tail_ref), custom_call_target="tpu_custom_call" | custom-call | tf_op jit(solution)/shard_map/pallas_call | solution.py:704

commit v10 on v9

--- a/solution.py
+++ b/solution.py
@@ -282,6 +282,7 @@
                 state = jnp.concatenate([states[(2 * j + k) // 4, (2 * j + k) % 4, 0:BLK, :].astype(BF16) for k in range(2)], axis=1)
                 y = yloc[p, :, cols] + dot(cf, state) * dot(start, spread[:, cols])
                 ybuf[p, :, cols] = y.astype(BF16)
+        for i, p, _ in prompts:
             y_copy(l, p).start()
 
     def final_inputs(p, buf):

time: 61.7 us -> 61.7 us (level)
  no operation moved by 1% of the time
where the time goes in v10:
time: 61.7 us; the launch traced here: 61.6 us
  Pallas kernels  60.9 us (99%)
  between operations  0.64 us (1%)
    pallas_call x1, Pallas kernels, forward(): pl.pallas_call(kernel, out_shape=(pltpu.VMEM((NB, SEG, D_MODEL), F32), pl...  58.7 us
    pallas_call x1, Pallas kernels, forward(): pl.pallas_call(copy_kernel, out_shape=(jax.ShapeDtypeStruct(r.shape, F32)...  2.25 us

profile of v10, /device:TPU:11, one launch (start us, length us, event | category | flops | bytes accessed | tf_op | source)
XLA Modules:
  0.0 61.6 jit_solution(5803323850142655565)
XLA Ops:
  0.6 58.7 %shard_map.121 = (f32[4,64,1536]{2,1,0:T(8,128)S(1)}, f32[4,2,12,64,128]{4,3,2,1,0:T(8,128)S(1)}, bf16[2,4,16,3328]{3,2,1,0:T(8,128)(2,1)S(1)}) custom-call(f32[4,64,1536]{2,1,0:T(8,128)} %resid_hbm.1, f32[2,1536]{1,0:T(2,128)} %pre_hbm.1, bf16[2,6448,1536]{2,1,0:T(8,128)(2,1)} %bitcast.3, f32[2,4,3328]{2,1,0:T(4,128)} %bitcast.4, f32[2,3328]{1,0:T(2,128)} %cb_hbm.1, ...), custom_call_target="tpu_custom_call" | custom-call | tf_op jit(solution)/shard_map/pallas_call | solution.py:649
  59.3 2.2 %shard_map.122 = (f32[4,64,1536]{2,1,0:T(8,128)}, f32[4,2,12,64,128]{4,3,2,1,0:T(8,128)}, bf16[4,3,2,3328]{3,2,1,0:T(2,128)(2,1)}) custom-call(f32[4,64,1536]{2,1,0:T(8,128)S(1)} %get-tuple-element.9.r_ref, f32[4,2,12,64,128]{4,3,2,1,0:T(8,128)S(1)} %get-tuple-element.10.ssm_ref, bf16[2,4,16,3328]{3,2,1,0:T(8,128)(2,1)S(1)} %get-tuple-element.11.tail_ref), custom_call_target="tpu_custom_call" | custom-call | tf_op jit(solution)/shard_map/pallas_call | solution.py:705
